TPU v7x, 32 devices: a whole 2x2x4 slice. The times are simulated.
32 devices in a mesh: wide: 8 (over y, x, core), narrow: 4 (over z).
Axes of the slice: x: 2, y: 2, z: 4, core: 2. Of those that a mesh axis runs over, the one named last changes fastest.
Arguments:
- tokens: bfloat16 [8192, 2048], P(('wide', 'narrow')), may hold values from -6 to 6
- out_grad: bfloat16 [8192, 2048], P(('wide', 'narrow')), may hold values from -6 to 6
- captions: bfloat16 [4096, 4096], P(('wide', 'narrow')), may hold values from -6 to 6
- image_blocks: int32 [32, 256], P('wide'), may hold values from 0 to 3, never falling along the last dimension, each value on 1 to 128 neighbouring positions
- caption_owner: int32 [8, 512], P('wide'), may hold values from 0 to 3, never falling along the last dimension, each value on 1 to 256 neighbouring positions
- norm_gains: float32 [3, 2048], replicated, may hold values from 0.25 to 1.75
- norm_shifts: float32 [3, 2048], replicated, may hold values from -3 to 3
- w_query: float32 [2048, 2048], P('wide', 'narrow'), may hold values from -0.125 to 0.125
- w_key: float32 [2048, 2048], P('wide', 'narrow'), may hold values from -0.125 to 0.125
- w_value: float32 [2048, 2048], P('wide', 'narrow'), may hold values from -0.125 to 0.125
- w_out: float32 [2048, 2048], P('narrow', 'wide'), may hold values from -0.375 to 0.375
- w_cross_query: float32 [2048, 2048], P('wide', 'narrow'), may hold values from -0.125 to 0.125
- w_cross_key: float32 [4096, 2048], P('wide', 'narrow'), may hold values from -0.09375 to 0.09375
- w_cross_value: float32 [4096, 2048], P('wide', 'narrow'), may hold values from -0.09375 to 0.09375
- w_cross_out: float32 [2048, 2048], P('narrow', 'wide'), may hold values from -0.375 to 0.375
- w_up: float32 [2048, 8192], P('wide', 'narrow'), may hold values from -0.125 to 0.125
- w_down: float32 [8192, 2048], P('narrow', 'wide'), may hold values from -0.0625 to 0.0625
Outputs:
- block_out: bfloat16 [8192, 2048], P(('wide', 'narrow'))
- grad_tokens: bfloat16 [8192, 2048], P(('wide', 'narrow'))
- grad_captions: bfloat16 [4096, 4096], P(('wide', 'narrow'))
- grad_norm_gains: float32 [3, 2048], replicated
- grad_norm_shifts: float32 [3, 2048], replicated
- grad_w_query: float32 [2048, 2048], P('wide', 'narrow')
- grad_w_key: float32 [2048, 2048], P('wide', 'narrow')
- grad_w_value: float32 [2048, 2048], P('wide', 'narrow')
- grad_w_out: float32 [2048, 2048], P('narrow', 'wide')
- grad_w_cross_query: float32 [2048, 2048], P('wide', 'narrow')
- grad_w_cross_key: float32 [4096, 2048], P('wide', 'narrow')
- grad_w_cross_value: float32 [4096, 2048], P('wide', 'narrow')
- grad_w_cross_out: float32 [2048, 2048], P('narrow', 'wide')
- grad_w_up: float32 [2048, 8192], P('wide', 'narrow')
- grad_w_down: float32 [8192, 2048], P('narrow', 'wide')
Inputs may be any that keep to these rules, and one draw needn't show every extreme that they name: `image_blocks`: within an image the block numbers never fall; each of the 4 blocks has 1 to 128 tokens, and one block of every image has exactly that many. `caption_owner`: within a group the owners never fall; every image of the group has 1 to 256 caption tokens, and one image of every group has exactly 256.
All inputs are finite; a program needn't handle non-finite values.
Results may differ from a plain program's by a relative error of at most 0.024.
Values may be sent and summed in bfloat16 or wider, within the bound.
A program may use at most 320 MiB of HBM per device.

v0:
```python
import jax
import jax.numpy as jnp
from jax import lax
from jax.sharding import PartitionSpec as P

HEAD_DIM = 128
PIX = 256


EPSILON = 1e-06
MASKED = -1000000000.0


def norm_apply(features, norm_gain, norm_shift):
    center = features - jnp.mean(features, axis=-1, keepdims=True)
    spread = jnp.mean(center * center, axis=-1, keepdims=True)
    return center * lax.rsqrt(spread + EPSILON) * norm_gain + norm_shift


def product(left_side, right_side):
    return jnp.dot(left_side, right_side, preferred_element_type=jnp.float32)


def left_inner_product(left_side, right_side):
    return lax.dot_general(
        left_side, right_side, (((0,), (0,)), ((), ())), preferred_element_type=jnp.float32
    )


def right_inner(left_side, right_side):
    return lax.dot_general(
        left_side, right_side, (((1,), (1,)), ((), ())), preferred_element_type=jnp.float32
    )


def spread_rows(local_rows):
    return lax.all_gather(local_rows, "narrow", axis=0, tiled=True)


def spread_grads(local_rows):
    return lax.all_gather(local_rows, "narrow", axis=0, tiled=True)


def sink_rows(partial_value):
    return lax.psum_scatter(partial_value, "narrow", scatter_dimension=0, tiled=True)


def sink_grads(partial_value):
    return lax.psum_scatter(
        partial_value.astype(jnp.bfloat16), "narrow", scatter_dimension=0, tiled=True
    ).astype(jnp.float32)


def score_block(queries, keys_in, allowed, score_scale):
    raw_scores = (
        jnp.einsum("iphe,iqhe->ihpq", queries, keys_in, preferred_element_type=jnp.float32)
        * score_scale
    )
    return jnp.where(allowed[:, None], raw_scores, MASKED)


def attend(queries, keys_in, values_in, allowed, score_scale):
    scores = score_block(queries, keys_in, allowed, score_scale)
    log_total = jax.nn.logsumexp(scores, axis=-1, keepdims=True)
    soft_weights = jnp.exp(scores - log_total).astype(jnp.bfloat16)
    mixture = jnp.einsum(
        "ihpq,iqhe->iphe", soft_weights, values_in, preferred_element_type=jnp.float32
    )
    return (mixture.astype(jnp.bfloat16), log_total)


def attention_backward(queries, keys_in, values_in, allowed, log_total, grad_mix, score_scale):
    scores = score_block(queries, keys_in, allowed, score_scale)
    soft_weights = jnp.exp(scores - log_total)
    grad_soft = jnp.einsum(
        "iphe,iqhe->ihpq", grad_mix, values_in, preferred_element_type=jnp.float32
    )
    grad_values = jnp.einsum(
        "ihpq,iphe->iqhe",
        soft_weights.astype(jnp.bfloat16),
        grad_mix,
        preferred_element_type=jnp.float32,
    ).astype(jnp.bfloat16)
    row_dot = jnp.sum(soft_weights * grad_soft, axis=-1, keepdims=True)
    grad_scores = (soft_weights * (grad_soft - row_dot) * score_scale).astype(jnp.bfloat16)
    query_rows_gradient = jnp.einsum(
        "ihpq,iqhe->iphe", grad_scores, keys_in, preferred_element_type=jnp.float32
    ).astype(jnp.bfloat16)
    grad_keys = jnp.einsum(
        "ihpq,iphe->iqhe", grad_scores, queries, preferred_element_type=jnp.float32
    ).astype(jnp.bfloat16)
    return (query_rows_gradient, grad_keys, grad_values)


def body(
    tokens,
    out_grad,
    captions,
    image_blocks,
    caption_owner,
    norm_gains,
    norm_shifts,
    w_query,
    w_key,
    w_value,
    w_out,
    w_cross_query,
    w_cross_key,
    w_cross_value,
    w_cross_out,
    w_up,
    w_down,
):
    score_scale = HEAD_DIM ** (-0.5)
    images_here = lax.axis_size("narrow")
    group_rows = PIX * images_here
    gathered = (
        lax.all_gather(w_query.astype(jnp.bfloat16), "wide", axis=0, tiled=True),
        lax.all_gather(w_key.astype(jnp.bfloat16), "wide", axis=0, tiled=True),
        lax.all_gather(w_value.astype(jnp.bfloat16), "wide", axis=0, tiled=True),
        lax.all_gather(w_out.astype(jnp.bfloat16), "wide", axis=1, tiled=True),
        lax.all_gather(w_cross_query.astype(jnp.bfloat16), "wide", axis=0, tiled=True),
        lax.all_gather(w_cross_key.astype(jnp.bfloat16), "wide", axis=0, tiled=True),
        lax.all_gather(w_cross_value.astype(jnp.bfloat16), "wide", axis=0, tiled=True),
        lax.all_gather(w_cross_out.astype(jnp.bfloat16), "wide", axis=1, tiled=True),
        lax.all_gather(w_up.astype(jnp.bfloat16), "wide", axis=0, tiled=True),
        lax.all_gather(w_down.astype(jnp.bfloat16), "wide", axis=1, tiled=True),
    )
    (
        full_query,
        full_key,
        full_value,
        full_out,
        full_cquery,
        full_ckey,
        full_cvalue,
        whole_cross_output,
        full_up,
        full_down,
    ) = gathered
    slice_width = full_query.shape[1]
    local_heads = slice_width // HEAD_DIM
    self_shape = (images_here, PIX, local_heads, HEAD_DIM)
    residual0 = tokens.astype(jnp.float32)
    first_normalized = spread_rows(
        norm_apply(residual0, norm_gains[0], norm_shifts[0]).astype(jnp.bfloat16)
    )
    self_query = product(first_normalized, full_query).astype(jnp.bfloat16).reshape(self_shape)
    self_keys = product(first_normalized, full_key).astype(jnp.bfloat16).reshape(self_shape)
    self_values = product(first_normalized, full_value).astype(jnp.bfloat16).reshape(self_shape)
    self_allowed = image_blocks[:, :, None] == image_blocks[:, None, :]
    self_mix, self_total = attend(self_query, self_keys, self_values, self_allowed, score_scale)
    self_flat = self_mix.reshape(group_rows, slice_width)
    residual1 = residual0 + sink_rows(product(self_flat, full_out))
    normed2 = spread_rows(norm_apply(residual1, norm_gains[1], norm_shifts[1]).astype(jnp.bfloat16))
    cross_query = (
        product(normed2, full_cquery)
        .astype(jnp.bfloat16)
        .reshape(1, group_rows, local_heads, HEAD_DIM)
    )
    text_rows = lax.all_gather(captions, "narrow", axis=0, tiled=True)
    text_count = text_rows.shape[0]
    cross_keys = (
        product(text_rows, full_ckey)
        .astype(jnp.bfloat16)
        .reshape(1, text_count, local_heads, HEAD_DIM)
    )
    cross_values = (
        product(text_rows, full_cvalue)
        .astype(jnp.bfloat16)
        .reshape(1, text_count, local_heads, HEAD_DIM)
    )
    image_of = jnp.arange(group_rows, dtype=jnp.int32) // PIX
    cross_allowed = (image_of[:, None] == caption_owner[0][None, :])[None]
    cross_mix, cross_total = attend(
        cross_query, cross_keys, cross_values, cross_allowed, score_scale
    )
    cross_flat = cross_mix.reshape(group_rows, slice_width)
    residual2 = residual1 + sink_rows(product(cross_flat, whole_cross_output))
    normed3 = spread_rows(norm_apply(residual2, norm_gains[2], norm_shifts[2]).astype(jnp.bfloat16))
    hidden = product(normed3, full_up)
    acted = jax.nn.gelu(hidden).astype(jnp.bfloat16)
    block_out = (residual2 + sink_rows(product(acted, full_down))).astype(jnp.bfloat16)
    fetched = (
        lax.all_gather(w_query.astype(jnp.bfloat16), "wide", axis=0, tiled=True),
        lax.all_gather(w_key.astype(jnp.bfloat16), "wide", axis=0, tiled=True),
        lax.all_gather(w_value.astype(jnp.bfloat16), "wide", axis=0, tiled=True),
        lax.all_gather(w_out.astype(jnp.bfloat16), "wide", axis=1, tiled=True),
        lax.all_gather(w_cross_query.astype(jnp.bfloat16), "wide", axis=0, tiled=True),
        lax.all_gather(w_cross_key.astype(jnp.bfloat16), "wide", axis=0, tiled=True),
        lax.all_gather(w_cross_value.astype(jnp.bfloat16), "wide", axis=0, tiled=True),
        lax.all_gather(w_cross_out.astype(jnp.bfloat16), "wide", axis=1, tiled=True),
        lax.all_gather(w_up.astype(jnp.bfloat16), "wide", axis=0, tiled=True),
        lax.all_gather(w_down.astype(jnp.bfloat16), "wide", axis=1, tiled=True),
    )
    (
        back_query,
        back_key,
        back_value,
        back_out,
        back_cquery,
        back_ckey,
        back_cvalue,
        back_cout,
        back_up,
        back_down,
    ) = fetched
    grad3 = out_grad.astype(jnp.float32)
    mlp_grad = spread_grads(out_grad)
    grad_acted = right_inner(mlp_grad, back_down)
    grad_down = left_inner_product(acted, mlp_grad)
    unused_gelu, gelu_back = jax.vjp(jax.nn.gelu, hidden)
    grad_hidden = gelu_back(grad_acted)[0].astype(jnp.bfloat16)
    grad_up = left_inner_product(normed3, grad_hidden)
    grad_normed3 = sink_grads(right_inner(grad_hidden, back_up))
    unused_norm3, norm_back3 = jax.vjp(norm_apply, residual2, norm_gains[2], norm_shifts[2])
    grad_res3, grad_gain3, grad_shift3 = norm_back3(grad_normed3)
    grad2 = grad3 + grad_res3
    cross_grad = spread_grads(grad2.astype(jnp.bfloat16))
    grad_cout = left_inner_product(cross_flat, cross_grad)
    grad_cmix = (
        right_inner(cross_grad, back_cout)
        .astype(jnp.bfloat16)
        .reshape(1, group_rows, local_heads, HEAD_DIM)
    )
    grad_cq, grad_ck, grad_cv = attention_backward(
        cross_query, cross_keys, cross_values, cross_allowed, cross_total, grad_cmix, score_scale
    )
    grad_cq = grad_cq.reshape(group_rows, slice_width)
    grad_ck = grad_ck.reshape(text_count, slice_width)
    grad_cv = grad_cv.reshape(text_count, slice_width)
    grad_cquery = left_inner_product(normed2, grad_cq)
    grad_ckey = left_inner_product(text_rows, grad_ck)
    grad_cvalue = left_inner_product(text_rows, grad_cv)
    grad_text = lax.psum_scatter(
        (right_inner(grad_ck, back_ckey) + right_inner(grad_cv, back_cvalue)).astype(jnp.bfloat16),
        "narrow",
        scatter_dimension=0,
        tiled=True,
    )
    grad_normed2 = sink_grads(right_inner(grad_cq, back_cquery))
    unused_norm2, norm_back2 = jax.vjp(norm_apply, residual1, norm_gains[1], norm_shifts[1])
    grad_res2, grad_gain2, grad_shift2 = norm_back2(grad_normed2)
    grad1 = grad2 + grad_res2
    self_grad = spread_grads(grad1.astype(jnp.bfloat16))
    grad_sout = left_inner_product(self_flat, self_grad)
    grad_smix = right_inner(self_grad, back_out).astype(jnp.bfloat16).reshape(self_shape)
    grad_sq, self_key_gradient, grad_sv = attention_backward(
        self_query, self_keys, self_values, self_allowed, self_total, grad_smix, score_scale
    )
    grad_sq = grad_sq.reshape(group_rows, slice_width)
    self_key_gradient = self_key_gradient.reshape(group_rows, slice_width)
    grad_sv = grad_sv.reshape(group_rows, slice_width)
    grad_squery = left_inner_product(first_normalized, grad_sq)
    self_key_rows_gradient = left_inner_product(first_normalized, self_key_gradient)
    grad_svalue = left_inner_product(first_normalized, grad_sv)
    grad_normed1 = sink_grads(
        right_inner(grad_sq, back_query)
        + right_inner(self_key_gradient, back_key)
        + right_inner(grad_sv, back_value)
    )
    unused_norm1, norm_back1 = jax.vjp(norm_apply, residual0, norm_gains[0], norm_shifts[0])
    grad_res1, grad_gain1, grad_shift1 = norm_back1(grad_normed1)
    grad_tokens = (grad1 + grad_res1).astype(jnp.bfloat16)
    gain_grads, shift_grads = lax.psum(
        (
            jnp.stack([grad_gain1, grad_gain2, grad_gain3]),
            jnp.stack([grad_shift1, grad_shift2, grad_shift3]),
        ),
        ("wide", "narrow"),
    )
    summed = (
        lax.psum_scatter(
            grad_squery.astype(jnp.bfloat16), "wide", scatter_dimension=0, tiled=True
        ).astype(jnp.float32),
        lax.psum_scatter(
            self_key_rows_gradient.astype(jnp.bfloat16), "wide", scatter_dimension=0, tiled=True
        ).astype(jnp.float32),
        lax.psum_scatter(
            grad_svalue.astype(jnp.bfloat16), "wide", scatter_dimension=0, tiled=True
        ).astype(jnp.float32),
        lax.psum_scatter(
            grad_sout.astype(jnp.bfloat16), "wide", scatter_dimension=1, tiled=True
        ).astype(jnp.float32),
        lax.psum_scatter(
            grad_cquery.astype(jnp.bfloat16), "wide", scatter_dimension=0, tiled=True
        ).astype(jnp.float32),
        lax.psum_scatter(
            grad_ckey.astype(jnp.bfloat16), "wide", scatter_dimension=0, tiled=True
        ).astype(jnp.float32),
        lax.psum_scatter(
            grad_cvalue.astype(jnp.bfloat16), "wide", scatter_dimension=0, tiled=True
        ).astype(jnp.float32),
        lax.psum_scatter(
            grad_cout.astype(jnp.bfloat16), "wide", scatter_dimension=1, tiled=True
        ).astype(jnp.float32),
        lax.psum_scatter(
            grad_up.astype(jnp.bfloat16), "wide", scatter_dimension=0, tiled=True
        ).astype(jnp.float32),
        lax.psum_scatter(
            grad_down.astype(jnp.bfloat16), "wide", scatter_dimension=1, tiled=True
        ).astype(jnp.float32),
    )
    return (
        block_out,
        grad_tokens,
        grad_text,
        gain_grads,
        shift_grads,
        summed[0],
        summed[1],
        summed[2],
        summed[3],
        summed[4],
        summed[5],
        summed[6],
        summed[7],
        summed[8],
        summed[9],
    )


def solution(mesh):
    in_specs = (
        P(("wide", "narrow"), None),
        P(("wide", "narrow"), None),
        P(("wide", "narrow"), None),
        P("wide", None),
        P("wide", None),
        P(),
        P(),
        P("wide", "narrow"),
        P("wide", "narrow"),
        P("wide", "narrow"),
        P("narrow", "wide"),
        P("wide", "narrow"),
        P("wide", "narrow"),
        P("wide", "narrow"),
        P("narrow", "wide"),
        P("wide", "narrow"),
        P("narrow", "wide"),
    )
    out_specs = (
        P(("wide", "narrow"), None),
        P(("wide", "narrow"), None),
        P(("wide", "narrow"), None),
        P(),
        P(),
        P("wide", "narrow"),
        P("wide", "narrow"),
        P("wide", "narrow"),
        P("narrow", "wide"),
        P("wide", "narrow"),
        P("wide", "narrow"),
        P("wide", "narrow"),
        P("narrow", "wide"),
        P("wide", "narrow"),
        P("narrow", "wide"),
    )
    return jax.shard_map(body, mesh=mesh, in_specs=in_specs, out_specs=out_specs, check_vma=False)
```

profile of v0, /device:TPU:0, one launch (start us, length us, event | category | flops | bytes accessed | tf_op | source)
XLA Modules:
  0.0 2328.8 jit_solution(16515197786778117844)
XLA Ops:
  20.1 20.9 all-gather.24.cloned.1.call-done
  41.0 82.9 %all-gather.18.cloned.1.call-done = bf16[1024,2048]{1,0:T(8,128)(2,1)} async-done(((bf16[256,2048]{1,0:T(8,128)(2,1)}), bf16[1024,2048]{1,0:T(8,128)(2,1)}) %all-gather.18.cloned.1.call-update) | async-done | bytes 4194320 | tf_op jit(solution)/shard_map/all_gather | solution.py:37
  130.0 22.7 all-gather.22.cloned.1.call-done
  158.8 24.0 %all-gather.20.cloned.1.call-done = bf16[2048,512]{1,0:T(8,128)(2,1)} async-done(((bf16[256,512]{1,0:T(8,128)(2,1)}), bf16[2048,512]{1,0:T(8,128)(2,1)}) %all-gather.20.cloned.1.call-update) | async-done | bytes 2097168 | tf_op jit(solution)/shard_map/all_gather | solution.py:120
  225.7 139.6 %reduce-scatter.18.cloned.1.call-done = f32[256,2048]{1,0:T(8,128)} async-done(((f32[1024,2048]{1,0:T(8,128)}), f32[256,2048]{1,0:T(8,128)}) %reduce-scatter.18.cloned.1.call-update) | async-done | bytes 2097168 | tf_op jit(solution)/shard_map/reduce_scatter | solution.py:45
  370.4 77.9 %all-gather.28.cloned.1.call-done = bf16[512,4096]{1,0:T(8,128)(2,1)} async-done(((bf16[128,4096]{1,0:T(8,128)(2,1)}), bf16[512,4096]{1,0:T(8,128)(2,1)}) %all-gather.28.cloned.1.call-update) | async-done | bytes 4194320 | tf_op jit(solution)/shard_map/all_gather | solution.py:161
  448.3 37.6 %all-gather.36.cloned.1.call-done = bf16[4096,512]{1,0:T(8,128)(2,1)} async-done(((bf16[512,512]{1,0:T(8,128)(2,1)}), bf16[4096,512]{1,0:T(8,128)(2,1)}) %all-gather.36.cloned.1.call-update) | async-done | bytes 4194320 | tf_op jit(solution)/shard_map/all_gather | solution.py:123
  491.7 33.2 %all-gather.30.cloned.1.call-done = bf16[4096,512]{1,0:T(8,128)(2,1)} async-done(((bf16[512,512]{1,0:T(8,128)(2,1)}), bf16[4096,512]{1,0:T(8,128)(2,1)}) %all-gather.30.cloned.1.call-update) | async-done | bytes 4194320 | tf_op jit(solution)/shard_map/all_gather | solution.py:124
  531.5 23.5 %all-gather.34.cloned.1.call-done = bf16[2048,512]{1,0:T(8,128)(2,1)} async-done(((bf16[256,512]{1,0:T(8,128)(2,1)}), bf16[2048,512]{1,0:T(8,128)(2,1)}) %all-gather.34.cloned.1.call-update) | async-done | bytes 2097168 | tf_op jit(solution)/shard_map/all_gather | solution.py:122
  555.0 82.9 %all-gather.32.cloned.1.call-done = bf16[1024,2048]{1,0:T(8,128)(2,1)} async-done(((bf16[256,2048]{1,0:T(8,128)(2,1)}), bf16[1024,2048]{1,0:T(8,128)(2,1)}) %all-gather.32.cloned.1.call-update) | async-done | bytes 4194320 | tf_op jit(solution)/shard_map/all_gather | solution.py:37
  680.6 138.6 %reduce-scatter.20.cloned.1.call-done = f32[256,2048]{1,0:T(8,128)} async-done(((f32[1024,2048]{1,0:T(8,128)}), f32[256,2048]{1,0:T(8,128)}) %reduce-scatter.20.cloned.1.call-update) | async-done | bytes 2097168 | tf_op jit(solution)/shard_map/reduce_scatter | solution.py:45
  823.9 78.1 %all-gather.46.cloned.1.call-done = bf16[1024,2048]{1,0:T(8,128)(2,1)} async-done(((bf16[256,2048]{1,0:T(8,128)(2,1)}), bf16[1024,2048]{1,0:T(8,128)(2,1)}) %all-gather.46.cloned.1.call-update) | async-done | bytes 4194320 | tf_op jit(solution)/shard_map/all_gather | solution.py:41
  902.0 56.7 %all-gather.44.cloned.1.call-done = bf16[2048,2048]{1,0:T(8,128)(2,1)} async-done(((bf16[2048,256]{1,0:T(8,128)(2,1)}), bf16[2048,2048]{1,0:T(8,128)(2,1)}) %all-gather.44.cloned.1.call-update) | async-done | bytes 8388624 | tf_op jit(solution)/shard_map/all_gather | solution.py:127
  973.3 42.0 %all-gather.42.cloned.1.call-done = bf16[2048,2048]{1,0:T(8,128)(2,1)} async-done(((bf16[256,2048]{1,0:T(8,128)(2,1)}), bf16[2048,2048]{1,0:T(8,128)(2,1)}) %all-gather.42.cloned.1.call-update) | async-done | bytes 8388624 | tf_op jit(solution)/shard_map/all_gather | solution.py:126
  1015.3 82.8 %all-gather.40.cloned.1.call-done = bf16[1024,2048]{1,0:T(8,128)(2,1)} async-done(((bf16[256,2048]{1,0:T(8,128)(2,1)}), bf16[1024,2048]{1,0:T(8,128)(2,1)}) %all-gather.40.cloned.1.call-update) | async-done | bytes 4194320 | tf_op jit(solution)/shard_map/all_gather | solution.py:37
  1098.0 20.0 fusion.8
  1147.4 58.9 %reduce-scatter.24.cloned.1.call-done = bf16[256,2048]{1,0:T(8,128)(2,1)} async-done(((bf16[1024,2048]{1,0:T(8,128)(2,1)}), bf16[256,2048]{1,0:T(8,128)(2,1)}) %reduce-scatter.24.cloned.1.call-update) | async-done | bytes 1048592 | tf_op jit(solution)/shard_map/reduce_scatter | solution.py:49
  1209.6 144.2 %reduce-scatter.22.cloned.1.call-done = f32[256,2048]{1,0:T(8,128)} async-done(((f32[1024,2048]{1,0:T(8,128)}), f32[256,2048]{1,0:T(8,128)}) %reduce-scatter.22.cloned.1.call-update) | async-done | bytes 2097168 | tf_op jit(solution)/shard_map/reduce_scatter | solution.py:45
  1361.1 81.1 %all-gather.48.cloned.1.call-done = bf16[1024,2048]{1,0:T(8,128)(2,1)} async-done(((bf16[256,2048]{1,0:T(8,128)(2,1)}), bf16[1024,2048]{1,0:T(8,128)(2,1)}) %all-gather.48.cloned.1.call-update) | async-done | bytes 4194320 | tf_op jit(solution)/shard_map/all_gather | solution.py:41
  1474.3 75.4 %reduce-scatter.26.cloned.1.call-done = bf16[256,2048]{1,0:T(8,128)(2,1)} async-done(((bf16[1024,2048]{1,0:T(8,128)(2,1)}), bf16[256,2048]{1,0:T(8,128)(2,1)}) %reduce-scatter.26.cloned.1.call-update) | async-done | bytes 1048592 | tf_op jit(solution)/shard_map/reduce_scatter | solution.py:49
  1730.9 55.3 %reduce-scatter.50.cloned.1.call-done = bf16[2048,256]{1,0:T(8,128)(2,1)} async-done(((bf16[2048,2048]{1,0:T(8,128)(2,1)}), bf16[2048,256]{1,0:T(8,128)(2,1)}) %reduce-scatter.50.cloned.1.call-update) | async-done | bytes 1048592 | tf_op jit(solution)/shard_map/reduce_scatter | solution.py:300
  1788.9 41.7 %reduce-scatter.46.cloned.1.call-done = bf16[512,256]{1,0:T(8,128)(2,1)} async-done(((bf16[512,2048]{1,0:T(8,128)(2,1)}), bf16[512,256]{1,0:T(8,128)(2,1)}) %reduce-scatter.46.cloned.1.call-update) | async-done | bytes 262160 | tf_op jit(solution)/shard_map/reduce_scatter | solution.py:294
  1832.4 42.5 %reduce-scatter.40.cloned.1.call-done = bf16[256,512]{1,0:T(8,128)(2,1)} async-done(((bf16[2048,512]{1,0:T(8,128)(2,1)}), bf16[256,512]{1,0:T(8,128)(2,1)}) %reduce-scatter.40.cloned.1.call-update) | async-done | bytes 262160 | tf_op jit(solution)/shard_map/reduce_scatter | solution.py:285
  1876.7 52.5 %reduce-scatter.44.cloned.1.call-done = bf16[512,512]{0,1:T(8,128)(2,1)} async-done(((bf16[4096,512]{0,1:T(8,128)(2,1)}), bf16[512,512]{0,1:T(8,128)(2,1)}) %reduce-scatter.44.cloned.1.call-update) | async-done | bytes 524304 | tf_op jit(solution)/shard_map/reduce_scatter | solution.py:291
  1931.5 52.2 %reduce-scatter.42.cloned.1.call-done = bf16[512,512]{0,1:T(8,128)(2,1)} async-done(((bf16[4096,512]{0,1:T(8,128)(2,1)}), bf16[512,512]{0,1:T(8,128)(2,1)}) %reduce-scatter.42.cloned.1.call-update) | async-done | bytes 524304 | tf_op jit(solution)/shard_map/reduce_scatter | solution.py:288
  1985.9 42.2 %reduce-scatter.38.cloned.1.call-done = bf16[512,256]{1,0:T(8,128)(2,1)} async-done(((bf16[512,2048]{1,0:T(8,128)(2,1)}), bf16[512,256]{1,0:T(8,128)(2,1)}) %reduce-scatter.38.cloned.1.call-update) | async-done | bytes 262160 | tf_op jit(solution)/shard_map/reduce_scatter | solution.py:282
  2029.9 42.5 %reduce-scatter.32.cloned.1.call-done = bf16[256,512]{1,0:T(8,128)(2,1)} async-done(((bf16[2048,512]{1,0:T(8,128)(2,1)}), bf16[256,512]{1,0:T(8,128)(2,1)}) %reduce-scatter.32.cloned.1.call-update) | async-done | bytes 262160 | tf_op jit(solution)/shard_map/reduce_scatter | solution.py:273
  2074.2 42.6 %reduce-scatter.34.cloned.1.call-done = bf16[256,512]{1,0:T(8,128)(2,1)} async-done(((bf16[2048,512]{1,0:T(8,128)(2,1)}), bf16[256,512]{1,0:T(8,128)(2,1)}) %reduce-scatter.34.cloned.1.call-update) | async-done | bytes 262160 | tf_op jit(solution)/shard_map/reduce_scatter | solution.py:276
  2118.7 42.6 %reduce-scatter.36.cloned.1.call-done = bf16[256,512]{1,0:T(8,128)(2,1)} async-done(((bf16[2048,512]{1,0:T(8,128)(2,1)}), bf16[256,512]{1,0:T(8,128)(2,1)}) %reduce-scatter.36.cloned.1.call-update) | async-done | bytes 262160 | tf_op jit(solution)/shard_map/reduce_scatter | solution.py:279
  2163.1 77.2 %reduce-scatter.28.cloned.1.call-done = bf16[256,2048]{1,0:T(8,128)(2,1)} async-done(((bf16[1024,2048]{1,0:T(8,128)(2,1)}), bf16[256,2048]{1,0:T(8,128)(2,1)}) %reduce-scatter.28.cloned.1.call-update) | async-done | bytes 1048592 | tf_op jit(solution)/shard_map/reduce_scatter | solution.py:49
  2244.7 46.0 %all-reduce = (f32[3,2048]{1,0:T(4,128)}, f32[3,2048]{1,0:T(4,128)}) all-reduce(f32[3,2048]{1,0:T(4,128)S(1)} %get-tuple-element.79, f32[3,2048]{1,0:T(4,128)S(1)} %get-tuple-element.80), channel_id=1, replica_groups=mesh['wide'=8,'narrow'=4] {'wide','narrow'}, use_global_device_ids=true, to_apply=%region_28.29 | all-reduce | flops 12288 | bytes 98304 | tf_op jit(solution)/shard_map/psum | solution.py:265
  2294.1 27.5 %reduce-scatter.30.cloned.1.call-done = bf16[128,4096]{1,0:T(8,128)(2,1)} async-done(((bf16[512,4096]{1,0:T(8,128)(2,1)}), bf16[128,4096]{1,0:T(8,128)(2,1)}) %reduce-scatter.30.cloned.1.call-update) | async-done | bytes 1048592 | tf_op jit(solution)/shard_map/reduce_scatter | solution.py:235
  (326 shorter events, 425.0 us)
Async XLA Ops:
  17.4 135.3 %all-gather.22.cloned.1.call-start = ((), (), s32[]{:S(2)}) async-start(), calls=%async_computation.19 | async-start | bytes 2359296 | tf_op jit(solution)/shard_map/all_gather | solution.py:118
  18.2 164.6 %all-gather.20.cloned.1.call-start = ((), (), s32[]{:S(2)}) async-start(), calls=%async_computation.18 | async-start | bytes 2359296 | tf_op jit(solution)/shard_map/all_gather | solution.py:120
  19.0 194.2 %all-gather.26.cloned.1.call-start = ((), (), s32[]{:S(2)}) async-start(), calls=%async_computation.21 | async-start | bytes 2359296 | tf_op jit(solution)/shard_map/all_gather | solution.py:121
  19.8 345.5 %reduce-scatter.18.cloned.1.call-start = ((), (), s32[]{:S(2)}) async-start(), calls=%async_computation.22 | async-start | bytes 10485760 | tf_op jit(solution)/shard_map/reduce_scatter | solution.py:45
  220.6 227.7 %all-gather.28.cloned.1.call-start = ((), (), s32[]{:S(2)}) async-start(), calls=%async_computation.23 | async-start | bytes 5242880 | tf_op jit(solution)/shard_map/all_gather | solution.py:161
  221.3 264.5 %all-gather.36.cloned.1.call-start = ((), (), s32[]{:S(2)}) async-start(), calls=%async_computation.27 | async-start | bytes 4718592 | tf_op jit(solution)/shard_map/all_gather | solution.py:123
  222.6 302.3 %all-gather.30.cloned.1.call-start = ((), (), s32[]{:S(2)}) async-start(), calls=%async_computation.24 | async-start | bytes 4718592 | tf_op jit(solution)/shard_map/all_gather | solution.py:124
  223.6 331.5 %all-gather.34.cloned.1.call-start = ((), (), s32[]{:S(2)}) async-start(), calls=%async_computation.26 | async-start | bytes 2359296 | tf_op jit(solution)/shard_map/all_gather | solution.py:122
  225.4 412.5 %all-gather.32.cloned.1.call-start = ((), (), s32[]{:S(2)}) async-start(), calls=%async_computation.25 | async-start | bytes 5242880 | tf_op jit(solution)/shard_map/all_gather | solution.py:37
  369.1 297.8 %all-gather.38.cloned.1.call-start = ((), (), s32[]{:S(2)}) async-start(), calls=%async_computation.28 | async-start | bytes 2359296 | tf_op jit(solution)/shard_map/all_gather | solution.py:125
  369.9 449.3 %reduce-scatter.20.cloned.1.call-start = ((), (), s32[]{:S(2)}) async-start(), calls=%async_computation.29 | async-start | bytes 10485760 | tf_op jit(solution)/shard_map/reduce_scatter | solution.py:45
  674.4 227.6 %all-gather.46.cloned.1.call-start = ((), (), s32[]{:S(2)}) async-start(), calls=%async_computation.34 | async-start | bytes 5242880 | tf_op jit(solution)/shard_map/all_gather | solution.py:41
  675.0 283.7 %all-gather.44.cloned.1.call-start = ((), (), s32[]{:S(2)}) async-start(), calls=%async_computation.32 | async-start | bytes 9437184 | tf_op jit(solution)/shard_map/all_gather | solution.py:127
  677.7 337.5 %all-gather.42.cloned.1.call-start = ((), (), s32[]{:S(2)}) async-start(), calls=%async_computation.31 | async-start | bytes 9437184 | tf_op jit(solution)/shard_map/all_gather | solution.py:126
  680.5 417.5 %all-gather.40.cloned.1.call-start = ((), (), s32[]{:S(2)}) async-start(), calls=%async_computation.30 | async-start | bytes 5242880 | tf_op jit(solution)/shard_map/all_gather | solution.py:37
  823.8 382.4 %reduce-scatter.24.cloned.1.call-start = ((), (), s32[]{:S(2)}) async-start(), calls=%async_computation.35 | async-start | bytes 5242880 | tf_op jit(solution)/shard_map/reduce_scatter | solution.py:49
  1130.9 222.9 %reduce-scatter.22.cloned.1.call-start = ((), (), s32[]{:S(2)}) async-start(), calls=%async_computation.33 | async-start | bytes 10485760 | tf_op jit(solution)/shard_map/reduce_scatter | solution.py:45
  1147.3 294.8 %all-gather.48.cloned.1.call-start = ((), (), s32[]{:S(2)}) async-start(), calls=%async_computation.36 | async-start | bytes 5242880 | tf_op jit(solution)/shard_map/all_gather | solution.py:41
  1360.6 189.0 %reduce-scatter.26.cloned.1.call-start = ((), (), s32[]{:S(2)}) async-start(), calls=%async_computation.37 | async-start | bytes 5242880 | tf_op jit(solution)/shard_map/reduce_scatter | solution.py:49
  1474.2 163.8 %all-gather.50.cloned.1.call-start = ((), (), s32[]{:S(2)}) async-start(), calls=%async_computation.38 | async-start | bytes 5242880 | tf_op jit(solution)/shard_map/all_gather | solution.py:41
  1556.7 171.3 %reduce-scatter.48.cloned.1.call-start = ((), (), s32[]{:S(2)}) async-start(), calls=%async_computation.49 | async-start | bytes 9437184 | tf_op jit(solution)/shard_map/reduce_scatter | solution.py:297
  1571.0 215.2 %reduce-scatter.50.cloned.1.call-start = ((), (), s32[]{:S(2)}) async-start(), calls=%async_computation.50 | async-start | bytes 9437184 | tf_op jit(solution)/shard_map/reduce_scatter | solution.py:300
  1586.6 244.0 %reduce-scatter.46.cloned.1.call-start = ((), (), s32[]{:S(2)}) async-start(), calls=%async_computation.48 | async-start | bytes 2359296 | tf_op jit(solution)/shard_map/reduce_scatter | solution.py:294
  1593.7 281.2 %reduce-scatter.40.cloned.1.call-start = ((), (), s32[]{:S(2)}) async-start(), calls=%async_computation.45 | async-start | bytes 2359296 | tf_op jit(solution)/shard_map/reduce_scatter | solution.py:285
  1600.2 329.0 %reduce-scatter.44.cloned.1.call-start = ((), (), s32[]{:S(2)}) async-start(), calls=%async_computation.47 | async-start | bytes 4718592 | tf_op jit(solution)/shard_map/reduce_scatter | solution.py:291
  1611.5 372.2 %reduce-scatter.42.cloned.1.call-start = ((), (), s32[]{:S(2)}) async-start(), calls=%async_computation.46 | async-start | bytes 4718592 | tf_op jit(solution)/shard_map/reduce_scatter | solution.py:288
  1633.3 394.8 %reduce-scatter.38.cloned.1.call-start = ((), (), s32[]{:S(2)}) async-start(), calls=%async_computation.44 | async-start | bytes 2359296 | tf_op jit(solution)/shard_map/reduce_scatter | solution.py:282
  1644.0 428.5 %reduce-scatter.32.cloned.1.call-start = ((), (), s32[]{:S(2)}) async-start(), calls=%async_computation.41 | async-start | bytes 2359296 | tf_op jit(solution)/shard_map/reduce_scatter | solution.py:273
  1673.0 443.9 %reduce-scatter.34.cloned.1.call-start = ((), (), s32[]{:S(2)}) async-start(), calls=%async_computation.42 | async-start | bytes 2359296 | tf_op jit(solution)/shard_map/reduce_scatter | solution.py:276
  1692.0 469.4 %reduce-scatter.36.cloned.1.call-start = ((), (), s32[]{:S(2)}) async-start(), calls=%async_computation.43 | async-start | bytes 2359296 | tf_op jit(solution)/shard_map/reduce_scatter | solution.py:279
  1704.1 536.2 %reduce-scatter.28.cloned.1.call-start = ((), (), s32[]{:S(2)}) async-start(), calls=%async_computation.39 | async-start | bytes 5242880 | tf_op jit(solution)/shard_map/reduce_scatter | solution.py:49
  1717.1 604.5 %reduce-scatter.30.cloned.1.call-start = ((), (), s32[]{:S(2)}) async-start(), calls=%async_computation.40 | async-start | bytes 5242880 | tf_op jit(solution)/shard_map/reduce_scatter | solution.py:235
  (72 other events, 5014.7 us)
Sparse Core Ops, SparseCore 0:
  10.5 30.4 all-gather.23
  43.2 80.7 all-gather.17
  155.0 27.7 all-gather.19
  185.1 28.0 all-gather.25
  220.7 144.6 reduce-scatter.17
  366.9 81.3 all-gather.27
  450.7 35.0 all-gather.35
  488.3 36.5 all-gather.29
  527.2 27.7 all-gather.33
  557.2 80.7 all-gather.31
  674.5 144.6 reduce-scatter.19
  820.6 81.3 all-gather.45
  904.3 54.3 all-gather.43
  961.0 54.2 all-gather.41
  1017.3 80.7 all-gather.39
  1131.0 75.2 reduce-scatter.23
  1208.6 145.1 reduce-scatter.21
  1360.8 81.3 all-gather.47
  1474.4 75.2 reduce-scatter.25
  1556.8 81.2 all-gather.49
  1641.5 69.9 reduce-scatter.47
  1714.8 71.2 reduce-scatter.49
  1789.4 41.1 reduce-scatter.45
  1833.8 41.1 reduce-scatter.39
  1878.1 51.0 reduce-scatter.43
  1932.6 51.0 reduce-scatter.41
  1987.0 41.1 reduce-scatter.37
  2031.3 41.1 reduce-scatter.31
  2075.7 41.1 reduce-scatter.33
  2120.2 41.1 reduce-scatter.35
  2163.5 76.7 reduce-scatter.27
  2243.2 78.3 reduce-scatter.29
  (2 shorter events, 52.7 us)
where the time goes:
time: 2340 us; the launch traced here: 2330 us
  waiting for transfers between devices  1860 us (79%)
  matrix products  303 us (13%)
  other arithmetic  70.4 us (3%)
  blocking collectives  46 us (2%)
  local copies, waits for them, and re-layouts  30.4 us (1%)
    reduce_scatter x3, waiting for transfers between devices, sink_rows(): lax.psum_scatter(partial_value, 'narrow', scatter_dimension=0, tiled=True)  422 us
    all_gather x3, waiting for transfers between devices, spread_rows(): return lax.all_gather(local_rows, 'narrow', axis=0, tiled=True)  249 us
    reduce_scatter x3, waiting for transfers between devices, sink_grads(): lax.psum_scatter(partial_value.astype(jnp.bfloat16), 'narrow', scatter_di...  211 us
    all_gather x3, waiting for transfers between devices, spread_grads(): return lax.all_gather(local_rows, 'narrow', axis=0, tiled=True)  163 us
    dot_general x10, matrix products, product(): return jnp.dot(left_side, right_side, preferred_element_type=jnp.float32)  85.5 us
    all_gather x1, waiting for transfers between devices, body(): text_rows = lax.all_gather(captions, 'narrow', axis=0, tiled=True)  77.9 us
    dot_general x10, matrix products, left_inner_product(): lax.dot_general(left_side, right_side, (((0,), (0,)), ((), ())), preferre...  76.9 us
    dot_general x10, matrix products, right_inner(): lax.dot_general(left_side, right_side, (((1,), (1,)), ((), ())), preferre...  64.8 us
  transfers between devices with their start and end apart: 34, of which 33 were waited for; matrix products, arithmetic and copies ran while one was open for 13% of the time, Pallas kernels for 0%

commit v1 on v0

v1 whole, which is shorter than its diff:
```python
import jax
import jax.numpy as jnp
from jax import lax
from jax.sharding import PartitionSpec as P

HEAD_DIM = 128
PIX = 256
CHUNKS = 2

EPSILON = 1e-06
MASKED = -1000000000.0
BF = jnp.bfloat16
F32 = jnp.float32


def product(left_side, right_side):
    return lax.dot_general(
        left_side,
        right_side,
        (((left_side.ndim - 1,), (0,)), ((), ())),
        preferred_element_type=F32,
    )


def right_inner(left_side, right_side):
    return lax.dot_general(
        left_side,
        right_side,
        (((left_side.ndim - 1,), (1,)), ((), ())),
        preferred_element_type=F32,
    )


def left_inner(left_side, right_side):
    rows = tuple(range(left_side.ndim - 1))
    return lax.dot_general(left_side, right_side, ((rows, rows), ((), ())), preferred_element_type=F32)


def spread(rows):
    n = lax.axis_size("narrow")
    here = lax.axis_index("narrow")
    up, down = [rows], [rows]
    for step in range(1, n):
        up.append(lax.ppermute(up[-1], "narrow", [(k, k + 1) for k in range(step - 1, n - 1)]))
        down.append(lax.ppermute(down[-1], "narrow", [(k, k - 1) for k in range(1, n - step + 1)]))
    parts = [rows] + [jnp.where(here >= s, up[s], down[n - s]) for s in range(1, n)]
    return jnp.stack(parts)


def sink(parts):
    n = lax.axis_size("narrow")
    up = down = None
    for step in range(1, n):
        one, other = parts[step], parts[n - step]
        if up is not None:
            one = up.astype(F32) + one.astype(F32)
            other = down.astype(F32) + other.astype(F32)
        up = lax.ppermute(one.astype(BF), "narrow", [(k, k + 1) for k in range(step)])
        down = lax.ppermute(other.astype(BF), "narrow", [(k, k - 1) for k in range(n - step, n)])
    return up.astype(F32) + down.astype(F32) + parts[0].astype(F32)


def norm_stats(features):
    center = features - jnp.mean(features, axis=-1, keepdims=True)
    rstd = lax.rsqrt(jnp.mean(center * center, axis=-1, keepdims=True) + EPSILON)
    return center * rstd, rstd


def norm_back(grad, xhat, rstd, gain):
    scaled = grad * gain
    return rstd * (
        scaled
        - jnp.mean(scaled, axis=-1, keepdims=True)
        - xhat * jnp.mean(scaled * xhat, axis=-1, keepdims=True)
    )


def norm_sums(grad, xhat):
    return jnp.stack([jnp.sum(grad * xhat, axis=0), jnp.sum(grad, axis=0)])


def score_block(queries, keys_in, allowed, score_scale):
    raw = jnp.einsum("iphe,iqhe->ihpq", queries, keys_in, preferred_element_type=F32)
    return jnp.where(allowed[:, None], raw * score_scale, MASKED)


def attend(queries, keys_in, values_in, allowed, score_scale):
    scores = score_block(queries, keys_in, allowed, score_scale)
    log_total = jax.nn.logsumexp(scores, axis=-1, keepdims=True)
    soft = jnp.exp(scores - log_total).astype(BF)
    mixture = jnp.einsum("ihpq,iqhe->iphe", soft, values_in, preferred_element_type=F32)
    return mixture.astype(BF), log_total


def attend_back(queries, keys_in, values_in, allowed, log_total, grad_mix, score_scale):
    soft = jnp.exp(score_block(queries, keys_in, allowed, score_scale) - log_total)
    grad_soft = jnp.einsum("iphe,iqhe->ihpq", grad_mix, values_in, preferred_element_type=F32)
    grad_values = jnp.einsum("ihpq,iphe->iqhe", soft.astype(BF), grad_mix, preferred_element_type=F32)
    row_dot = jnp.sum(soft * grad_soft, axis=-1, keepdims=True)
    grad_scores = (soft * (grad_soft - row_dot) * score_scale).astype(BF)
    grad_queries = jnp.einsum("ihpq,iqhe->iphe", grad_scores, keys_in, preferred_element_type=F32)
    grad_keys = jnp.einsum("ihpq,iphe->iqhe", grad_scores, queries, preferred_element_type=F32)
    return grad_queries.astype(BF), grad_keys, grad_values


def after(value, *others):
    return lax.optimization_barrier((value, *others))[0]


def body(
    tokens,
    out_grad,
    captions,
    image_blocks,
    caption_owner,
    norm_gains,
    norm_shifts,
    w_query,
    w_key,
    w_value,
    w_out,
    w_cross_query,
    w_cross_key,
    w_cross_value,
    w_cross_out,
    w_up,
    w_down,
):
    scale = HEAD_DIM ** (-0.5)
    n = lax.axis_size("narrow")
    here = lax.axis_index("narrow")
    width = w_query.shape[1]
    heads = width // HEAD_DIM
    part = PIX // CHUNKS
    chunks = [slice(c * part, (c + 1) * part) for c in range(CHUNKS)]
    image_of = (here - jnp.arange(n)) % n

    def rows_of(*pieces):
        return lax.all_gather(
            jnp.concatenate([p.astype(BF) for p in pieces], axis=1), "wide", axis=0, tiled=True
        )

    def columns_of(piece):
        return lax.all_gather(piece.astype(BF), "wide", axis=1, tiled=True)

    def to_rows(g):
        return lax.psum_scatter(g.astype(BF), "wide", scatter_dimension=0, tiled=True).astype(F32)

    def to_columns(g):
        return lax.psum_scatter(g.astype(BF), "wide", scatter_dimension=1, tiled=True).astype(F32)

    full_qkv = rows_of(w_query, w_key, w_value)
    full_out = columns_of(w_out)
    full_ckv = rows_of(w_cross_key, w_cross_value)
    full_cq = rows_of(w_cross_query)
    full_cout = columns_of(w_cross_out)
    full_up = rows_of(w_up)
    full_down = columns_of(w_down)

    residual0 = tokens.astype(F32)
    xhat1, rstd1 = norm_stats(residual0)
    own1 = (xhat1 * norm_gains[0] + norm_shifts[0]).astype(BF)
    normed1 = spread(own1)
    qkv = product(normed1, full_qkv).astype(BF)
    heads_of = lambda x: x.reshape(x.shape[:-1] + (x.shape[-1] // HEAD_DIM, HEAD_DIM))
    self_q, self_k, self_v = [heads_of(qkv[..., k * width : (k + 1) * width]) for k in range(3)]
    blocks = image_blocks[image_of]
    self_allowed = blocks[:, :, None] == blocks[:, None, :]
    self_mix, self_total = attend(self_q, self_k, self_v, self_allowed, scale)
    self_mix = self_mix.reshape(n, PIX, width)

    text = spread(after(captions, normed1))
    text_count = text.shape[0] * text.shape[1]
    text_rows = text.reshape(text_count, text.shape[2])
    ckv = product(text_rows, full_ckv).astype(BF)
    cross_k = heads_of(ckv[None, :, :width])
    cross_v = heads_of(ckv[None, :, width:])
    owner = caption_owner[0].reshape(n, -1)[image_of].reshape(-1)
    part_image = jnp.repeat(image_of, part)
    cross_allowed = (part_image[:, None] == owner[None, :])[None]

    state = []
    for rows in chunks:
        residual1 = residual0[rows] + sink(product(self_mix[:, rows], full_out).astype(BF))
        xhat2, rstd2 = norm_stats(residual1)
        state.append((residual1, xhat2, rstd2))
    normed2 = [spread((s[1] * norm_gains[1] + norm_shifts[1]).astype(BF)) for s in state]
    grad_all = spread(after(out_grad, normed2[0]))

    cross_q, cross_mix, cross_total, state3 = [], [], [], []
    for c in range(CHUNKS):
        q = heads_of(product(normed2[c], full_cq).astype(BF).reshape(1, n * part, width))
        mix, total = attend(q, cross_k, cross_v, cross_allowed, scale)
        mix = mix.reshape(n, part, width)
        residual2 = state[c][0] + sink(product(mix, full_cout).astype(BF))
        xhat3, rstd3 = norm_stats(residual2)
        cross_q.append(q)
        cross_mix.append(mix)
        cross_total.append(total)
        state3.append((residual2, xhat3, rstd3))
    normed3 = [spread((s[1] * norm_gains[2] + norm_shifts[2]).astype(BF)) for s in state3]

    block_out, acts, grad_hiddens, grad2, sums3 = [], [], [], [], []
    for c, rows in enumerate(chunks):
        hidden = product(normed3[c], full_up)
        grad_rows = grad_all[:, rows]
        acted, gelu_back = jax.vjp(jax.nn.gelu, hidden)
        acted = acted.astype(BF)
        grad_hidden = gelu_back(right_inner(grad_rows, full_down))[0].astype(BF)
        acts.append(acted)
        grad_hiddens.append(grad_hidden)
        grad_n3 = sink(right_inner(grad_hidden, full_up).astype(BF))
        residual2, xhat3, rstd3 = state3[c]
        sums3.append(norm_sums(grad_n3, xhat3))
        grad2.append(out_grad[rows].astype(F32) + norm_back(grad_n3, xhat3, rstd3, norm_gains[2]))
        block_out.append(
            (residual2 + sink(product(acted, full_down).astype(BF))).astype(BF)
        )
    cat = lambda xs: jnp.concatenate(xs, axis=1)
    acted, grad_hidden, n3 = cat(acts), cat(grad_hiddens), cat(normed3)
    grad_down = left_inner(acted, cat([grad_all[:, rows] for rows in chunks]))
    grad_up = left_inner(n3, grad_hidden)

    e2 = [spread(g.astype(BF)) for g in grad2]
    own_down = to_columns(grad_down)
    own_up = to_rows(grad_up)
    e2[-1] = after(e2[-1], grad_down, grad_up)
    grad1, sums2, grad_cqs, grad_ck, grad_cv = [], [], [], 0.0, 0.0
    for c in range(CHUNKS):
        grad_mix = heads_of(right_inner(e2[c], full_cout).astype(BF).reshape(1, n * part, width))
        gq, gk, gv = attend_back(
            cross_q[c], cross_k, cross_v, cross_allowed, cross_total[c], grad_mix, scale
        )
        gq = gq.reshape(n, part, width)
        grad_cqs.append(gq)
        grad_ck = grad_ck + gk
        grad_cv = grad_cv + gv
        grad_n2 = sink(right_inner(gq, full_cq).astype(BF))
        _, xhat2, rstd2 = state[c]
        sums2.append(norm_sums(grad_n2, xhat2))
        grad1.append(grad2[c] + norm_back(grad_n2, xhat2, rstd2, norm_gains[1]))
    grad_cout = left_inner(cat(cross_mix), cat(e2))
    grad_cq = left_inner(cat(normed2), cat(grad_cqs))
    grad_ckv = jnp.concatenate(
        [grad_ck.reshape(text_count, width), grad_cv.reshape(text_count, width)], axis=1
    ).astype(BF)
    grad_text_part = right_inner(grad_ckv, full_ckv).astype(BF).reshape(n, -1, text.shape[2])
    grad_wckv = left_inner(text_rows, grad_ckv)

    e1 = [spread(g.astype(BF)) for g in grad1]
    own_cout = to_columns(grad_cout)
    own_cq = to_rows(grad_cq)
    own_ckv = to_rows(grad_wckv)
    e1[-1] = after(e1[-1], grad_cout, grad_cq, grad_wckv, grad_text_part)
    grad_mix = heads_of(cat([right_inner(e, full_out).astype(BF) for e in e1]))
    grad_mix = after(grad_mix, own_down, own_up)
    gq, gk, gv = attend_back(self_q, self_k, self_v, self_allowed, self_total, grad_mix, scale)
    grad_qkv = jnp.concatenate(
        [g.astype(BF).reshape(n, PIX, width) for g in (gq, gk, gv)], axis=-1
    )
    grad_out = left_inner(self_mix, cat(e1))
    grad_wqkv = left_inner(normed1, grad_qkv)
    grad_n1 = sink(right_inner(after(grad_qkv, grad_wqkv), full_qkv).astype(BF))
    grad_text = sink(after(grad_text_part, grad_mix)).astype(BF)
    grad1 = jnp.concatenate(grad1)
    grad_n1 = after(grad_n1, own_cout, own_cq, own_ckv)
    grad_tokens = (grad1 + norm_back(grad_n1, xhat1, rstd1, norm_gains[0])).astype(BF)
    sums = lax.psum(
        jnp.stack([norm_sums(grad_n1, xhat1), sum(sums2), sum(sums3)]), ("wide", "narrow")
    )

    own_out = to_columns(grad_out)
    own_qkv = to_rows(grad_wqkv)
    return (
        jnp.concatenate(block_out),
        grad_tokens,
        grad_text,
        sums[:, 0],
        sums[:, 1],
        own_qkv[:, :width],
        own_qkv[:, width : 2 * width],
        own_qkv[:, 2 * width :],
        own_out,
        own_cq,
        own_ckv[:, :width],
        own_ckv[:, width:],
        own_cout,
        own_up,
        own_down,
    )

def solution(mesh):
    in_specs = (
        P(("wide", "narrow"), None),
        P(("wide", "narrow"), None),
        P(("wide", "narrow"), None),
        P("wide", None),
        P("wide", None),
        P(),
        P(),
        P("wide", "narrow"),
        P("wide", "narrow"),
        P("wide", "narrow"),
        P("narrow", "wide"),
        P("wide", "narrow"),
        P("wide", "narrow"),
        P("wide", "narrow"),
        P("narrow", "wide"),
        P("wide", "narrow"),
        P("narrow", "wide"),
    )
    out_specs = (
        P(("wide", "narrow"), None),
        P(("wide", "narrow"), None),
        P(("wide", "narrow"), None),
        P(),
        P(),
        P("wide", "narrow"),
        P("wide", "narrow"),
        P("wide", "narrow"),
        P("narrow", "wide"),
        P("wide", "narrow"),
        P("wide", "narrow"),
        P("wide", "narrow"),
        P("narrow", "wide"),
        P("wide", "narrow"),
        P("narrow", "wide"),
    )
    return jax.shard_map(body, mesh=mesh, in_specs=in_specs, out_specs=out_specs, check_vma=False)
```

time: 2340 us -> 1270 us (0.54)
  waiting for transfers between devices: 1860 us -> 343 us
  starting transfers between devices: 3.27 us -> 400 us
  other arithmetic: 70.4 us -> 118 us
    reduce_scatter x17 -> x7, waiting for transfers between devices: 1080 us -> 0.07 us  [the longest x4 0.05 us: to_rows(): lax.psum_scatter(g.astype(BF), 'wide', scatter_dimension=0, tiled=True)]
    all_gather x17 -> x7, waiting for transfers between devices: 783 us -> 0.05 us  [the longest x3 0.04 us: columns_of(): return lax.all_gather(piece.astype(BF), 'wide', axis=1, tiled=True)]
    ppermute x0 -> x138, starting transfers between devices: none -> 399 us  [the longest x36 207 us: sink(): lax.ppermute(one.astype(BF), 'narrow', [(k, k + 1) for k in range(step)])]
    ppermute x0 -> x138, waiting for transfers between devices: none -> 342 us  [the longest x33 192 us: spread(): lax.ppermute(down[-1], 'narrow', [(k, k - 1) for k in range(1, n - step +...]
    another operation x1 -> x40, other arithmetic: 0.05 us -> 33.9 us  [the longest x38 33.8 us: spread(): return jnp.stack(parts)]
    convert_element_type x24 -> x48, other arithmetic: 42.9 us -> 64.9 us  [the longest x24 25.7 us: sink(): one.astype(BF)]
    dot_general x42 -> x49, matrix products: 303 us -> 283 us  [the longest x12 73.2 us: right_inner(): lax.dot_general(left_side, right_side, (((left_side.ndim - 1,), (1,)), ((...]
  transfers between devices with their start and end apart: 34 -> 152, of which waited for: 33 -> 43; matrix products, arithmetic and copies ran while one was open for 13% -> 31% of each run, Pallas kernels for 0% -> 0%
where the time goes in v1:
time: 1270 us; the launch traced here: 1260 us
  starting transfers between devices  400 us (31%)
  waiting for transfers between devices  343 us (27%)
  matrix products  283 us (22%)
  other arithmetic  118 us (9%)
  local copies, waits for them, and re-layouts  52 us (4%)
  blocking collectives  46.3 us (4%)
  between operations  18.3 us (1%)
    ppermute x36, starting transfers between devices, sink(): lax.ppermute(one.astype(BF), 'narrow', [(k, k + 1) for k in range(step)])  207 us
    ppermute x33, waiting for transfers between devices, spread(): lax.ppermute(down[-1], 'narrow', [(k, k - 1) for k in range(1, n - step +...  192 us
    ppermute x33, starting transfers between devices, spread(): lax.ppermute(up[-1], 'narrow', [(k, k + 1) for k in range(step - 1, n - 1)])  111 us
    ppermute x36, waiting for transfers between devices, sink(): lax.ppermute(one.astype(BF), 'narrow', [(k, k + 1) for k in range(step)])  88.1 us
    dot_general x12, matrix products, right_inner(): lax.dot_general(left_side, right_side, (((left_side.ndim - 1,), (1,)), ((...  73.2 us
    dot_general x12, matrix products, product(): lax.dot_general(left_side, right_side, (((left_side.ndim - 1,), (0,)), ((...  70 us
    dot_general x7, matrix products, left_inner(): lax.dot_general(left_side, right_side, ((rows, rows), ((), ())), preferre...  53.6 us
    psum x1, blocking collectives, body(): lax.psum(jnp.stack([norm_sums(grad_n1, xhat1), sum(sums2), sum(sums3)]),...  46.3 us
  transfers between devices with their start and end apart: 152, of which 43 were waited for; matrix products, arithmetic and copies ran while one was open for 31% of the time, Pallas kernels for 0%

profile of v1, /device:TPU:0, one launch (start us, length us, event | category | flops | bytes accessed | tf_op | source)
XLA Modules:
  0.0 1260.4 jit_solution(11094651704214098811)
XLA Ops:
  29.6 20.4 %collective-permute-done = bf16[256,2048]{1,0:T(8,128)(2,1)} collective-permute-done((bf16[256,2048]{1,0:T(8,128)(2,1)}, bf16[256,2048]{1,0:T(8,128)(2,1)}, u32[]{:S(2)}, u32[]{:S(2)}) %collective-permute-start) | collective-permute-done | bytes 1048608 | tf_op jit(solution)/shard_map/ppermute | solution.py:44
  67.9 15.2 %collective-permute-done.13 = bf16[128,4096]{1,0:T(8,128)(2,1)} collective-permute-done((bf16[128,4096]{1,0:T(8,128)(2,1)}, bf16[128,4096]{1,0:T(8,128)(2,1)}, u32[]{:S(2)}, u32[]{:S(2)}) %collective-permute-start.13) | collective-permute-done | bytes 1048608 | tf_op jit(solution)/shard_map/ppermute | solution.py:45
  86.0 19.5 %collective-permute-done.2 = bf16[256,2048]{1,0:T(8,128)(2,1)} collective-permute-done((bf16[256,2048]{1,0:T(8,128)(2,1)}, bf16[256,2048]{1,0:T(8,128)(2,1)}, u32[]{:S(2)}, u32[]{:S(2)}) %collective-permute-start.2) | collective-permute-done | bytes 1048608 | tf_op jit(solution)/shard_map/ppermute | solution.py:45
  111.1 37.3 %collective-permute-done.3 = bf16[256,2048]{1,0:T(8,128)(2,1)S(1)} collective-permute-done((bf16[256,2048]{1,0:T(8,128)(2,1)}, bf16[256,2048]{1,0:T(8,128)(2,1)S(1)}, u32[]{:S(2)}, u32[]{:S(2)}) %collective-permute-start.3) | collective-permute-done | bytes 1048608 | tf_op jit(solution)/shard_map/ppermute | solution.py:45
  149.5 10.5 fusion.97
  255.8 15.9 %collective-permute-start.18 = (bf16[128,2048]{1,0:T(8,128)(2,1)S(1)}, bf16[128,2048]{1,0:T(8,128)(2,1)S(1)}, u32[]{:S(2)}, u32[]{:S(2)}) collective-permute-start(bf16[128,2048]{1,0:T(8,128)(2,1)S(1)} %get-tuple-element.167), channel_id=1, source_target_pairs={{0,1},{1,2},{2,3},{4,5},{5,6},{6,7},{8,9},{9,10},{10,11},{12,13},{... | collective-permute-start | bytes 1572872 | tf_op jit(solution)/shard_map/ppermute | solution.py:44
  313.5 34.7 %collective-permute-done.21 = bf16[128,2048]{1,0:T(8,128)(2,1)S(1)} collective-permute-done((bf16[128,2048]{1,0:T(8,128)(2,1)S(1)}, bf16[128,2048]{1,0:T(8,128)(2,1)S(1)}, u32[]{:S(2)}, u32[]{:S(2)}) %collective-permute-start.21) | collective-permute-done | bytes 524320 | tf_op jit(solution)/shard_map/ppermute | solution.py:45
  414.5 21.3 %collective-permute-start.55 = (bf16[128,2048]{1,0:T(8,128)(2,1)S(1)}, bf16[128,2048]{1,0:T(8,128)(2,1)S(1)}, u32[]{:S(2)}, u32[]{:S(2)}) collective-permute-start(bf16[128,2048]{1,0:T(8,128)(2,1)S(1)} %get-tuple-element.128), channel_id=1, source_target_pairs={{0,1},{1,2},{4,5},{5,6},{8,9},{9,10},{12,13},{13,14},{16,17},{17,1... | collective-permute-start | bytes 1572872 | tf_op jit(solution)/shard_map/ppermute | solution.py:58
  449.5 10.2 collective-permute-start.56
  486.2 15.6 %collective-permute-start.60 = (bf16[128,2048]{1,0:T(8,128)(2,1)S(1)}, bf16[128,2048]{1,0:T(8,128)(2,1)S(1)}, u32[]{:S(2)}, u32[]{:S(2)}) collective-permute-start(bf16[128,2048]{1,0:T(8,128)(2,1)S(1)} %get-tuple-element.166), channel_id=1, source_target_pairs={{0,1},{1,2},{2,3},{4,5},{5,6},{6,7},{8,9},{9,10},{10,11},{12,13},{... | collective-permute-start | bytes 1572872 | tf_op jit(solution)/shard_map/ppermute | solution.py:44
  542.2 11.9 multiply_convert_fusion.3
  554.1 10.5 fusion.36
  572.1 11.0 fusion.29
  584.5 11.9 convolution_bitcast_fusion.1
  610.0 9.3 fusion.129
  633.4 11.2 convolution_bitcast_fusion.2
  664.6 11.7 collective-permute-start.67
  678.6 10.4 collective-permute-start.37
  700.0 10.2 collective-permute-start.98
  711.9 10.2 collective-permute-start.68
  723.8 9.4 collective-permute-start.38
  735.0 9.5 collective-permute-start.80
  777.0 9.4 collective-permute-start.102
  905.4 10.0 collective-permute-start.109
  981.7 10.1 convolution_convert_fusion
  999.9 10.2 collective-permute-done.123
  1045.0 10.0 fusion.224
  1056.4 9.9 fusion.221
  1097.9 19.3 %collective-permute-done.126 = bf16[256,2048]{1,0:T(8,128)(2,1)S(1)} collective-permute-done((bf16[256,2048]{1,0:T(8,128)(2,1)S(1)}, bf16[256,2048]{1,0:T(8,128)(2,1)S(1)}, u32[]{:S(2)}, u32[]{:S(2)}) %collective-permute-start.126) | collective-permute-done | bytes 1048608 | tf_op jit(solution)/shard_map/ppermute | solution.py:58
  1123.0 16.6 %collective-permute-done.132 = bf16[128,4096]{1,0:T(8,128)(2,1)S(1)} collective-permute-done((bf16[128,4096]{1,0:T(8,128)(2,1)S(1)}, bf16[128,4096]{1,0:T(8,128)(2,1)S(1)}, u32[]{:S(2)}, u32[]{:S(2)}) %collective-permute-start.132) | collective-permute-done | bytes 1048608 | tf_op jit(solution)/shard_map/ppermute | solution.py:58
  1148.3 13.8 %collective-permute-done.127 = bf16[256,2048]{1,0:T(8,128)(2,1)S(1)} collective-permute-done((bf16[256,2048]{1,0:T(8,128)(2,1)S(1)}, bf16[256,2048]{1,0:T(8,128)(2,1)S(1)}, u32[]{:S(2)}, u32[]{:S(2)}) %collective-permute-start.127) | collective-permute-done | bytes 1048608 | tf_op jit(solution)/shard_map/ppermute | solution.py:58
  1197.7 46.3 %psum.7 = f32[3,2,2048]{2,0,1:T(4,128)S(1)} all-reduce(f32[3,2,2048]{2,0,1:T(4,128)S(1)} %pad_maximum_fusion.14), channel_id=1, replica_groups=mesh['wide'=8,'narrow'=4] {'wide','narrow'}, use_global_device_ids=true, to_apply=%region_44.45 | all-reduce | flops 12288 | bytes 98304 | tf_op jit(solution)/shard_map/psum | solution.py:268
  (833 shorter events, 758.7 us)
Async XLA Ops:
  7.2 142.3 %all-gather.8.cloned.1.call-start = ((), (), s32[]{:S(2)}) async-start(), calls=%async_computation.7 | async-start | bytes 7077888 | tf_op jit(solution)/shard_map/all_gather | solution.py:139
  11.6 156.9 %all-gather.10.cloned.1.call-start = ((), (), s32[]{:S(2)}) async-start(), calls=%async_computation.8 | async-start | bytes 2359296 | tf_op jit(solution)/shard_map/all_gather | solution.py:144
  12.4 339.1 %all-gather.14.cloned.1.call-start = ((), (), s32[]{:S(2)}) async-start(), calls=%async_computation.10 | async-start | bytes 2359296 | tf_op jit(solution)/shard_map/all_gather | solution.py:139
  14.4 352.9 %all-gather.12.cloned.1.call-start = ((), (), s32[]{:S(2)}) async-start(), calls=%async_computation.9 | async-start | bytes 9437184 | tf_op jit(solution)/shard_map/all_gather | solution.py:139
  17.0 376.3 %all-gather.16.cloned.1.call-start = ((), (), s32[]{:S(2)}) async-start(), calls=%async_computation.11 | async-start | bytes 2359296 | tf_op jit(solution)/shard_map/all_gather | solution.py:144
  18.8 523.4 %all-gather.18.cloned.1.call-start = ((), (), s32[]{:S(2)}) async-start(), calls=%async_computation.12 | async-start | bytes 9437184 | tf_op jit(solution)/shard_map/all_gather | solution.py:139
  20.0 534.1 %all-gather.20.cloned.1.call-start = ((), (), s32[]{:S(2)}) async-start(), calls=%async_computation.13 | async-start | bytes 9437184 | tf_op jit(solution)/shard_map/all_gather | solution.py:144
  62.9 965.4 %reduce-scatter.10.cloned.1.call-start = ((), (), s32[]{:S(2)}) async-start(), calls=%async_computation.15 | async-start | bytes 9437184 | tf_op jit(solution)/shard_map/reduce_scatter | solution.py:147
  65.1 43.3 %collective-permute-start.5 = (bf16[256,2048]{1,0:T(8,128)(2,1)}, bf16[256,2048]{1,0:T(8,128)(2,1)}, u32[]{:S(2)}, u32[]{:S(2)}) collective-permute-start(bf16[256,2048]{1,0:T(8,128)(2,1)} %collective-permute-done.4), channel_id=1, source_target_pairs={{2,3},{6,7},{10,11},{14,15},{18,19},{22,23},{26,27},{30,31}} | collective-permute-start | bytes 3145736 | tf_op jit(solution)/shard_map/ppermute | solution.py:44
  83.1 94.0 %collective-permute-start.14 = (bf16[128,4096]{1,0:T(8,128)(2,1)}, bf16[128,4096]{1,0:T(8,128)(2,1)}, u32[]{:S(2)}, u32[]{:S(2)}) collective-permute-start(bf16[128,4096]{1,0:T(8,128)(2,1)} %collective-permute-done.13), channel_id=1, source_target_pairs={{1,0},{2,1},{5,4},{6,5},{9,8},{10,9},{13,12},{14,13},{17,16},{18,1... | collective-permute-start | bytes 3145736 | tf_op jit(solution)/shard_map/ppermute | solution.py:45
  84.4 118.8 %collective-permute-start.16 = (bf16[128,4096]{1,0:T(8,128)(2,1)}, bf16[128,4096]{1,0:T(8,128)(2,1)}, u32[]{:S(2)}, u32[]{:S(2)}) collective-permute-start(bf16[128,4096]{1,0:T(8,128)(2,1)} %collective-permute-done.12), channel_id=1, source_target_pairs={{1,2},{2,3},{5,6},{6,7},{9,10},{10,11},{13,14},{14,15},{17,18},{18... | collective-permute-start | bytes 3145736 | tf_op jit(solution)/shard_map/ppermute | solution.py:44
  186.0 44.0 %collective-permute-start.15 = (bf16[128,4096]{1,0:T(8,128)(2,1)}, bf16[128,4096]{1,0:T(8,128)(2,1)S(1)}, u32[]{:S(2)}, u32[]{:S(2)}) collective-permute-start(bf16[128,4096]{1,0:T(8,128)(2,1)} %collective-permute-done.14), channel_id=1, source_target_pairs={{1,0},{5,4},{9,8},{13,12},{17,16},{21,20},{25,24},{29,28}} | collective-permute-start | bytes 3145736 | tf_op jit(solution)/shard_map/ppermute | solution.py:45
  208.4 63.3 %collective-permute-start.73 = (bf16[256,2048]{1,0:T(8,128)(2,1)S(1)}, bf16[256,2048]{1,0:T(8,128)(2,1)}, u32[]{:S(2)}, u32[]{:S(2)}) collective-permute-start(bf16[256,2048]{1,0:T(8,128)(2,1)S(1)} %copy-done.46), channel_id=1, source_target_pairs={{1,0},{2,1},{3,2},{5,4},{6,5},{7,6},{9,8},{10,9},{11,10},{13,12},{... | collective-permute-start | bytes 3145736 | tf_op jit(solution)/shard_map/ppermute | solution.py:45
  231.4 64.6 %collective-permute-start.72 = (bf16[256,2048]{1,0:T(8,128)(2,1)S(1)}, bf16[256,2048]{1,0:T(8,128)(2,1)}, u32[]{:S(2)}, u32[]{:S(2)}) collective-permute-start(bf16[256,2048]{1,0:T(8,128)(2,1)S(1)} %copy-done.46), channel_id=1, source_target_pairs={{0,1},{1,2},{2,3},{4,5},{5,6},{6,7},{8,9},{9,10},{10,11},{12,13},{... | collective-permute-start | bytes 3145736 | tf_op jit(solution)/shard_map/ppermute | solution.py:44
  296.0 116.2 %collective-permute-start.74 = (bf16[256,2048]{1,0:T(8,128)(2,1)}, bf16[256,2048]{1,0:T(8,128)(2,1)}, u32[]{:S(2)}, u32[]{:S(2)}) collective-permute-start(bf16[256,2048]{1,0:T(8,128)(2,1)} %collective-permute-done.73), channel_id=1, source_target_pairs={{1,0},{2,1},{5,4},{6,5},{9,8},{10,9},{13,12},{14,13},{17,16},{18,1... | collective-permute-start | bytes 3145736 | tf_op jit(solution)/shard_map/ppermute | solution.py:45
  303.2 142.5 %collective-permute-start.76 = (bf16[256,2048]{1,0:T(8,128)(2,1)}, bf16[256,2048]{1,0:T(8,128)(2,1)}, u32[]{:S(2)}, u32[]{:S(2)}) collective-permute-start(bf16[256,2048]{1,0:T(8,128)(2,1)} %collective-permute-done.72), channel_id=1, source_target_pairs={{1,2},{2,3},{5,6},{6,7},{9,10},{10,11},{13,14},{14,15},{17,18},{18... | collective-permute-start | bytes 3145736 | tf_op jit(solution)/shard_map/ppermute | solution.py:44
  304.9 43.4 %collective-permute-start.21 = (bf16[128,2048]{1,0:T(8,128)(2,1)S(1)}, bf16[128,2048]{1,0:T(8,128)(2,1)S(1)}, u32[]{:S(2)}, u32[]{:S(2)}) collective-permute-start(bf16[128,2048]{1,0:T(8,128)(2,1)S(1)} %collective-permute-done.20), channel_id=1, source_target_pairs={{1,0},{5,4},{9,8},{13,12},{17,16},{21,20},{25,24},{29,28}} | collective-permute-start | bytes 1572872 | tf_op jit(solution)/shard_map/ppermute | solution.py:45
  311.1 46.8 %collective-permute-start.51 = (bf16[128,2048]{1,0:T(8,128)(2,1)}, bf16[128,2048]{1,0:T(8,128)(2,1)}, u32[]{:S(2)}, u32[]{:S(2)}) collective-permute-start(bf16[128,2048]{1,0:T(8,128)(2,1)} %collective-permute-done.50), channel_id=1, source_target_pairs={{1,0},{5,4},{9,8},{13,12},{17,16},{21,20},{25,24},{29,28}} | collective-permute-start | bytes 1572872 | tf_op jit(solution)/shard_map/ppermute | solution.py:45
  412.9 71.9 %collective-permute-start.75 = (bf16[256,2048]{1,0:T(8,128)(2,1)}, bf16[256,2048]{1,0:T(8,128)(2,1)S(1)}, u32[]{:S(2)}, u32[]{:S(2)}) collective-permute-start(bf16[256,2048]{1,0:T(8,128)(2,1)} %collective-permute-done.74), channel_id=1, source_target_pairs={{1,0},{5,4},{9,8},{13,12},{17,16},{21,20},{25,24},{29,28}} | collective-permute-start | bytes 3145736 | tf_op jit(solution)/shard_map/ppermute | solution.py:45
  448.4 55.5 %collective-permute-start.77 = (bf16[256,2048]{1,0:T(8,128)(2,1)}, bf16[256,2048]{1,0:T(8,128)(2,1)S(1)}, u32[]{:S(2)}, u32[]{:S(2)}) collective-permute-start(bf16[256,2048]{1,0:T(8,128)(2,1)} %collective-permute-done.76), channel_id=1, source_target_pairs={{2,3},{6,7},{10,11},{14,15},{18,19},{22,23},{26,27},{30,31}} | collective-permute-start | bytes 3145736 | tf_op jit(solution)/shard_map/ppermute | solution.py:44
  596.3 434.8 %reduce-scatter.8.cloned.1.call-start = ((), (), s32[]{:S(2)}) async-start(), calls=%async_computation.14 | async-start | bytes 9437184 | tf_op jit(solution)/shard_map/reduce_scatter | solution.py:150
  606.2 49.7 %collective-permute-start.96 = (bf16[128,2048]{1,0:T(8,128)(2,1)}, bf16[128,2048]{1,0:T(8,128)(2,1)}, u32[]{:S(2)}, u32[]{:S(2)}) collective-permute-start(bf16[128,2048]{1,0:T(8,128)(2,1)} %get-tuple-element.106), channel_id=1, source_target_pairs={{0,1},{4,5},{8,9},{12,13},{16,17},{20,21},{24,25},{28,29}} | collective-permute-start | bytes 1572872 | tf_op jit(solution)/shard_map/ppermute | solution.py:58
  608.5 48.3 %collective-permute-start.99 = (bf16[128,2048]{1,0:T(8,128)(2,1)}, bf16[128,2048]{1,0:T(8,128)(2,1)}, u32[]{:S(2)}, u32[]{:S(2)}) collective-permute-start(bf16[128,2048]{1,0:T(8,128)(2,1)} %get-tuple-element.107), channel_id=1, source_target_pairs={{3,2},{7,6},{11,10},{15,14},{19,18},{23,22},{27,26},{31,30}} | collective-permute-start | bytes 1572872 | tf_op jit(solution)/shard_map/ppermute | solution.py:59
  655.9 514.1 %reduce-scatter.12.cloned.1.call-start = ((), (), s32[]{:S(2)}) async-start(), calls=%async_computation.16 | async-start | bytes 2359296 | tf_op jit(solution)/shard_map/reduce_scatter | solution.py:150
  874.8 297.0 %reduce-scatter.14.cloned.1.call-start = ((), (), s32[]{:S(2)}) async-start(), calls=%async_computation.17 | async-start | bytes 2359296 | tf_op jit(solution)/shard_map/reduce_scatter | solution.py:147
  934.6 239.0 %reduce-scatter.20.cloned.1.call-start = ((), (), s32[]{:S(2)}) async-start(), calls=%async_computation.20 | async-start | bytes 2359296 | tf_op jit(solution)/shard_map/reduce_scatter | solution.py:150
  1020.8 174.0 %reduce-scatter.16.cloned.1.call-start = ((), (), s32[]{:S(2)}) async-start(), calls=%async_computation.18 | async-start | bytes 9437184 | tf_op jit(solution)/shard_map/reduce_scatter | solution.py:147
  1021.5 229.8 %reduce-scatter.18.cloned.1.call-start = ((), (), s32[]{:S(2)}) async-start(), calls=%async_computation.19 | async-start | bytes 7077888 | tf_op jit(solution)/shard_map/reduce_scatter | solution.py:147
  1095.4 44.2 %collective-permute-start.132 = (bf16[128,4096]{1,0:T(8,128)(2,1)S(1)}, bf16[128,4096]{1,0:T(8,128)(2,1)S(1)}, u32[]{:S(2)}, u32[]{:S(2)}) collective-permute-start(bf16[128,4096]{1,0:T(8,128)(2,1)S(1)} %get-tuple-element.73), channel_id=1, source_target_pairs={{0,1},{4,5},{8,9},{12,13},{16,17},{20,21},{24,25},{28,29}} | collective-permute-start | bytes 3145736 | tf_op jit(solution)/shard_map/ppermute | solution.py:58
  1117.8 44.3 %collective-permute-start.127 = (bf16[256,2048]{1,0:T(8,128)(2,1)S(1)}, bf16[256,2048]{1,0:T(8,128)(2,1)S(1)}, u32[]{:S(2)}, u32[]{:S(2)}) collective-permute-start(bf16[256,2048]{1,0:T(8,128)(2,1)S(1)} %get-tuple-element.77), channel_id=1, source_target_pairs={{0,1},{1,2},{4,5},{5,6},{8,9},{9,10},{12,13},{13,14},{16,17},{17,1... | collective-permute-start | bytes 3145736 | tf_op jit(solution)/shard_map/ppermute | solution.py:58
  1184.3 63.7 %collective-permute-start.134 = (bf16[128,4096]{1,0:T(8,128)(2,1)}, bf16[128,4096]{1,0:T(8,128)(2,1)}, u32[]{:S(2)}, u32[]{:S(2)}) collective-permute-start(bf16[128,4096]{1,0:T(8,128)(2,1)} %get-tuple-element.69), channel_id=1, source_target_pairs={{0,1},{1,2},{2,3},{4,5},{5,6},{6,7},{8,9},{9,10},{10,11},{12,13},{... | collective-permute-start | bytes 3145736 | tf_op jit(solution)/shard_map/ppermute | solution.py:58
  1190.0 58.0 %collective-permute-start.137 = (bf16[128,4096]{1,0:T(8,128)(2,1)}, bf16[128,4096]{1,0:T(8,128)(2,1)}, u32[]{:S(2)}, u32[]{:S(2)}) collective-permute-start(bf16[128,4096]{1,0:T(8,128)(2,1)} %get-tuple-element.70), channel_id=1, source_target_pairs={{1,0},{2,1},{3,2},{5,4},{6,5},{7,6},{9,8},{10,9},{11,10},{13,12},{... | collective-permute-start | bytes 3145736 | tf_op jit(solution)/shard_map/ppermute | solution.py:59
  (274 other events, 5994.7 us)
Sparse Core Ops, SparseCore 0:
  11.7 48.1 all-gather.7
  62.3 28.0 all-gather.9
  92.9 27.7 all-gather.13
  123.0 54.2 all-gather.11
  179.0 28.0 all-gather.15
  209.5 54.2 all-gather.17
  266.2 55.8 all-gather.19
  596.5 80.4 reduce-scatter.9
  680.4 71.2 reduce-scatter.7
  874.9 45.0 reduce-scatter.11
  934.7 43.1 reduce-scatter.13
  1020.9 40.3 reduce-scatter.19
  1064.8 71.5 reduce-scatter.15
  1139.6 61.7 reduce-scatter.17

commit v2 on v1

--- a/solution.py
+++ b/solution.py
@@ -36,28 +36,47 @@
     return lax.dot_general(left_side, right_side, ((rows, rows), ((), ())), preferred_element_type=F32)
 
 
-def spread(rows):
+def after(value, *others):
+    if not others:
+        return value
+    nothing = sum(o[(0,) * o.ndim].astype(F32) for o in others) * 0.0
+    return value + nothing.astype(value.dtype)
+
+
+def whole(value):
+    return lax.optimization_barrier(value)
+
+
+def spread(name, rows, gates={}):
     n = lax.axis_size("narrow")
     here = lax.axis_index("narrow")
-    up, down = [rows], [rows]
-    for step in range(1, n):
-        up.append(lax.ppermute(up[-1], "narrow", [(k, k + 1) for k in range(step - 1, n - 1)]))
-        down.append(lax.ppermute(down[-1], "narrow", [(k, k - 1) for k in range(1, n - step + 1)]))
-    parts = [rows] + [jnp.where(here >= s, up[s], down[n - s]) for s in range(1, n)]
-    return jnp.stack(parts)
-
-
-def sink(parts):
+    with jax.named_scope("spread_" + name):
+        up, down = [rows], [rows]
+        for step in range(1, n):
+            one, other = after(up[-1], *gates.get(step, ())), after(down[-1], *gates.get(step, ()))
+            up.append(lax.ppermute(one, "narrow", [(k, k + 1) for k in range(step - 1, n - 1)]))
+            down.append(lax.ppermute(other, "narrow", [(k, k - 1) for k in range(1, n - step + 1)]))
+        parts = [rows] + [jnp.where(here >= s, up[s], down[n - s]) for s in range(1, n)]
+        return jnp.stack(parts), [(up[s], down[s]) for s in range(1, n)]
+
+
+def sink(name, parts, gates={}):
     n = lax.axis_size("narrow")
-    up = down = None
-    for step in range(1, n):
-        one, other = parts[step], parts[n - step]
-        if up is not None:
-            one = up.astype(F32) + one.astype(F32)
-            other = down.astype(F32) + other.astype(F32)
-        up = lax.ppermute(one.astype(BF), "narrow", [(k, k + 1) for k in range(step)])
-        down = lax.ppermute(other.astype(BF), "narrow", [(k, k - 1) for k in range(n - step, n)])
-    return up.astype(F32) + down.astype(F32) + parts[0].astype(F32)
+    hops = []
+    with jax.named_scope("sink_" + name):
+        for step in range(1, n):
+            one, other = parts[step], parts[n - step]
+            gate = gates.get(step, ())
+            if callable(gate):
+                gate = gate(hops[0])
+            if hops:
+                one = hops[-1][0].astype(F32) + one.astype(F32)
+                other = hops[-1][1].astype(F32) + other.astype(F32)
+            one, other = after(one, *gate), after(other, *gate)
+            up = lax.ppermute(one.astype(BF), "narrow", [(k, k + 1) for k in range(step)])
+            down = lax.ppermute(other.astype(BF), "narrow", [(k, k - 1) for k in range(n - step, n)])
+            hops.append((up, down))
+        return up.astype(F32) + down.astype(F32) + parts[0].astype(F32), hops
 
 
 def norm_stats(features):
@@ -101,10 +120,6 @@
     grad_queries = jnp.einsum("ihpq,iqhe->iphe", grad_scores, keys_in, preferred_element_type=F32)
     grad_keys = jnp.einsum("ihpq,iphe->iqhe", grad_scores, queries, preferred_element_type=F32)
     return grad_queries.astype(BF), grad_keys, grad_values
-
-
-def after(value, *others):
-    return lax.optimization_barrier((value, *others))[0]
 
 
 def body(
@@ -160,7 +175,7 @@
     residual0 = tokens.astype(F32)
     xhat1, rstd1 = norm_stats(residual0)
     own1 = (xhat1 * norm_gains[0] + norm_shifts[0]).astype(BF)
-    normed1 = spread(own1)
+    normed1 = spread("n1", own1)[0]
     qkv = product(normed1, full_qkv).astype(BF)
     heads_of = lambda x: x.reshape(x.shape[:-1] + (x.shape[-1] // HEAD_DIM, HEAD_DIM))
     self_q, self_k, self_v = [heads_of(qkv[..., k * width : (k + 1) * width]) for k in range(3)]
@@ -169,7 +184,7 @@
     self_mix, self_total = attend(self_q, self_k, self_v, self_allowed, scale)
     self_mix = self_mix.reshape(n, PIX, width)
 
-    text = spread(after(captions, normed1))
+    text = spread("text", after(captions, normed1[1], normed1[n - 1]), {2: (self_mix,)})[0]
     text_count = text.shape[0] * text.shape[1]
     text_rows = text.reshape(text_count, text.shape[2])
     ckv = product(text_rows, full_ckv).astype(BF)
@@ -180,90 +195,145 @@
     cross_allowed = (part_image[:, None] == owner[None, :])[None]
 
     state = []
-    for rows in chunks:
-        residual1 = residual0[rows] + sink(product(self_mix[:, rows], full_out).astype(BF))
+    for c, rows in enumerate(chunks):
+        residual1 = residual0[rows] + sink(f"r1_{c}", product(self_mix[:, rows], full_out).astype(BF))[0]
         xhat2, rstd2 = norm_stats(residual1)
         state.append((residual1, xhat2, rstd2))
-    normed2 = [spread((s[1] * norm_gains[1] + norm_shifts[1]).astype(BF)) for s in state]
-    grad_all = spread(after(out_grad, normed2[0]))
+    normed2 = [
+        spread(f"n2_{c}", (s[1] * norm_gains[1] + norm_shifts[1]).astype(BF))[0] for c, s in enumerate(state)
+    ]
+    grad_all, og_hops = spread("og", after(out_grad, normed2[0][1], normed2[0][n - 1]))
 
     cross_q, cross_mix, cross_total, state3 = [], [], [], []
     for c in range(CHUNKS):
+        if c > 0:
+            normed2[c] = after(normed2[c], sent, *og_hops[0])
         q = heads_of(product(normed2[c], full_cq).astype(BF).reshape(1, n * part, width))
         mix, total = attend(q, cross_k, cross_v, cross_allowed, scale)
         mix = mix.reshape(n, part, width)
-        residual2 = state[c][0] + sink(product(mix, full_cout).astype(BF))
+        sent = whole(product(mix, full_cout).astype(BF))
+        residual2 = state[c][0] + sink(f"r2_{c}", sent)[0]
         xhat3, rstd3 = norm_stats(residual2)
         cross_q.append(q)
         cross_mix.append(mix)
         cross_total.append(total)
         state3.append((residual2, xhat3, rstd3))
-    normed3 = [spread((s[1] * norm_gains[2] + norm_shifts[2]).astype(BF)) for s in state3]
-
-    block_out, acts, grad_hiddens, grad2, sums3 = [], [], [], [], []
+    normed3 = [
+        spread(f"n3_{c}", (s[1] * norm_gains[2] + norm_shifts[2]).astype(BF))[0] for c, s in enumerate(state3)
+    ]
+
+    cat = lambda xs: jnp.concatenate(xs, axis=1)
+    acts, grad_hiddens, parts3 = [], [], []
     for c, rows in enumerate(chunks):
+        if c > 0:
+            normed3[c] = after(normed3[c], parts3[c - 1])
         hidden = product(normed3[c], full_up)
         grad_rows = grad_all[:, rows]
         acted, gelu_back = jax.vjp(jax.nn.gelu, hidden)
-        acted = acted.astype(BF)
         grad_hidden = gelu_back(right_inner(grad_rows, full_down))[0].astype(BF)
-        acts.append(acted)
+        if c > 0:
+            grad_hidden = after(grad_hidden, *hops3[0])
+        acts.append(acted.astype(BF))
         grad_hiddens.append(grad_hidden)
-        grad_n3 = sink(right_inner(grad_hidden, full_up).astype(BF))
-        residual2, xhat3, rstd3 = state3[c]
-        sums3.append(norm_sums(grad_n3, xhat3))
-        grad2.append(out_grad[rows].astype(F32) + norm_back(grad_n3, xhat3, rstd3, norm_gains[2]))
-        block_out.append(
-            (residual2 + sink(product(acted, full_down).astype(BF))).astype(BF)
-        )
-    cat = lambda xs: jnp.concatenate(xs, axis=1)
-    acted, grad_hidden, n3 = cat(acts), cat(grad_hiddens), cat(normed3)
-    grad_down = left_inner(acted, cat([grad_all[:, rows] for rows in chunks]))
-    grad_up = left_inner(n3, grad_hidden)
-
-    e2 = [spread(g.astype(BF)) for g in grad2]
+        parts3.append(whole(right_inner(grad_hidden, full_up).astype(BF)))
+        if c == 0:
+            grad_n3, hops3 = sink("d3_0", parts3[0])
+            grad_n3s = [grad_n3]
+    down_parts = [whole(product(after(acted, parts3[-1]), full_down).astype(BF)) for acted in acts]
+
+    late = {}
+
+    def down_weight(hop):
+        every = cat([grad_all[:, rows] for rows in chunks])
+        late["down"] = whole(left_inner(after(cat(acts), *hop, *down_parts), every).astype(BF))
+        return (late["down"],)
+
+    for c in range(1, CHUNKS):
+        grad_n3, hops3 = sink(f"d3_{c}", parts3[c], {2: down_parts, 3: down_weight} if c == CHUNKS - 1 else {})
+        grad_n3s.append(grad_n3)
+    grad_down = late["down"]
+    grad_up = whole(left_inner(after(cat(normed3), *hops3[1]), cat(grad_hiddens)).astype(BF))
     own_down = to_columns(grad_down)
     own_up = to_rows(grad_up)
-    e2[-1] = after(e2[-1], grad_down, grad_up)
-    grad1, sums2, grad_cqs, grad_ck, grad_cv = [], [], [], 0.0, 0.0
+    grad2, sums3, e2 = [], [], []
+    for c, rows in enumerate(chunks):
+        _, xhat3, rstd3 = state3[c]
+        sums3.append(norm_sums(grad_n3s[c], xhat3))
+        grad2.append(
+            out_grad[rows].astype(F32) + norm_back(grad_n3s[c], xhat3, rstd3, norm_gains[2])
+        )
+        e2.append(spread(f"e2_{c}", grad2[c].astype(BF), {1: (grad_up,) if c > 0 else ()})[0])
+
+    all_parts = [jnp.concatenate([p[k] for p in down_parts]) for k in range(n)]
+    out_sum, out_hops = sink("out", all_parts, {1: (e2[-1][1], e2[-1][n - 1])})
+    block_out = (jnp.concatenate([s[0] for s in state3]) + out_sum).astype(BF)
+    parts2, grad_cqs, grad_ck, grad_cv = [], [], 0.0, 0.0
     for c in range(CHUNKS):
-        grad_mix = heads_of(right_inner(e2[c], full_cout).astype(BF).reshape(1, n * part, width))
+        if c > 0:
+            e2[c] = after(e2[c], parts2[c - 1])
+        grad_mix = right_inner(e2[c], full_cout).astype(BF).reshape(1, n * part, width)
+        if c > 0:
+            grad_mix = after(grad_mix, *out_hops[0])
         gq, gk, gv = attend_back(
-            cross_q[c], cross_k, cross_v, cross_allowed, cross_total[c], grad_mix, scale
+            cross_q[c], cross_k, cross_v, cross_allowed, cross_total[c], heads_of(grad_mix), scale
         )
         gq = gq.reshape(n, part, width)
         grad_cqs.append(gq)
         grad_ck = grad_ck + gk
         grad_cv = grad_cv + gv
-        grad_n2 = sink(right_inner(gq, full_cq).astype(BF))
+        parts2.append(whole(right_inner(gq, full_cq).astype(BF)))
+    grad_ckv = jnp.concatenate(
+        [grad_ck.reshape(text_count, width), grad_cv.reshape(text_count, width)], axis=1
+    ).astype(BF)
+    def cross_weights(hop):
+        late["cout"] = whole(left_inner(after(cat(cross_mix), own_down, *hop), cat(e2)).astype(BF))
+        late["cq"] = whole(left_inner(cat(normed2), after(cat(grad_cqs), *hop)).astype(BF))
+        return late["cout"], late["cq"]
+
+    grad1, sums2, e1 = [], [], []
+    for c in range(CHUNKS):
+        last = c == CHUNKS - 1
+        grad_n2, hops2 = sink(f"d2_{c}", parts2[c], {2: (grad_ckv,), 3: cross_weights} if last else {})
         _, xhat2, rstd2 = state[c]
         sums2.append(norm_sums(grad_n2, xhat2))
         grad1.append(grad2[c] + norm_back(grad_n2, xhat2, rstd2, norm_gains[1]))
-    grad_cout = left_inner(cat(cross_mix), cat(e2))
-    grad_cq = left_inner(cat(normed2), cat(grad_cqs))
-    grad_ckv = jnp.concatenate(
-        [grad_ck.reshape(text_count, width), grad_cv.reshape(text_count, width)], axis=1
-    ).astype(BF)
-    grad_text_part = right_inner(grad_ckv, full_ckv).astype(BF).reshape(n, -1, text.shape[2])
-    grad_wckv = left_inner(text_rows, grad_ckv)
-
-    e1 = [spread(g.astype(BF)) for g in grad1]
-    own_cout = to_columns(grad_cout)
-    own_cq = to_rows(grad_cq)
+        if last:
+            grad_wckv = whole(left_inner(text_rows, after(grad_ckv, own_up, *hops2[1])).astype(BF))
+            grad_text_part = whole(
+                right_inner(after(grad_ckv, *hops2[1]), full_ckv).astype(BF).reshape(n, -1, text.shape[2])
+            )
+        e1.append(spread(f"e1_{c}", grad1[c].astype(BF), {1: (grad_wckv,), 2: (grad_text_part,)} if last else {})[0])
+    own_cout = to_columns(late["cout"])
+    own_cq = to_rows(late["cq"])
     own_ckv = to_rows(grad_wckv)
-    e1[-1] = after(e1[-1], grad_cout, grad_cq, grad_wckv, grad_text_part)
-    grad_mix = heads_of(cat([right_inner(e, full_out).astype(BF) for e in e1]))
-    grad_mix = after(grad_mix, own_down, own_up)
-    gq, gk, gv = attend_back(self_q, self_k, self_v, self_allowed, self_total, grad_mix, scale)
-    grad_qkv = jnp.concatenate(
-        [g.astype(BF).reshape(n, PIX, width) for g in (gq, gk, gv)], axis=-1
-    )
-    grad_out = left_inner(self_mix, cat(e1))
+
+    grad_text, text_hops = sink("text", grad_text_part, {1: (e1[-1][1], e1[-1][n - 1])})
+    grad_text = grad_text.astype(BF)
+    odd = [k for k in range(n) if k != 0 and k != n // 2]
+    even = [0, n // 2]
+    pieces = [None] * n
+    grad_parts = [None] * n
+    for group, which in enumerate((odd, even)):
+        pick = lambda x: jnp.stack([x[k] for k in which])
+        grad_mix = cat([right_inner(pick(e), full_out).astype(BF) for e in e1])
+        if group > 0:
+            grad_mix = after(grad_mix, back, own_cout, own_cq)
+        gq, gk, gv = attend_back(
+            pick(self_q), pick(self_k), pick(self_v), pick(self_allowed), pick(self_total), heads_of(grad_mix), scale
+        )
+        grads = jnp.concatenate(
+            [g.astype(BF).reshape(len(which), PIX, width) for g in (gq, gk, gv)], axis=-1
+        )
+        moved = text_hops[0] if group == 0 else ()
+        back = whole(right_inner(after(grads, *moved), full_qkv).astype(BF))
+        for i, k in enumerate(which):
+            pieces[k] = grads[i]
+            grad_parts[k] = back[i]
+    grad_n1, hops1 = sink("d1", grad_parts)
+    grad_qkv = after(jnp.stack(pieces), *hops1[0])
     grad_wqkv = left_inner(normed1, grad_qkv)
-    grad_n1 = sink(right_inner(after(grad_qkv, grad_wqkv), full_qkv).astype(BF))
-    grad_text = sink(after(grad_text_part, grad_mix)).astype(BF)
+    grad_out = sum(left_inner(self_mix[:, rows], e) for rows, e in zip(chunks, e1))
     grad1 = jnp.concatenate(grad1)
-    grad_n1 = after(grad_n1, own_cout, own_cq, own_ckv)
     grad_tokens = (grad1 + norm_back(grad_n1, xhat1, rstd1, norm_gains[0])).astype(BF)
     sums = lax.psum(
         jnp.stack([norm_sums(grad_n1, xhat1), sum(sums2), sum(sums3)]), ("wide", "narrow")
@@ -272,7 +342,7 @@
     own_out = to_columns(grad_out)
     own_qkv = to_rows(grad_wqkv)
     return (
-        jnp.concatenate(block_out),
+        block_out,
         grad_tokens,
         grad_text,
         sums[:, 0],

time: 1270 us -> 1330 us (1.047)
  starting transfers between devices: 400 us -> 328 us
  local copies, waits for them, and re-layouts: 52 us -> 119 us
  between operations: 18.3 us -> 53 us
  other arithmetic: 118 us -> 151 us
    ppermute x36 -> x33, starting transfers between devices: 207 us -> 143 us  [sink(): lax.ppermute(one.astype(BF), 'narrow', [(k, k + 1) for k in range(step)])]
    slice x1 -> x51, local copies, waits for them, and re-layouts: 1.69 us -> 43.3 us  [the longest x45 40.1 us: after(): nothing = sum((o[(0,) * o.ndim].astype(F32) for o in others)) * 0.0]
    ppermute x36 -> x33, waiting for transfers between devices: 41.4 us -> 21.5 us  [sink(): lax.ppermute(other.astype(BF), 'narrow', [(k, k - 1) for k in range(n - s...]
    ppermute x66, waiting for transfers between devices: 212 us -> 231 us  [the longest x33 227 us: spread(): lax.ppermute(other, 'narrow', [(k, k - 1) for k in range(1, n - step + 1)])]
    unnamed x308 -> x474, local copies, waits for them, and re-layouts: 16.1 us -> 28.7 us
    convert_element_type x24 -> x22, other arithmetic: 25.7 us -> 37 us  [sink(): one.astype(BF)]
    ppermute x36 -> x33, waiting for transfers between devices: 88.1 us -> 77 us  [sink(): lax.ppermute(one.astype(BF), 'narrow', [(k, k + 1) for k in range(step)])]
    dot_general x7 -> x8, matrix products: 53.6 us -> 62.4 us  [left_inner(): lax.dot_general(left_side, right_side, ((rows, rows), ((), ())), preferre...]
  transfers between devices with their start and end apart: 152 -> 146, of which waited for: 43 -> 42; matrix products, arithmetic and copies ran while one was open for 31% -> 38% of each run, Pallas kernels for 0% -> 0%
where the time goes in v2:
time: 1330 us; the launch traced here: 1310 us
  waiting for transfers between devices  330 us (25%)
  starting transfers between devices  328 us (25%)
  matrix products  290 us (22%)
  other arithmetic  151 us (11%)
  local copies, waits for them, and re-layouts  119 us (9%)
  between operations  53 us (4%)
  blocking collectives  40.8 us (3%)
    ppermute x33, waiting for transfers between devices, spread(): lax.ppermute(other, 'narrow', [(k, k - 1) for k in range(1, n - step + 1)])  227 us
    ppermute x33, starting transfers between devices, sink(): lax.ppermute(one.astype(BF), 'narrow', [(k, k + 1) for k in range(step)])  143 us
    ppermute x33, starting transfers between devices, spread(): lax.ppermute(one, 'narrow', [(k, k + 1) for k in range(step - 1, n - 1)])  99.1 us
    ppermute x33, waiting for transfers between devices, sink(): lax.ppermute(one.astype(BF), 'narrow', [(k, k + 1) for k in range(step)])  77 us
    dot_general x12, matrix products, product(): lax.dot_general(left_side, right_side, (((left_side.ndim - 1,), (0,)), ((...  65.4 us
    dot_general x15, matrix products, right_inner(): lax.dot_general(left_side, right_side, (((left_side.ndim - 1,), (1,)), ((...  64.7 us
    dot_general x8, matrix products, left_inner(): lax.dot_general(left_side, right_side, ((rows, rows), ((), ())), preferre...  62.4 us
    ppermute x33, starting transfers between devices, spread(): lax.ppermute(other, 'narrow', [(k, k - 1) for k in range(1, n - step + 1)])  43.2 us
  transfers between devices with their start and end apart: 146, of which 42 were waited for; matrix products, arithmetic and copies ran while one was open for 38% of the time, Pallas kernels for 0%

profile of v2, /device:TPU:0, one launch (start us, length us, event | category | flops | bytes accessed | tf_op | source)
XLA Modules:
  0.0 1312.5 jit_solution(14613554446413724819)
XLA Ops:
  25.0 21.2 %collective-permute-done.1 = bf16[256,2048]{1,0:T(8,128)(2,1)S(1)} collective-permute-done((bf16[256,2048]{1,0:T(8,128)(2,1)S(1)}, bf16[256,2048]{1,0:T(8,128)(2,1)S(1)}, u32[]{:S(2)}, u32[]{:S(2)}) %collective-permute-start.1) | collective-permute-done | bytes 1048608 | tf_op jit(solution)/shard_map/spread_n1/ppermute | solution.py:58
  49.7 22.9 %collective-permute-done.2 = bf16[256,2048]{1,0:T(8,128)(2,1)} collective-permute-done((bf16[256,2048]{1,0:T(8,128)(2,1)S(1)}, bf16[256,2048]{1,0:T(8,128)(2,1)}, u32[]{:S(2)}, u32[]{:S(2)}) %collective-permute-start.2) | collective-permute-done | bytes 1048608 | tf_op jit(solution)/shard_map/spread_n1/ppermute | solution.py:58
  76.8 21.5 %collective-permute-done.3 = bf16[256,2048]{1,0:T(8,128)(2,1)} collective-permute-done((bf16[256,2048]{1,0:T(8,128)(2,1)}, bf16[256,2048]{1,0:T(8,128)(2,1)}, u32[]{:S(2)}, u32[]{:S(2)}) %collective-permute-start.3) | collective-permute-done | bytes 1048608 | tf_op jit(solution)/shard_map/spread_n1/ppermute | solution.py:58
  104.6 9.4 fusion.76
  191.5 12.3 collective-permute-start.12
  208.9 14.3 %collective-permute-start.36 = (bf16[128,2048]{1,0:T(8,128)(2,1)S(1)}, bf16[128,2048]{1,0:T(8,128)(2,1)S(1)}, u32[]{:S(2)}, u32[]{:S(2)}) collective-permute-start(bf16[128,2048]{1,0:T(8,128)(2,1)S(1)} %get-tuple-element.170), channel_id=1, source_target_pairs={{0,1},{1,2},{2,3},{4,5},{5,6},{6,7},{8,9},{9,10},{10,11},{12,13},{... | collective-permute-start | bytes 1572872 | tf_op jit(solution)/shard_map/spread_n2_1/ppermute | solution.py:57
  246.8 9.2 collective-permute-done.19
  279.6 19.4 %collective-permute-done.21 = bf16[128,2048]{1,0:T(8,128)(2,1)S(1)} collective-permute-done((bf16[128,2048]{1,0:T(8,128)(2,1)S(1)}, bf16[128,2048]{1,0:T(8,128)(2,1)S(1)}, u32[]{:S(2)}, u32[]{:S(2)}) %collective-permute-start.21) | collective-permute-done | bytes 524320 | tf_op jit(solution)/shard_map/spread_n2_0/ppermute | solution.py:58
  322.4 9.1 convolution_convert_fusion.8
  347.6 16.1 %collective-permute-start.24 = (bf16[128,2048]{1,0:T(8,128)(2,1)}, bf16[128,2048]{1,0:T(8,128)(2,1)}, u32[]{:S(2)}, u32[]{:S(2)}) collective-permute-start(bf16[128,2048]{1,0:T(8,128)(2,1)} %get-tuple-element.110), channel_id=1, source_target_pairs={{0,1},{4,5},{8,9},{12,13},{16,17},{20,21},{24,25},{28,29}} | collective-permute-start | bytes 1572872 | tf_op jit(solution)/shard_map/sink_r2_0/ppermute | solution.py:76
  430.9 11.8 collective-permute-start.46
  451.8 13.9 %collective-permute-start.60 = (bf16[128,2048]{1,0:T(8,128)(2,1)S(1)}, bf16[128,2048]{1,0:T(8,128)(2,1)S(1)}, u32[]{:S(2)}, u32[]{:S(2)}) collective-permute-start(bf16[128,2048]{1,0:T(8,128)(2,1)S(1)} %get-tuple-element.168), channel_id=1, source_target_pairs={{0,1},{1,2},{2,3},{4,5},{5,6},{6,7},{8,9},{9,10},{10,11},{12,13},{... | collective-permute-start | bytes 1572872 | tf_op jit(solution)/shard_map/spread_n3_1/ppermute | solution.py:57
  476.0 29.8 %collective-permute-done.61 = bf16[128,2048]{1,0:T(8,128)(2,1)S(1)} collective-permute-done((bf16[128,2048]{1,0:T(8,128)(2,1)S(1)}, bf16[128,2048]{1,0:T(8,128)(2,1)S(1)}, u32[]{:S(2)}, u32[]{:S(2)}) %collective-permute-start.61) | collective-permute-done | bytes 524320 | tf_op jit(solution)/shard_map/spread_n3_1/ppermute | solution.py:58
  508.5 8.5 collective-permute-done.51
  537.3 9.8 collective-permute-done.53
  548.0 11.9 multiply_convert_fusion.3
  559.9 10.5 fusion.32
  592.0 9.2 fusion.118
  611.3 8.2 fusion.111
  632.1 14.1 %bitcast_convert_fusion.1 = bf16[2048,2048]{1,0:T(8,128)(2,1)} fusion(bf16[4,128,2048]{2,1,0:T(8,128)(2,1)} %copy-done.230, bf16[4,128,2048]{2,1,0:T(8,128)(2,1)} %get-tuple-element.187, bf16[]{:T(256)S(6)} %mul.553, bf16[1,256,2048]{2,1,0:T(8,128)(2,1)} %copy-done.72, bf16[1,256,2048]{2,1,0:T(8,128)(2,1)} %copy-done.71, ...), kind=kOutput, calls=%fused_computation.7 | convolution fusion | flops 8613003264 | bytes 16777218 | tf_op jit(solution)/shard_map/sink_d3_1/dot_general | solution.py:36
  664.8 8.6 collective-permute-done.86
  690.9 12.9 bitcast_convert_fusion
  784.6 9.9 fusion.279
  808.4 10.2 fusion.122
  835.1 8.8 fusion.282
  859.1 8.8 fusion.241
  943.5 10.4 convolution_convert_fusion
  996.3 10.4 collective-permute-done.110
  1026.1 9.4 collective-permute-done.117
  1140.1 8.8 bitcast_convert_fusion.2
  1179.0 26.9 %collective-permute-done.128 = bf16[128,4096]{1,0:T(8,128)(2,1)S(1)} collective-permute-done((bf16[128,4096]{1,0:T(8,128)(2,1)S(1)}, bf16[128,4096]{1,0:T(8,128)(2,1)S(1)}, u32[]{:S(2)}, u32[]{:S(2)}) %collective-permute-start.128) | collective-permute-done | bytes 1048608 | tf_op jit(solution)/shard_map/sink_text/ppermute | solution.py:76
  1254.9 40.8 %psum.7 = f32[3,2,2048]{2,0,1:T(4,128)S(1)} all-reduce(f32[3,2,2048]{2,0,1:T(4,128)S(1)} %pad_maximum_fusion.16), channel_id=1, replica_groups=mesh['wide'=8,'narrow'=4] {'wide','narrow'}, use_global_device_ids=true, to_apply=%region_44.45 | all-reduce | flops 12288 | bytes 98304 | tf_op jit(solution)/shard_map/psum | solution.py:338
  (1071 shorter events, 810.4 us)
Async XLA Ops:
  7.2 97.4 %all-gather.8.cloned.1.call-start = ((), (), s32[]{:S(2)}) async-start(), calls=%async_computation.7 | async-start | bytes 7077888 | tf_op jit(solution)/shard_map/all_gather | solution.py:154
  11.6 111.0 %all-gather.10.cloned.1.call-start = ((), (), s32[]{:S(2)}) async-start(), calls=%async_computation.8 | async-start | bytes 2359296 | tf_op jit(solution)/shard_map/all_gather | solution.py:159
  12.4 295.9 %all-gather.14.cloned.1.call-start = ((), (), s32[]{:S(2)}) async-start(), calls=%async_computation.10 | async-start | bytes 2359296 | tf_op jit(solution)/shard_map/all_gather | solution.py:154
  13.2 309.1 %all-gather.12.cloned.1.call-start = ((), (), s32[]{:S(2)}) async-start(), calls=%async_computation.9 | async-start | bytes 9437184 | tf_op jit(solution)/shard_map/all_gather | solution.py:154
  14.6 327.5 %all-gather.16.cloned.1.call-start = ((), (), s32[]{:S(2)}) async-start(), calls=%async_computation.11 | async-start | bytes 2359296 | tf_op jit(solution)/shard_map/all_gather | solution.py:159
  15.4 532.6 %all-gather.18.cloned.1.call-start = ((), (), s32[]{:S(2)}) async-start(), calls=%async_computation.12 | async-start | bytes 9437184 | tf_op jit(solution)/shard_map/all_gather | solution.py:154
  16.7 543.2 %all-gather.20.cloned.1.call-start = ((), (), s32[]{:S(2)}) async-start(), calls=%async_computation.13 | async-start | bytes 9437184 | tf_op jit(solution)/shard_map/all_gather | solution.py:159
  103.2 59.0 %collective-permute-start.13 = (bf16[128,4096]{1,0:T(8,128)(2,1)}, bf16[128,4096]{1,0:T(8,128)(2,1)}, u32[]{:S(2)}, u32[]{:S(2)}) collective-permute-start(bf16[128,4096]{1,0:T(8,128)(2,1)} %broadcast_add_fusion.3), channel_id=1, source_target_pairs={{1,0},{2,1},{3,2},{5,4},{6,5},{7,6},{9,8},{10,9},{11,10},{13,12},{... | collective-permute-start | bytes 3145736 | tf_op jit(solution)/shard_map/spread_text/ppermute | solution.py:58
  142.3 746.4 %reduce-scatter.8.cloned.1.call-start = ((), (), s32[]{:S(2)}) async-start(), calls=%async_computation.14 | async-start | bytes 9437184 | tf_op jit(solution)/shard_map/reduce_scatter | solution.py:165
  258.3 56.4 %collective-permute-start.41 = (bf16[128,2048]{1,0:T(8,128)(2,1)}, bf16[128,2048]{1,0:T(8,128)(2,1)}, u32[]{:S(2)}, u32[]{:S(2)}) collective-permute-start(bf16[128,2048]{1,0:T(8,128)(2,1)} %collective-permute-done.40), channel_id=1, source_target_pairs={{2,3},{6,7},{10,11},{14,15},{18,19},{22,23},{26,27},{30,31}} | collective-permute-start | bytes 1572872 | tf_op jit(solution)/shard_map/spread_n2_1/ppermute | solution.py:57
  267.1 49.5 %collective-permute-start.39 = (bf16[128,2048]{1,0:T(8,128)(2,1)}, bf16[128,2048]{1,0:T(8,128)(2,1)}, u32[]{:S(2)}, u32[]{:S(2)}) collective-permute-start(bf16[128,2048]{1,0:T(8,128)(2,1)} %collective-permute-done.38), channel_id=1, source_target_pairs={{1,0},{5,4},{9,8},{13,12},{17,16},{21,20},{25,24},{29,28}} | collective-permute-start | bytes 1572872 | tf_op jit(solution)/shard_map/spread_n2_1/ppermute | solution.py:58
  304.1 61.2 %collective-permute-start.42 = (bf16[256,2048]{1,0:T(8,128)(2,1)}, bf16[256,2048]{1,0:T(8,128)(2,1)}, u32[]{:S(2)}, u32[]{:S(2)}) collective-permute-start(bf16[256,2048]{1,0:T(8,128)(2,1)} %broadcast_add_fusion), channel_id=1, source_target_pairs={{0,1},{1,2},{2,3},{4,5},{5,6},{6,7},{8,9},{9,10},{10,11},{12,13},{... | collective-permute-start | bytes 3145736 | tf_op jit(solution)/shard_map/spread_og/ppermute | solution.py:57
  306.6 61.3 %collective-permute-start.43 = (bf16[256,2048]{1,0:T(8,128)(2,1)}, bf16[256,2048]{1,0:T(8,128)(2,1)}, u32[]{:S(2)}, u32[]{:S(2)}) collective-permute-start(bf16[256,2048]{1,0:T(8,128)(2,1)} %broadcast_add_fusion), channel_id=1, source_target_pairs={{1,0},{2,1},{3,2},{5,4},{6,5},{7,6},{9,8},{10,9},{11,10},{13,12},{... | collective-permute-start | bytes 3145736 | tf_op jit(solution)/shard_map/spread_og/ppermute | solution.py:58
  465.7 51.9 %collective-permute-start.59 = (bf16[256,2048]{1,0:T(8,128)(2,1)S(1)}, bf16[256,2048]{1,0:T(8,128)(2,1)S(1)}, u32[]{:S(2)}, u32[]{:S(2)}) collective-permute-start(bf16[256,2048]{1,0:T(8,128)(2,1)S(1)} %collective-permute-done.58), channel_id=1, source_target_pairs={{2,3},{6,7},{10,11},{14,15},{18,19},{22,23},{26,27},{30,31}} | collective-permute-start | bytes 3145736 | tf_op jit(solution)/shard_map/spread_og/ppermute | solution.py:57
  466.6 54.0 %collective-permute-start.57 = (bf16[256,2048]{1,0:T(8,128)(2,1)S(1)}, bf16[256,2048]{1,0:T(8,128)(2,1)S(1)}, u32[]{:S(2)}, u32[]{:S(2)}) collective-permute-start(bf16[256,2048]{1,0:T(8,128)(2,1)S(1)} %collective-permute-done.56), channel_id=1, source_target_pairs={{1,0},{5,4},{9,8},{13,12},{17,16},{21,20},{25,24},{29,28}} | collective-permute-start | bytes 3145736 | tf_op jit(solution)/shard_map/spread_og/ppermute | solution.py:58
  523.3 57.9 %collective-permute-start.65 = (bf16[128,2048]{1,0:T(8,128)(2,1)}, bf16[128,2048]{1,0:T(8,128)(2,1)}, u32[]{:S(2)}, u32[]{:S(2)}) collective-permute-start(bf16[128,2048]{1,0:T(8,128)(2,1)} %collective-permute-done.64), channel_id=1, source_target_pairs={{2,3},{6,7},{10,11},{14,15},{18,19},{22,23},{26,27},{30,31}} | collective-permute-start | bytes 1572872 | tf_op jit(solution)/shard_map/spread_n3_1/ppermute | solution.py:57
  530.2 51.1 %collective-permute-start.63 = (bf16[128,2048]{1,0:T(8,128)(2,1)}, bf16[128,2048]{1,0:T(8,128)(2,1)}, u32[]{:S(2)}, u32[]{:S(2)}) collective-permute-start(bf16[128,2048]{1,0:T(8,128)(2,1)} %collective-permute-done.62), channel_id=1, source_target_pairs={{1,0},{5,4},{9,8},{13,12},{17,16},{21,20},{25,24},{29,28}} | collective-permute-start | bytes 1572872 | tf_op jit(solution)/shard_map/spread_n3_1/ppermute | solution.py:58
  646.3 294.2 %reduce-scatter.10.cloned.1.call-start = ((), (), s32[]{:S(2)}) async-start(), calls=%async_computation.15 | async-start | bytes 9437184 | tf_op jit(solution)/shard_map/reduce_scatter | solution.py:162
  744.7 314.1 %reduce-scatter.14.cloned.1.call-start = ((), (), s32[]{:S(2)}) async-start(), calls=%async_computation.17 | async-start | bytes 2359296 | tf_op jit(solution)/shard_map/reduce_scatter | solution.py:162
  764.9 60.3 %collective-permute-start.80 = (bf16[256,2048]{1,0:T(8,128)(2,1)}, bf16[256,2048]{1,0:T(8,128)(2,1)}, u32[]{:S(2)}, u32[]{:S(2)}) collective-permute-start(bf16[256,2048]{1,0:T(8,128)(2,1)} %fusion.368), channel_id=1, source_target_pairs={{0,1},{4,5},{8,9},{12,13},{16,17},{20,21},{24,25},{28,29}} | collective-permute-start | bytes 3145736 | tf_op jit(solution)/shard_map/sink_out/ppermute | solution.py:76
  772.1 54.3 %collective-permute-start.83 = (bf16[256,2048]{1,0:T(8,128)(2,1)}, bf16[256,2048]{1,0:T(8,128)(2,1)}, u32[]{:S(2)}, u32[]{:S(2)}) collective-permute-start(bf16[256,2048]{1,0:T(8,128)(2,1)} %fusion.367), channel_id=1, source_target_pairs={{3,2},{7,6},{11,10},{15,14},{19,18},{23,22},{27,26},{31,30}} | collective-permute-start | bytes 3145736 | tf_op jit(solution)/shard_map/sink_out/ppermute | solution.py:77
  853.9 50.9 %collective-permute-start.97 = (bf16[128,2048]{1,0:T(8,128)(2,1)}, bf16[128,2048]{1,0:T(8,128)(2,1)}, u32[]{:S(2)}, u32[]{:S(2)}) collective-permute-start(bf16[128,2048]{1,0:T(8,128)(2,1)} %get-tuple-element.80), channel_id=1, source_target_pairs={{0,1},{1,2},{4,5},{5,6},{8,9},{9,10},{12,13},{13,14},{16,17},{17,1... | collective-permute-start | bytes 1572872 | tf_op jit(solution)/shard_map/sink_d2_0/ppermute | solution.py:76
  856.0 48.8 %collective-permute-start.100 = (bf16[128,2048]{1,0:T(8,128)(2,1)}, bf16[128,2048]{1,0:T(8,128)(2,1)}, u32[]{:S(2)}, u32[]{:S(2)}) collective-permute-start(bf16[128,2048]{1,0:T(8,128)(2,1)} %get-tuple-element.81), channel_id=1, source_target_pairs={{2,1},{3,2},{6,5},{7,6},{10,9},{11,10},{14,13},{15,14},{18,17},{19... | collective-permute-start | bytes 1572872 | tf_op jit(solution)/shard_map/sink_d2_0/ppermute | solution.py:77
  917.7 146.6 %reduce-scatter.12.cloned.1.call-start = ((), (), s32[]{:S(2)}) async-start(), calls=%async_computation.16 | async-start | bytes 2359296 | tf_op jit(solution)/shard_map/reduce_scatter | solution.py:165
  995.5 245.3 %reduce-scatter.18.cloned.1.call-start = ((), (), s32[]{:S(2)}) async-start(), calls=%async_computation.19 | async-start | bytes 2359296 | tf_op jit(solution)/shard_map/reduce_scatter | solution.py:165
  1039.8 260.6 %reduce-scatter.20.cloned.1.call-start = ((), (), s32[]{:S(2)}) async-start(), calls=%async_computation.20 | async-start | bytes 9437184 | tf_op jit(solution)/shard_map/reduce_scatter | solution.py:162
  1042.1 261.1 %reduce-scatter.16.cloned.1.call-start = ((), (), s32[]{:S(2)}) async-start(), calls=%async_computation.18 | async-start | bytes 7077888 | tf_op jit(solution)/shard_map/reduce_scatter | solution.py:162
  1054.9 94.1 %collective-permute-start.84 = (bf16[256,2048]{1,0:T(8,128)(2,1)}, bf16[256,2048]{1,0:T(8,128)(2,1)}, u32[]{:S(2)}, u32[]{:S(2)}) collective-permute-start(bf16[256,2048]{1,0:T(8,128)(2,1)} %get-tuple-element.141), channel_id=1, source_target_pairs={{2,1},{3,2},{6,5},{7,6},{10,9},{11,10},{14,13},{15,14},{18,17},{19... | collective-permute-start | bytes 3145736 | tf_op jit(solution)/shard_map/sink_out/ppermute | solution.py:77
  1056.5 96.7 %collective-permute-start.81 = (bf16[256,2048]{1,0:T(8,128)(2,1)}, bf16[256,2048]{1,0:T(8,128)(2,1)}, u32[]{:S(2)}, u32[]{:S(2)}) collective-permute-start(bf16[256,2048]{1,0:T(8,128)(2,1)} %get-tuple-element.140), channel_id=1, source_target_pairs={{0,1},{1,2},{4,5},{5,6},{8,9},{9,10},{12,13},{13,14},{16,17},{17,1... | collective-permute-start | bytes 3145736 | tf_op jit(solution)/shard_map/sink_out/ppermute | solution.py:76
  1151.9 58.0 %collective-permute-start.85 = (bf16[256,2048]{1,0:T(8,128)(2,1)S(1)}, bf16[256,2048]{1,0:T(8,128)(2,1)S(1)}, u32[]{:S(2)}, u32[]{:S(2)}) collective-permute-start(bf16[256,2048]{1,0:T(8,128)(2,1)S(1)} %add_convert_fusion.2), channel_id=1, source_target_pairs={{1,0},{2,1},{3,2},{5,4},{6,5},{7,6},{9,8},{10,9},{11,10},{13,12},{... | collective-permute-start | bytes 3145736 | tf_op jit(solution)/shard_map/sink_out/ppermute | solution.py:77
  1154.9 61.7 %collective-permute-start.82 = (bf16[256,2048]{1,0:T(8,128)(2,1)S(1)}, bf16[256,2048]{1,0:T(8,128)(2,1)S(1)}, u32[]{:S(2)}, u32[]{:S(2)}) collective-permute-start(bf16[256,2048]{1,0:T(8,128)(2,1)S(1)} %add_convert_fusion.3), channel_id=1, source_target_pairs={{0,1},{1,2},{2,3},{4,5},{5,6},{6,7},{8,9},{9,10},{10,11},{12,13},{... | collective-permute-start | bytes 3145736 | tf_op jit(solution)/shard_map/sink_out/ppermute | solution.py:76
  1176.7 51.7 %collective-permute-start.123 = (bf16[256,2048]{1,0:T(8,128)(2,1)S(1)}, bf16[256,2048]{1,0:T(8,128)(2,1)S(1)}, u32[]{:S(2)}, u32[]{:S(2)}) collective-permute-start(bf16[256,2048]{1,0:T(8,128)(2,1)S(1)} %get-tuple-element.74), channel_id=1, source_target_pairs={{0,1},{1,2},{4,5},{5,6},{8,9},{9,10},{12,13},{13,14},{16,17},{17,1... | collective-permute-start | bytes 3145736 | tf_op jit(solution)/shard_map/sink_d1/ppermute | solution.py:76
  (348 other events, 6723.9 us)
Sparse Core Ops, SparseCore 0:
  11.7 48.1 all-gather.7
  62.3 28.0 all-gather.9
  92.9 27.7 all-gather.13
  122.5 54.2 all-gather.11
  178.5 28.0 all-gather.15
  208.4 54.2 all-gather.17
  264.5 55.8 all-gather.19
  646.4 69.4 reduce-scatter.7
  744.8 71.8 reduce-scatter.9
  917.8 42.4 reduce-scatter.13
  995.6 48.3 reduce-scatter.11
  1047.1 41.1 reduce-scatter.17
  1091.7 71.5 reduce-scatter.19
  1166.5 61.7 reduce-scatter.15

commit v3 on v1

--- a/solution.py
+++ b/solution.py
@@ -105,6 +105,20 @@
 
 def after(value, *others):
     return lax.optimization_barrier((value, *others))[0]
+
+
+def follow(value, other):
+    return value + (other[(0,) * other.ndim].astype(F32) * 0.0).astype(value.dtype)
+
+
+def exchange_sum(value):
+    for axis in ("wide", "narrow"):
+        size = lax.axis_size(axis)
+        step = 1
+        while step < size:
+            value = value + lax.ppermute(value, axis, [(k, k ^ step) for k in range(size)])
+            step *= 2
+    return value
 
 
 def body(
@@ -135,6 +149,9 @@
     chunks = [slice(c * part, (c + 1) * part) for c in range(CHUNKS)]
     image_of = (here - jnp.arange(n)) % n
 
+    def relative(blocks):
+        return jnp.stack([lax.dynamic_index_in_dim(blocks, image_of[s], 0, False) for s in range(n)])
+
     def rows_of(*pieces):
         return lax.all_gather(
             jnp.concatenate([p.astype(BF) for p in pieces], axis=1), "wide", axis=0, tiled=True
@@ -169,13 +186,12 @@
     self_mix, self_total = attend(self_q, self_k, self_v, self_allowed, scale)
     self_mix = self_mix.reshape(n, PIX, width)
 
-    text = spread(after(captions, normed1))
-    text_count = text.shape[0] * text.shape[1]
-    text_rows = text.reshape(text_count, text.shape[2])
+    text_rows = lax.all_gather(captions, "narrow", axis=0, tiled=True)
+    text_count, text_width = text_rows.shape
     ckv = product(text_rows, full_ckv).astype(BF)
     cross_k = heads_of(ckv[None, :, :width])
     cross_v = heads_of(ckv[None, :, width:])
-    owner = caption_owner[0].reshape(n, -1)[image_of].reshape(-1)
+    owner = caption_owner[0]
     part_image = jnp.repeat(image_of, part)
     cross_allowed = (part_image[:, None] == owner[None, :])[None]
 
@@ -185,7 +201,7 @@
         xhat2, rstd2 = norm_stats(residual1)
         state.append((residual1, xhat2, rstd2))
     normed2 = [spread((s[1] * norm_gains[1] + norm_shifts[1]).astype(BF)) for s in state]
-    grad_all = spread(after(out_grad, normed2[0]))
+    grad_all = relative(lax.all_gather(out_grad, "narrow", axis=0))
 
     cross_q, cross_mix, cross_total, state3 = [], [], [], []
     for c in range(CHUNKS):
@@ -200,8 +216,10 @@
         state3.append((residual2, xhat3, rstd3))
     normed3 = [spread((s[1] * norm_gains[2] + norm_shifts[2]).astype(BF)) for s in state3]
 
-    block_out, acts, grad_hiddens, grad2, sums3 = [], [], [], [], []
+    out_parts, acts, grad_hiddens, grad2, sums3 = [], [], [], [], []
     for c, rows in enumerate(chunks):
+        if c > 0:
+            normed3[c] = follow(normed3[c], sent)
         hidden = product(normed3[c], full_up)
         grad_rows = grad_all[:, rows]
         acted, gelu_back = jax.vjp(jax.nn.gelu, hidden)
@@ -209,17 +227,19 @@
         grad_hidden = gelu_back(right_inner(grad_rows, full_down))[0].astype(BF)
         acts.append(acted)
         grad_hiddens.append(grad_hidden)
-        grad_n3 = sink(right_inner(grad_hidden, full_up).astype(BF))
+        sent = lax.optimization_barrier(right_inner(grad_hidden, full_up).astype(BF))
+        grad_n3 = sink(sent)
         residual2, xhat3, rstd3 = state3[c]
         sums3.append(norm_sums(grad_n3, xhat3))
         grad2.append(out_grad[rows].astype(F32) + norm_back(grad_n3, xhat3, rstd3, norm_gains[2]))
-        block_out.append(
-            (residual2 + sink(product(acted, full_down).astype(BF))).astype(BF)
-        )
+        out_parts.append(product(acted, full_down).astype(BF))
     cat = lambda xs: jnp.concatenate(xs, axis=1)
     acted, grad_hidden, n3 = cat(acts), cat(grad_hiddens), cat(normed3)
     grad_down = left_inner(acted, cat([grad_all[:, rows] for rows in chunks]))
     grad_up = left_inner(n3, grad_hidden)
+
+    out_sum = lax.psum_scatter(relative(cat(out_parts)), "narrow", scatter_dimension=0)
+    block_out = (jnp.concatenate([s[0] for s in state3]) + out_sum.astype(F32)).astype(BF)
 
     e2 = [spread(g.astype(BF)) for g in grad2]
     own_down = to_columns(grad_down)
@@ -244,7 +264,7 @@
     grad_ckv = jnp.concatenate(
         [grad_ck.reshape(text_count, width), grad_cv.reshape(text_count, width)], axis=1
     ).astype(BF)
-    grad_text_part = right_inner(grad_ckv, full_ckv).astype(BF).reshape(n, -1, text.shape[2])
+    grad_text_part = right_inner(grad_ckv, full_ckv).astype(BF).reshape(n, -1, text_width)
     grad_wckv = left_inner(text_rows, grad_ckv)
 
     e1 = [spread(g.astype(BF)) for g in grad1]
@@ -261,18 +281,16 @@
     grad_out = left_inner(self_mix, cat(e1))
     grad_wqkv = left_inner(normed1, grad_qkv)
     grad_n1 = sink(right_inner(after(grad_qkv, grad_wqkv), full_qkv).astype(BF))
-    grad_text = sink(after(grad_text_part, grad_mix)).astype(BF)
+    grad_text = sink(relative(after(grad_text_part, grad_mix))).astype(BF)
     grad1 = jnp.concatenate(grad1)
     grad_n1 = after(grad_n1, own_cout, own_cq, own_ckv)
     grad_tokens = (grad1 + norm_back(grad_n1, xhat1, rstd1, norm_gains[0])).astype(BF)
-    sums = lax.psum(
-        jnp.stack([norm_sums(grad_n1, xhat1), sum(sums2), sum(sums3)]), ("wide", "narrow")
-    )
+    sums = exchange_sum(jnp.stack([norm_sums(grad_n1, xhat1), sum(sums2), sum(sums3)]))
 
     own_out = to_columns(grad_out)
     own_qkv = to_rows(grad_wqkv)
     return (
-        jnp.concatenate(block_out),
+        block_out,
         grad_tokens,
         grad_text,
         sums[:, 0],

time: 1270 us -> 1390 us (1.094)
  waiting for transfers between devices: 343 us -> 580 us
  starting transfers between devices: 400 us -> 322 us
  blocking collectives: 46.3 us -> 0 us
    ppermute x36 -> x30, waiting for transfers between devices: 88.1 us -> 320 us  [sink(): lax.ppermute(one.astype(BF), 'narrow', [(k, k + 1) for k in range(step)])]
    ppermute x36 -> x30, starting transfers between devices: 207 us -> 142 us  [sink(): lax.ppermute(one.astype(BF), 'narrow', [(k, k + 1) for k in range(step)])]
    psum x1 -> x0, blocking collectives: 46.3 us -> none  [body(): lax.psum(jnp.stack([norm_sums(grad_n1, xhat1), sum(sums2), sum(sums3)]),...]
    ppermute x36 -> x30, waiting for transfers between devices: 41.4 us -> 0.08 us  [sink(): lax.ppermute(other.astype(BF), 'narrow', [(k, k - 1) for k in range(n - s...]
    all_gather x3, waiting for transfers between devices: 0.04 us -> 32.8 us  [columns_of(): return lax.all_gather(piece.astype(BF), 'wide', axis=1, tiled=True)]
    ppermute x0 -> x5, waiting for transfers between devices: none -> 26.5 us  [exchange_sum(): lax.ppermute(value, axis, [(k, k ^ step) for k in range(size)])]
    ppermute x0 -> x5, starting transfers between devices: none -> 25.3 us  [exchange_sum(): lax.ppermute(value, axis, [(k, k ^ step) for k in range(size)])]
    ppermute x33 -> x27, starting transfers between devices: 111 us -> 86.5 us  [spread(): lax.ppermute(up[-1], 'narrow', [(k, k + 1) for k in range(step - 1, n - 1)])]
  transfers between devices with their start and end apart: 152 -> 136, of which waited for: 43 -> 52; matrix products, arithmetic and copies ran while one was open for 31% -> 29% of each run, Pallas kernels for 0% -> 0%
where the time goes in v3:
time: 1390 us; the launch traced here: 1380 us
  waiting for transfers between devices  580 us (42%)
  starting transfers between devices  322 us (23%)
  matrix products  290 us (21%)
  other arithmetic  112 us (8%)
  local copies, waits for them, and re-layouts  48 us (3%)
  between operations  25.5 us (2%)
    ppermute x30, waiting for transfers between devices, sink(): lax.ppermute(one.astype(BF), 'narrow', [(k, k + 1) for k in range(step)])  320 us
    ppermute x27, waiting for transfers between devices, spread(): lax.ppermute(down[-1], 'narrow', [(k, k - 1) for k in range(1, n - step +...  176 us
    ppermute x30, starting transfers between devices, sink(): lax.ppermute(one.astype(BF), 'narrow', [(k, k + 1) for k in range(step)])  142 us
    ppermute x27, starting transfers between devices, spread(): lax.ppermute(up[-1], 'narrow', [(k, k + 1) for k in range(step - 1, n - 1)])  86.5 us
    dot_general x12, matrix products, product(): lax.dot_general(left_side, right_side, (((left_side.ndim - 1,), (0,)), ((...  75.1 us
    dot_general x12, matrix products, right_inner(): lax.dot_general(left_side, right_side, (((left_side.ndim - 1,), (1,)), ((...  69.7 us
    dot_general x7, matrix products, left_inner(): lax.dot_general(left_side, right_side, ((rows, rows), ((), ())), preferre...  57.3 us
    ppermute x27, starting transfers between devices, spread(): lax.ppermute(down[-1], 'narrow', [(k, k - 1) for k in range(1, n - step +...  35.4 us
  transfers between devices with their start and end apart: 136, of which 52 were waited for; matrix products, arithmetic and copies ran while one was open for 29% of the time, Pallas kernels for 0%

profile of v3, /device:TPU:0, one launch (start us, length us, event | category | flops | bytes accessed | tf_op | source)
XLA Modules:
  0.0 1377.7 jit_solution(2369147938922174307)
XLA Ops:
  28.0 21.0 %collective-permute-done = bf16[256,2048]{1,0:T(8,128)(2,1)S(1)} collective-permute-done((bf16[256,2048]{1,0:T(8,128)(2,1)S(1)}, bf16[256,2048]{1,0:T(8,128)(2,1)S(1)}, u32[]{:S(2)}, u32[]{:S(2)}) %collective-permute-start) | collective-permute-done | bytes 1048608 | tf_op jit(solution)/shard_map/ppermute | solution.py:44
  57.5 22.6 %collective-permute-done.2 = bf16[256,2048]{1,0:T(8,128)(2,1)} collective-permute-done((bf16[256,2048]{1,0:T(8,128)(2,1)S(1)}, bf16[256,2048]{1,0:T(8,128)(2,1)}, u32[]{:S(2)}, u32[]{:S(2)}) %collective-permute-start.2) | collective-permute-done | bytes 1048608 | tf_op jit(solution)/shard_map/ppermute | solution.py:45
  86.0 19.6 %collective-permute-done.3 = bf16[256,2048]{1,0:T(8,128)(2,1)S(1)} collective-permute-done((bf16[256,2048]{1,0:T(8,128)(2,1)}, bf16[256,2048]{1,0:T(8,128)(2,1)S(1)}, u32[]{:S(2)}, u32[]{:S(2)}) %collective-permute-start.3) | collective-permute-done | bytes 1048608 | tf_op jit(solution)/shard_map/ppermute | solution.py:45
  133.5 18.8 %collective-permute-done.6 = bf16[128,2048]{1,0:T(8,128)(2,1)S(1)} collective-permute-done((bf16[128,2048]{1,0:T(8,128)(2,1)S(1)}, bf16[128,2048]{1,0:T(8,128)(2,1)S(1)}, u32[]{:S(2)}, u32[]{:S(2)}) %collective-permute-start.6) | collective-permute-done | bytes 524320 | tf_op jit(solution)/shard_map/ppermute | solution.py:58
  157.7 17.1 %collective-permute-done.24 = bf16[128,2048]{1,0:T(8,128)(2,1)S(1)} collective-permute-done((bf16[128,2048]{1,0:T(8,128)(2,1)S(1)}, bf16[128,2048]{1,0:T(8,128)(2,1)S(1)}, u32[]{:S(2)}, u32[]{:S(2)}) %collective-permute-start.24) | collective-permute-done | bytes 524320 | tf_op jit(solution)/shard_map/ppermute | solution.py:58
  180.2 17.0 %collective-permute-done.7 = bf16[128,2048]{1,0:T(8,128)(2,1)S(1)} collective-permute-done((bf16[128,2048]{1,0:T(8,128)(2,1)S(1)}, bf16[128,2048]{1,0:T(8,128)(2,1)S(1)}, u32[]{:S(2)}, u32[]{:S(2)}) %collective-permute-start.7) | collective-permute-done | bytes 524320 | tf_op jit(solution)/shard_map/ppermute | solution.py:58
  203.4 16.4 %collective-permute-done.25 = bf16[128,2048]{1,0:T(8,128)(2,1)S(1)} collective-permute-done((bf16[128,2048]{1,0:T(8,128)(2,1)S(1)}, bf16[128,2048]{1,0:T(8,128)(2,1)S(1)}, u32[]{:S(2)}, u32[]{:S(2)}) %collective-permute-start.25) | collective-permute-done | bytes 524320 | tf_op jit(solution)/shard_map/ppermute | solution.py:58
  226.3 16.0 %collective-permute-done.8 = bf16[128,2048]{1,0:T(8,128)(2,1)S(1)} collective-permute-done((bf16[128,2048]{1,0:T(8,128)(2,1)S(1)}, bf16[128,2048]{1,0:T(8,128)(2,1)S(1)}, u32[]{:S(2)}, u32[]{:S(2)}) %collective-permute-start.8) | collective-permute-done | bytes 524320 | tf_op jit(solution)/shard_map/ppermute | solution.py:58
  242.2 19.3 %collective-permute-done.26 = bf16[128,2048]{1,0:T(8,128)(2,1)S(1)} collective-permute-done((bf16[128,2048]{1,0:T(8,128)(2,1)S(1)}, bf16[128,2048]{1,0:T(8,128)(2,1)S(1)}, u32[]{:S(2)}, u32[]{:S(2)}) %collective-permute-start.26) | collective-permute-done | bytes 524320 | tf_op jit(solution)/shard_map/ppermute | solution.py:58
  373.6 19.3 %collective-permute-done.18 = bf16[128,2048]{1,0:T(8,128)(2,1)S(1)} collective-permute-done((bf16[128,2048]{1,0:T(8,128)(2,1)S(1)}, bf16[128,2048]{1,0:T(8,128)(2,1)S(1)}, u32[]{:S(2)}, u32[]{:S(2)}) %collective-permute-start.18) | collective-permute-done | bytes 524320 | tf_op jit(solution)/shard_map/ppermute | solution.py:58
  398.4 17.0 %collective-permute-done.36 = bf16[128,2048]{1,0:T(8,128)(2,1)S(1)} collective-permute-done((bf16[128,2048]{1,0:T(8,128)(2,1)S(1)}, bf16[128,2048]{1,0:T(8,128)(2,1)S(1)}, u32[]{:S(2)}, u32[]{:S(2)}) %collective-permute-start.36) | collective-permute-done | bytes 524320 | tf_op jit(solution)/shard_map/ppermute | solution.py:58
  420.8 17.0 %collective-permute-done.19 = bf16[128,2048]{1,0:T(8,128)(2,1)S(1)} collective-permute-done((bf16[128,2048]{1,0:T(8,128)(2,1)S(1)}, bf16[128,2048]{1,0:T(8,128)(2,1)S(1)}, u32[]{:S(2)}, u32[]{:S(2)}) %collective-permute-start.19) | collective-permute-done | bytes 524320 | tf_op jit(solution)/shard_map/ppermute | solution.py:58
  444.0 16.4 %collective-permute-done.37 = bf16[128,2048]{1,0:T(8,128)(2,1)S(1)} collective-permute-done((bf16[128,2048]{1,0:T(8,128)(2,1)S(1)}, bf16[128,2048]{1,0:T(8,128)(2,1)S(1)}, u32[]{:S(2)}, u32[]{:S(2)}) %collective-permute-start.37) | collective-permute-done | bytes 524320 | tf_op jit(solution)/shard_map/ppermute | solution.py:58
  466.4 15.7 %collective-permute-done.20 = bf16[128,2048]{1,0:T(8,128)(2,1)S(1)} collective-permute-done((bf16[128,2048]{1,0:T(8,128)(2,1)S(1)}, bf16[128,2048]{1,0:T(8,128)(2,1)S(1)}, u32[]{:S(2)}, u32[]{:S(2)}) %collective-permute-start.20) | collective-permute-done | bytes 524320 | tf_op jit(solution)/shard_map/ppermute | solution.py:58
  482.8 14.0 %collective-permute-done.38 = bf16[128,2048]{1,0:T(8,128)(2,1)S(1)} collective-permute-done((bf16[128,2048]{1,0:T(8,128)(2,1)S(1)}, bf16[128,2048]{1,0:T(8,128)(2,1)S(1)}, u32[]{:S(2)}, u32[]{:S(2)}) %collective-permute-start.38) | collective-permute-done | bytes 524320 | tf_op jit(solution)/shard_map/ppermute | solution.py:58
  563.8 11.9 multiply_convert_fusion.4
  575.8 32.7 %all-gather.25.cloned.1.call-done = bf16[2048,2048]{1,0:T(8,128)(2,1)} async-done(((bf16[2048,256]{1,0:T(8,128)(2,1)}), bf16[2048,2048]{1,0:T(8,128)(2,1)}) %all-gather.25.cloned.1.call-update) | async-done | bytes 8388624 | tf_op jit(solution)/shard_map/all_gather | solution.py:161
  646.2 13.5 convolution_bitcast_fusion.2
  659.7 14.4 %convolution_bitcast_fusion.3 = bf16[2048,2048]{1,0:T(8,128)(2,1)} fusion(bf16[4,128,2048]{2,1,0:T(8,128)(2,1)} %get-tuple-element.189, bf16[4,128,2048]{2,1,0:T(8,128)(2,1)} %get-tuple-element.187, bf16[1,256,2048]{2,1,0:T(8,128)(2,1)} %copy-done.45, bf16[1,256,2048]{2,1,0:T(8,128)(2,1)} %copy-done.46, bf16[1,256,2048]{2,1,0:T(8,128)(2,1)} %copy-done.47, ...), kind=kOutput, calls=%fused_computation.7 | convolution fusion | flops 8604614656 | bytes 16777216 | tf_op jit(solution)/shard_map/dot_general | solution.py:36
  736.0 10.8 collective-permute-done.74
  804.9 18.6 %collective-permute-done.81 = bf16[128,2048]{1,0:T(8,128)(2,1)S(1)} collective-permute-done((bf16[128,2048]{1,0:T(8,128)(2,1)S(1)}, bf16[128,2048]{1,0:T(8,128)(2,1)S(1)}, u32[]{:S(2)}, u32[]{:S(2)}) %collective-permute-start.81) | collective-permute-done | bytes 524320 | tf_op jit(solution)/shard_map/ppermute | solution.py:45
  947.9 19.9 %collective-permute-start.68 = (bf16[128,2048]{1,0:T(8,128)(2,1)}, bf16[128,2048]{1,0:T(8,128)(2,1)}, u32[]{:S(2)}, u32[]{:S(2)}) collective-permute-start(bf16[128,2048]{1,0:T(8,128)(2,1)} %get-tuple-element.99), channel_id=1, source_target_pairs={{0,1},{1,2},{2,3},{4,5},{5,6},{6,7},{8,9},{9,10},{10,11},{12,13},{... | collective-permute-start | bytes 1572872 | tf_op jit(solution)/shard_map/ppermute | solution.py:58
  981.3 11.5 collective-permute-start.86
  996.2 16.9 %collective-permute-done.86 = bf16[128,2048]{1,0:T(8,128)(2,1)S(1)} collective-permute-done((bf16[128,2048]{1,0:T(8,128)(2,1)S(1)}, bf16[128,2048]{1,0:T(8,128)(2,1)S(1)}, u32[]{:S(2)}, u32[]{:S(2)}) %collective-permute-start.86) | collective-permute-done | bytes 524320 | tf_op jit(solution)/shard_map/ppermute | solution.py:58
  1019.9 25.2 %collective-permute-start.96 = (bf16[128,2048]{1,0:T(8,128)(2,1)S(1)}, bf16[128,2048]{1,0:T(8,128)(2,1)S(1)}, u32[]{:S(2)}, u32[]{:S(2)}) collective-permute-start(bf16[128,2048]{1,0:T(8,128)(2,1)S(1)} %get-tuple-element.68), channel_id=1, source_target_pairs={{0,1},{1,2},{2,3},{4,5},{5,6},{6,7},{8,9},{9,10},{10,11},{12,13},{... | collective-permute-start | bytes 1572872 | tf_op jit(solution)/shard_map/ppermute | solution.py:44
  1088.5 11.1 collective-permute-done.99
  1170.6 10.6 fusion.94
  1189.1 17.9 %collective-permute-done.102 = bf16[256,2048]{1,0:T(8,128)(2,1)S(1)} collective-permute-done((bf16[256,2048]{1,0:T(8,128)(2,1)S(1)}, bf16[256,2048]{1,0:T(8,128)(2,1)S(1)}, u32[]{:S(2)}, u32[]{:S(2)}) %collective-permute-start.102) | collective-permute-done | bytes 1048608 | tf_op jit(solution)/shard_map/ppermute | solution.py:58
  1237.7 14.3 %collective-permute-done.103 = bf16[256,2048]{1,0:T(8,128)(2,1)} collective-permute-done((bf16[256,2048]{1,0:T(8,128)(2,1)}, bf16[256,2048]{1,0:T(8,128)(2,1)}, u32[]{:S(2)}, u32[]{:S(2)}) %collective-permute-start.103) | collective-permute-done | bytes 1048608 | tf_op jit(solution)/shard_map/ppermute | solution.py:58
  1284.8 12.2 collective-permute-done.104
  1321.9 19.2 %collective-permute-start.118 = (f32[3,2,2048]{2,0,1:T(4,128)S(1)}, f32[3,2,2048]{2,0,1:T(4,128)S(1)}, u32[]{:S(2)}, u32[]{:S(2)}) collective-permute-start(f32[3,2,2048]{2,0,1:T(4,128)S(1)} %add.569), channel_id=1, source_target_pairs={{0,2},{1,3},{2,0},{3,1},{4,6},{5,7},{6,4},{7,5},{8,10},{9,11},{10,... | collective-permute-start | bytes 147464 | tf_op jit(solution)/shard_map/ppermute | solution.py:119
  1344.0 20.7 %collective-permute-done.118 = f32[3,2,2048]{2,0,1:T(4,128)S(1)} collective-permute-done((f32[3,2,2048]{2,0,1:T(4,128)S(1)}, f32[3,2,2048]{2,0,1:T(4,128)S(1)}, u32[]{:S(2)}, u32[]{:S(2)}) %collective-permute-start.118) | collective-permute-done | bytes 49184 | tf_op jit(solution)/shard_map/ppermute | solution.py:119
  (774 shorter events, 803.3 us)
Async XLA Ops:
  7.2 99.4 %all-gather.11.cloned.1.call-start = ((), (), s32[]{:S(2)}) async-start(), calls=%async_computation.8 | async-start | bytes 7077888 | tf_op jit(solution)/shard_map/all_gather | solution.py:156
  11.6 112.8 %all-gather.13.cloned.1.call-start = ((), (), s32[]{:S(2)}) async-start(), calls=%async_computation.9 | async-start | bytes 2359296 | tf_op jit(solution)/shard_map/all_gather | solution.py:161
  12.4 310.2 %all-gather.19.cloned.1.call-start = ((), (), s32[]{:S(2)}) async-start(), calls=%async_computation.12 | async-start | bytes 2359296 | tf_op jit(solution)/shard_map/all_gather | solution.py:156
  13.2 325.2 %all-gather.17.cloned.1.call-start = ((), (), s32[]{:S(2)}) async-start(), calls=%async_computation.11 | async-start | bytes 5242880 | tf_op jit(solution)/shard_map/all_gather | solution.py:189
  13.8 324.6 %all-gather.15.cloned.1.call-start = ((), (), s32[]{:S(2)}) async-start(), calls=%async_computation.10 | async-start | bytes 9437184 | tf_op jit(solution)/shard_map/all_gather | solution.py:156
  16.5 346.2 %all-gather.21.cloned.1.call-start = ((), (), s32[]{:S(2)}) async-start(), calls=%async_computation.13 | async-start | bytes 2359296 | tf_op jit(solution)/shard_map/all_gather | solution.py:161
  18.4 507.7 %all-gather.27.cloned.1.call-start = ((), (), s32[]{:S(2)}) async-start(), calls=%async_computation.24 | async-start | bytes 5242880 | tf_op jit(solution)/shard_map/all_gather | solution.py:204
  19.2 544.7 %all-gather.23.cloned.1.call-start = ((), (), s32[]{:S(2)}) async-start(), calls=%async_computation.14 | async-start | bytes 9437184 | tf_op jit(solution)/shard_map/all_gather | solution.py:156
  20.4 588.1 %all-gather.25.cloned.1.call-start = ((), (), s32[]{:S(2)}) async-start(), calls=%async_computation.15 | async-start | bytes 9437184 | tf_op jit(solution)/shard_map/all_gather | solution.py:161
  131.5 43.3 %collective-permute-start.24 = (bf16[128,2048]{1,0:T(8,128)(2,1)S(1)}, bf16[128,2048]{1,0:T(8,128)(2,1)S(1)}, u32[]{:S(2)}, u32[]{:S(2)}) collective-permute-start(bf16[128,2048]{1,0:T(8,128)(2,1)S(1)} %get-tuple-element.147), channel_id=1, source_target_pairs={{0,1},{4,5},{8,9},{12,13},{16,17},{20,21},{24,25},{28,29}} | collective-permute-start | bytes 1572872 | tf_op jit(solution)/shard_map/ppermute | solution.py:58
  152.6 44.7 %collective-permute-start.7 = (bf16[128,2048]{1,0:T(8,128)(2,1)S(1)}, bf16[128,2048]{1,0:T(8,128)(2,1)S(1)}, u32[]{:S(2)}, u32[]{:S(2)}) collective-permute-start(bf16[128,2048]{1,0:T(8,128)(2,1)S(1)} %get-tuple-element.139), channel_id=1, source_target_pairs={{0,1},{1,2},{4,5},{5,6},{8,9},{9,10},{12,13},{13,14},{16,17},{17,1... | collective-permute-start | bytes 1572872 | tf_op jit(solution)/shard_map/ppermute | solution.py:58
  175.1 44.6 %collective-permute-start.25 = (bf16[128,2048]{1,0:T(8,128)(2,1)S(1)}, bf16[128,2048]{1,0:T(8,128)(2,1)S(1)}, u32[]{:S(2)}, u32[]{:S(2)}) collective-permute-start(bf16[128,2048]{1,0:T(8,128)(2,1)S(1)} %get-tuple-element.145), channel_id=1, source_target_pairs={{0,1},{1,2},{4,5},{5,6},{8,9},{9,10},{12,13},{13,14},{16,17},{17,1... | collective-permute-start | bytes 1572872 | tf_op jit(solution)/shard_map/ppermute | solution.py:58
  197.7 44.5 %collective-permute-start.8 = (bf16[128,2048]{1,0:T(8,128)(2,1)S(1)}, bf16[128,2048]{1,0:T(8,128)(2,1)S(1)}, u32[]{:S(2)}, u32[]{:S(2)}) collective-permute-start(bf16[128,2048]{1,0:T(8,128)(2,1)S(1)} %get-tuple-element.137), channel_id=1, source_target_pairs={{0,1},{1,2},{2,3},{4,5},{5,6},{6,7},{8,9},{9,10},{10,11},{12,13},{... | collective-permute-start | bytes 1572872 | tf_op jit(solution)/shard_map/ppermute | solution.py:58
  279.0 839.9 %reduce-scatter.13.cloned.1.call-start = ((), (), s32[]{:S(2)}) async-start(), calls=%async_computation.18 | async-start | bytes 9437184 | tf_op jit(solution)/shard_map/reduce_scatter | solution.py:164
  371.6 43.8 %collective-permute-start.36 = (bf16[128,2048]{1,0:T(8,128)(2,1)S(1)}, bf16[128,2048]{1,0:T(8,128)(2,1)S(1)}, u32[]{:S(2)}, u32[]{:S(2)}) collective-permute-start(bf16[128,2048]{1,0:T(8,128)(2,1)S(1)} %get-tuple-element.133), channel_id=1, source_target_pairs={{0,1},{4,5},{8,9},{12,13},{16,17},{20,21},{24,25},{28,29}} | collective-permute-start | bytes 1572872 | tf_op jit(solution)/shard_map/ppermute | solution.py:58
  393.2 44.6 %collective-permute-start.19 = (bf16[128,2048]{1,0:T(8,128)(2,1)S(1)}, bf16[128,2048]{1,0:T(8,128)(2,1)S(1)}, u32[]{:S(2)}, u32[]{:S(2)}) collective-permute-start(bf16[128,2048]{1,0:T(8,128)(2,1)S(1)} %get-tuple-element.125), channel_id=1, source_target_pairs={{0,1},{1,2},{4,5},{5,6},{8,9},{9,10},{12,13},{13,14},{16,17},{17,1... | collective-permute-start | bytes 1572872 | tf_op jit(solution)/shard_map/ppermute | solution.py:58
  415.7 44.6 %collective-permute-start.37 = (bf16[128,2048]{1,0:T(8,128)(2,1)S(1)}, bf16[128,2048]{1,0:T(8,128)(2,1)S(1)}, u32[]{:S(2)}, u32[]{:S(2)}) collective-permute-start(bf16[128,2048]{1,0:T(8,128)(2,1)S(1)} %get-tuple-element.131), channel_id=1, source_target_pairs={{0,1},{1,2},{4,5},{5,6},{8,9},{9,10},{12,13},{13,14},{16,17},{17,1... | collective-permute-start | bytes 1572872 | tf_op jit(solution)/shard_map/ppermute | solution.py:58
  438.2 43.9 %collective-permute-start.20 = (bf16[128,2048]{1,0:T(8,128)(2,1)S(1)}, bf16[128,2048]{1,0:T(8,128)(2,1)S(1)}, u32[]{:S(2)}, u32[]{:S(2)}) collective-permute-start(bf16[128,2048]{1,0:T(8,128)(2,1)S(1)} %get-tuple-element.123), channel_id=1, source_target_pairs={{0,1},{1,2},{2,3},{4,5},{5,6},{6,7},{8,9},{9,10},{10,11},{12,13},{... | collective-permute-start | bytes 1572872 | tf_op jit(solution)/shard_map/ppermute | solution.py:58
  538.9 86.2 %collective-permute-start.51 = (bf16[128,2048]{1,0:T(8,128)(2,1)}, bf16[128,2048]{1,0:T(8,128)(2,1)}, u32[]{:S(2)}, u32[]{:S(2)}) collective-permute-start(bf16[128,2048]{1,0:T(8,128)(2,1)} %collective-permute-done.50), channel_id=1, source_target_pairs={{1,0},{5,4},{9,8},{13,12},{17,16},{21,20},{25,24},{29,28}} | collective-permute-start | bytes 1572872 | tf_op jit(solution)/shard_map/ppermute | solution.py:45
  552.9 73.3 %collective-permute-start.53 = (bf16[128,2048]{1,0:T(8,128)(2,1)}, bf16[128,2048]{1,0:T(8,128)(2,1)}, u32[]{:S(2)}, u32[]{:S(2)}) collective-permute-start(bf16[128,2048]{1,0:T(8,128)(2,1)} %collective-permute-done.52), channel_id=1, source_target_pairs={{2,3},{6,7},{10,11},{14,15},{18,19},{22,23},{26,27},{30,31}} | collective-permute-start | bytes 1572872 | tf_op jit(solution)/shard_map/ppermute | solution.py:44
  659.7 462.1 %reduce-scatter.11.cloned.1.call-start = ((), (), s32[]{:S(2)}) async-start(), calls=%async_computation.17 | async-start | bytes 9437184 | tf_op jit(solution)/shard_map/reduce_scatter | solution.py:167
  674.2 541.5 %reduce-scatter.15.cloned.1.call-start = ((), (), s32[]{:S(2)}) async-start(), calls=%async_computation.19 | async-start | bytes 2359296 | tf_op jit(solution)/shard_map/reduce_scatter | solution.py:167
  829.3 388.2 %reduce-scatter.17.cloned.1.call-start = ((), (), s32[]{:S(2)}) async-start(), calls=%async_computation.20 | async-start | bytes 2359296 | tf_op jit(solution)/shard_map/reduce_scatter | solution.py:164
  872.6 389.6 %reduce-scatter.9.cloned.1.call-start = ((), (), s32[]{:S(2)}) async-start(), calls=%async_computation.16 | async-start | bytes 5242880 | tf_op jit(solution)/shard_map/reduce_scatter | solution.py:241
  893.2 371.6 %reduce-scatter.23.cloned.1.call-start = ((), (), s32[]{:S(2)}) async-start(), calls=%async_computation.23 | async-start | bytes 2359296 | tf_op jit(solution)/shard_map/reduce_scatter | solution.py:167
  932.9 46.7 %collective-permute-start.85 = (bf16[128,2048]{1,0:T(8,128)(2,1)}, bf16[128,2048]{1,0:T(8,128)(2,1)}, u32[]{:S(2)}, u32[]{:S(2)}) collective-permute-start(bf16[128,2048]{1,0:T(8,128)(2,1)} %get-tuple-element.113), channel_id=1, source_target_pairs={{0,1},{1,2},{4,5},{5,6},{8,9},{9,10},{12,13},{13,14},{16,17},{17,1... | collective-permute-start | bytes 1572872 | tf_op jit(solution)/shard_map/ppermute | solution.py:58
  947.9 46.2 %collective-permute-start.68 = (bf16[128,2048]{1,0:T(8,128)(2,1)}, bf16[128,2048]{1,0:T(8,128)(2,1)}, u32[]{:S(2)}, u32[]{:S(2)}) collective-permute-start(bf16[128,2048]{1,0:T(8,128)(2,1)} %get-tuple-element.99), channel_id=1, source_target_pairs={{0,1},{1,2},{2,3},{4,5},{5,6},{6,7},{8,9},{9,10},{10,11},{12,13},{... | collective-permute-start | bytes 1572872 | tf_op jit(solution)/shard_map/ppermute | solution.py:58
  1111.2 189.2 %reduce-scatter.19.cloned.1.call-start = ((), (), s32[]{:S(2)}) async-start(), calls=%async_computation.21 | async-start | bytes 9437184 | tf_op jit(solution)/shard_map/reduce_scatter | solution.py:164
  1111.7 256.9 %reduce-scatter.21.cloned.1.call-start = ((), (), s32[]{:S(2)}) async-start(), calls=%async_computation.22 | async-start | bytes 7077888 | tf_op jit(solution)/shard_map/reduce_scatter | solution.py:164
  1208.6 43.4 %collective-permute-start.103 = (bf16[256,2048]{1,0:T(8,128)(2,1)}, bf16[256,2048]{1,0:T(8,128)(2,1)}, u32[]{:S(2)}, u32[]{:S(2)}) collective-permute-start(bf16[256,2048]{1,0:T(8,128)(2,1)} %get-tuple-element.84), channel_id=1, source_target_pairs={{0,1},{1,2},{4,5},{5,6},{8,9},{9,10},{12,13},{13,14},{16,17},{17,1... | collective-permute-start | bytes 3145736 | tf_op jit(solution)/shard_map/ppermute | solution.py:58
  1277.7 87.7 %collective-permute-start.110 = (bf16[128,4096]{1,0:T(8,128)(2,1)}, bf16[128,4096]{1,0:T(8,128)(2,1)}, u32[]{:S(2)}, u32[]{:S(2)}) collective-permute-start(bf16[128,4096]{1,0:T(8,128)(2,1)} %get-tuple-element.64), channel_id=1, source_target_pairs={{0,1},{1,2},{2,3},{4,5},{5,6},{6,7},{8,9},{9,10},{10,11},{12,13},{... | collective-permute-start | bytes 3145736 | tf_op jit(solution)/shard_map/ppermute | solution.py:58
  1318.8 46.6 %collective-permute-start.113 = (bf16[128,4096]{1,0:T(8,128)(2,1)}, bf16[128,4096]{1,0:T(8,128)(2,1)}, u32[]{:S(2)}, u32[]{:S(2)}) collective-permute-start(bf16[128,4096]{1,0:T(8,128)(2,1)} %add_convert_fusion), channel_id=1, source_target_pairs={{1,0},{2,1},{3,2},{5,4},{6,5},{7,6},{9,8},{10,9},{11,10},{13,12},{... | collective-permute-start | bytes 3145736 | tf_op jit(solution)/shard_map/ppermute | solution.py:59
  (244 other events, 5870.9 us)
Sparse Core Ops, SparseCore 0:
  11.7 48.1 all-gather.10
  62.3 28.0 all-gather.12
  92.9 27.7 all-gather.18
  122.2 140.3 all-gather.16
  264.8 56.8 all-gather.14
  323.5 28.0 all-gather.20
  353.2 138.1 all-gather.26
  493.9 56.2 all-gather.22
  552.6 55.8 all-gather.24
  659.8 71.4 reduce-scatter.12
  734.8 71.2 reduce-scatter.10
  829.4 46.4 reduce-scatter.14
  879.1 41.1 reduce-scatter.16
  922.4 120.6 reduce-scatter.8
  1111.3 42.6 reduce-scatter.22
  1157.3 71.2 reduce-scatter.18
  1231.8 61.7 reduce-scatter.20

commit v4 on v1

--- a/solution.py
+++ b/solution.py
@@ -36,28 +36,51 @@
     return lax.dot_general(left_side, right_side, ((rows, rows), ((), ())), preferred_element_type=F32)
 
 
-def spread(rows):
+def follow(value, *others):
+    if not others:
+        return value
+    nothing = sum(o[(0,) * o.ndim].astype(F32) for o in others) * 0.0
+    return value + nothing.astype(value.dtype)
+
+
+def whole(value):
+    return lax.optimization_barrier(value)
+
+
+def after(value, *others):
+    return lax.optimization_barrier((value, *others))[0]
+
+
+def spread(name, rows, gates={}):
     n = lax.axis_size("narrow")
     here = lax.axis_index("narrow")
-    up, down = [rows], [rows]
-    for step in range(1, n):
-        up.append(lax.ppermute(up[-1], "narrow", [(k, k + 1) for k in range(step - 1, n - 1)]))
-        down.append(lax.ppermute(down[-1], "narrow", [(k, k - 1) for k in range(1, n - step + 1)]))
-    parts = [rows] + [jnp.where(here >= s, up[s], down[n - s]) for s in range(1, n)]
-    return jnp.stack(parts)
-
-
-def sink(parts):
+    with jax.named_scope("spread_" + name):
+        up, down = [rows], [rows]
+        for step in range(1, n):
+            one, other = follow(up[-1], *gates.get(step, ())), follow(down[-1], *gates.get(step, ()))
+            up.append(lax.ppermute(one, "narrow", [(k, k + 1) for k in range(step - 1, n - 1)]))
+            down.append(lax.ppermute(other, "narrow", [(k, k - 1) for k in range(1, n - step + 1)]))
+        parts = [rows] + [jnp.where(here >= s, up[s], down[n - s]) for s in range(1, n)]
+        return jnp.stack(parts), [(up[s], down[s]) for s in range(1, n)]
+
+
+def sink(name, parts, gates={}):
     n = lax.axis_size("narrow")
-    up = down = None
-    for step in range(1, n):
-        one, other = parts[step], parts[n - step]
-        if up is not None:
-            one = up.astype(F32) + one.astype(F32)
-            other = down.astype(F32) + other.astype(F32)
-        up = lax.ppermute(one.astype(BF), "narrow", [(k, k + 1) for k in range(step)])
-        down = lax.ppermute(other.astype(BF), "narrow", [(k, k - 1) for k in range(n - step, n)])
-    return up.astype(F32) + down.astype(F32) + parts[0].astype(F32)
+    hops = []
+    with jax.named_scope("sink_" + name):
+        for step in range(1, n):
+            one, other = parts[step], parts[n - step]
+            gate = gates.get(step, ())
+            if callable(gate):
+                gate = gate(hops[0])
+            if hops:
+                one = hops[-1][0].astype(F32) + one.astype(F32)
+                other = hops[-1][1].astype(F32) + other.astype(F32)
+            one, other = follow(one, *gate), follow(other, *gate)
+            up = lax.ppermute(one.astype(BF), "narrow", [(k, k + 1) for k in range(step)])
+            down = lax.ppermute(other.astype(BF), "narrow", [(k, k - 1) for k in range(n - step, n)])
+            hops.append((up, down))
+        return up.astype(F32) + down.astype(F32) + parts[0].astype(F32), hops
 
 
 def norm_stats(features):
@@ -101,10 +124,6 @@
     grad_queries = jnp.einsum("ihpq,iqhe->iphe", grad_scores, keys_in, preferred_element_type=F32)
     grad_keys = jnp.einsum("ihpq,iphe->iqhe", grad_scores, queries, preferred_element_type=F32)
     return grad_queries.astype(BF), grad_keys, grad_values
-
-
-def after(value, *others):
-    return lax.optimization_barrier((value, *others))[0]
 
 
 def body(
@@ -160,7 +179,7 @@
     residual0 = tokens.astype(F32)
     xhat1, rstd1 = norm_stats(residual0)
     own1 = (xhat1 * norm_gains[0] + norm_shifts[0]).astype(BF)
-    normed1 = spread(own1)
+    normed1 = spread("n1", own1)[0]
     qkv = product(normed1, full_qkv).astype(BF)
     heads_of = lambda x: x.reshape(x.shape[:-1] + (x.shape[-1] // HEAD_DIM, HEAD_DIM))
     self_q, self_k, self_v = [heads_of(qkv[..., k * width : (k + 1) * width]) for k in range(3)]
@@ -169,7 +188,7 @@
     self_mix, self_total = attend(self_q, self_k, self_v, self_allowed, scale)
     self_mix = self_mix.reshape(n, PIX, width)
 
-    text = spread(after(captions, normed1))
+    text = spread("text", follow(captions, normed1[1], normed1[n - 1]), {2: (self_mix,)})[0]
     text_count = text.shape[0] * text.shape[1]
     text_rows = text.reshape(text_count, text.shape[2])
     ckv = product(text_rows, full_ckv).astype(BF)
@@ -180,27 +199,34 @@
     cross_allowed = (part_image[:, None] == owner[None, :])[None]
 
     state = []
-    for rows in chunks:
-        residual1 = residual0[rows] + sink(product(self_mix[:, rows], full_out).astype(BF))
+    for c, rows in enumerate(chunks):
+        residual1 = residual0[rows] + sink(f"r1_{c}", product(self_mix[:, rows], full_out).astype(BF))[0]
         xhat2, rstd2 = norm_stats(residual1)
         state.append((residual1, xhat2, rstd2))
-    normed2 = [spread((s[1] * norm_gains[1] + norm_shifts[1]).astype(BF)) for s in state]
-    grad_all = spread(after(out_grad, normed2[0]))
+    normed2 = [
+        spread(f"n2_{c}", (s[1] * norm_gains[1] + norm_shifts[1]).astype(BF))[0] for c, s in enumerate(state)
+    ]
+    grad_all, og_hops = spread("og", follow(out_grad, normed2[0][1], normed2[0][n - 1]))
 
     cross_q, cross_mix, cross_total, state3 = [], [], [], []
     for c in range(CHUNKS):
+        if c > 0:
+            normed2[c] = follow(normed2[c], sent, *og_hops[0])
         q = heads_of(product(normed2[c], full_cq).astype(BF).reshape(1, n * part, width))
         mix, total = attend(q, cross_k, cross_v, cross_allowed, scale)
         mix = mix.reshape(n, part, width)
-        residual2 = state[c][0] + sink(product(mix, full_cout).astype(BF))
+        sent = whole(product(mix, full_cout).astype(BF))
+        residual2 = state[c][0] + sink(f"r2_{c}", sent, {1: og_hops[1]} if c > 0 else {})[0]
         xhat3, rstd3 = norm_stats(residual2)
         cross_q.append(q)
         cross_mix.append(mix)
         cross_total.append(total)
         state3.append((residual2, xhat3, rstd3))
-    normed3 = [spread((s[1] * norm_gains[2] + norm_shifts[2]).astype(BF)) for s in state3]
-
-    block_out, acts, grad_hiddens, grad2, sums3 = [], [], [], [], []
+    normed3 = [
+        spread(f"n3_{c}", (s[1] * norm_gains[2] + norm_shifts[2]).astype(BF))[0] for c, s in enumerate(state3)
+    ]
+
+    out_parts, acts, grad_hiddens, grad2, sums3 = [], [], [], [], []
     for c, rows in enumerate(chunks):
         hidden = product(normed3[c], full_up)
         grad_rows = grad_all[:, rows]
@@ -209,19 +235,21 @@
         grad_hidden = gelu_back(right_inner(grad_rows, full_down))[0].astype(BF)
         acts.append(acted)
         grad_hiddens.append(grad_hidden)
-        grad_n3 = sink(right_inner(grad_hidden, full_up).astype(BF))
+        grad_n3 = sink(f"d3_{c}", right_inner(grad_hidden, full_up).astype(BF))[0]
         residual2, xhat3, rstd3 = state3[c]
         sums3.append(norm_sums(grad_n3, xhat3))
         grad2.append(out_grad[rows].astype(F32) + norm_back(grad_n3, xhat3, rstd3, norm_gains[2]))
-        block_out.append(
-            (residual2 + sink(product(acted, full_down).astype(BF))).astype(BF)
-        )
+        out_parts.append(whole(product(acted, full_down).astype(BF)))
     cat = lambda xs: jnp.concatenate(xs, axis=1)
     acted, grad_hidden, n3 = cat(acts), cat(grad_hiddens), cat(normed3)
     grad_down = left_inner(acted, cat([grad_all[:, rows] for rows in chunks]))
     grad_up = left_inner(n3, grad_hidden)
 
-    e2 = [spread(g.astype(BF)) for g in grad2]
+    e2, e2_hops = map(list, zip(*[spread(f"e2_{c}", g.astype(BF)) for c, g in enumerate(grad2)]))
+    out_sum, out_hops = sink(
+        "out", [jnp.concatenate([p[k] for p in out_parts]) for k in range(n)], {1: e2_hops[-1][1]}
+    )
+    block_out = (jnp.concatenate([s[0] for s in state3]) + out_sum).astype(BF)
     own_down = to_columns(grad_down)
     own_up = to_rows(grad_up)
     e2[-1] = after(e2[-1], grad_down, grad_up)
@@ -235,7 +263,8 @@
         grad_cqs.append(gq)
         grad_ck = grad_ck + gk
         grad_cv = grad_cv + gv
-        grad_n2 = sink(right_inner(gq, full_cq).astype(BF))
+        sent = whole(right_inner(gq if c == 0 else follow(gq, *out_hops[0]), full_cq).astype(BF))
+        grad_n2 = sink(f"d2_{c}", sent, {1: out_hops[1]} if c > 0 else {})[0]
         _, xhat2, rstd2 = state[c]
         sums2.append(norm_sums(grad_n2, xhat2))
         grad1.append(grad2[c] + norm_back(grad_n2, xhat2, rstd2, norm_gains[1]))
@@ -244,24 +273,28 @@
     grad_ckv = jnp.concatenate(
         [grad_ck.reshape(text_count, width), grad_cv.reshape(text_count, width)], axis=1
     ).astype(BF)
-    grad_text_part = right_inner(grad_ckv, full_ckv).astype(BF).reshape(n, -1, text.shape[2])
+    grad_text_part = whole(right_inner(grad_ckv, full_ckv).astype(BF).reshape(n, -1, text.shape[2]))
     grad_wckv = left_inner(text_rows, grad_ckv)
 
-    e1 = [spread(g.astype(BF)) for g in grad1]
+    grad1[0] = follow(grad1[0], *out_hops[2])
+    e1, e1_hops = map(list, zip(*[spread(f"e1_{c}", g.astype(BF)) for c, g in enumerate(grad1)]))
     own_cout = to_columns(grad_cout)
     own_cq = to_rows(grad_cq)
     own_ckv = to_rows(grad_wckv)
-    e1[-1] = after(e1[-1], grad_cout, grad_cq, grad_wckv, grad_text_part)
+    e1[-1] = after(e1[-1], grad_cout, grad_cq, grad_wckv)
     grad_mix = heads_of(cat([right_inner(e, full_out).astype(BF) for e in e1]))
     grad_mix = after(grad_mix, own_down, own_up)
     gq, gk, gv = attend_back(self_q, self_k, self_v, self_allowed, self_total, grad_mix, scale)
+    grad_text, text_hops = sink("text", grad_text_part, {1: e1_hops[-1][1], 2: (gq,)})
+    grad_text = grad_text.astype(BF)
     grad_qkv = jnp.concatenate(
         [g.astype(BF).reshape(n, PIX, width) for g in (gq, gk, gv)], axis=-1
     )
+    grad_qkv = follow(grad_qkv, *text_hops[0])
     grad_out = left_inner(self_mix, cat(e1))
     grad_wqkv = left_inner(normed1, grad_qkv)
-    grad_n1 = sink(right_inner(after(grad_qkv, grad_wqkv), full_qkv).astype(BF))
-    grad_text = sink(after(grad_text_part, grad_mix)).astype(BF)
+    grad_n1_part = whole(right_inner(after(grad_qkv, grad_wqkv), full_qkv).astype(BF))
+    grad_n1 = sink("d1", grad_n1_part, {1: text_hops[1]})[0]
     grad1 = jnp.concatenate(grad1)
     grad_n1 = after(grad_n1, own_cout, own_cq, own_ckv)
     grad_tokens = (grad1 + norm_back(grad_n1, xhat1, rstd1, norm_gains[0])).astype(BF)
@@ -272,7 +305,7 @@
     own_out = to_columns(grad_out)
     own_qkv = to_rows(grad_wqkv)
     return (
-        jnp.concatenate(block_out),
+        block_out,
         grad_tokens,
         grad_text,
         sums[:, 0],

time: 1270 us -> 1250 us (0.984)
  starting transfers between devices: 400 us -> 337 us
  local copies, waits for them, and re-layouts: 52 us -> 95.2 us
  waiting for transfers between devices: 343 us -> 307 us
  other arithmetic: 118 us -> 143 us
  between operations: 18.3 us -> 34.9 us
    ppermute x36 -> x33, starting transfers between devices: 207 us -> 155 us  [sink(): lax.ppermute(one.astype(BF), 'narrow', [(k, k + 1) for k in range(step)])]
    slice x0 -> x25, local copies, waits for them, and re-layouts: none -> 24.7 us  [follow(): nothing = sum((o[(0,) * o.ndim].astype(F32) for o in others)) * 0.0]
    ppermute x66, waiting for transfers between devices: 212 us -> 190 us  [the longest x33 189 us: spread(): lax.ppermute(other, 'narrow', [(k, k - 1) for k in range(1, n - step + 1)])]
    ppermute x66, starting transfers between devices: 154 us -> 139 us  [the longest x33 95.9 us: spread(): lax.ppermute(one, 'narrow', [(k, k + 1) for k in range(step - 1, n - 1)])]
    ppermute x36 -> x33, waiting for transfers between devices: 41.4 us -> 29 us  [sink(): lax.ppermute(other.astype(BF), 'narrow', [(k, k - 1) for k in range(n - s...]
    convert_element_type x24 -> x21, other arithmetic: 25.7 us -> 33.8 us  [sink(): one.astype(BF)]
    ppermute x36 -> x33, starting transfers between devices: 38.2 us -> 41.6 us  [sink(): lax.ppermute(other.astype(BF), 'narrow', [(k, k - 1) for k in range(n - s...]
    another operation x38 -> x36, other arithmetic: 33.8 us -> 35.9 us  [spread(): return (jnp.stack(parts), [(up[s], down[s]) for s in range(1, n)])]
  transfers between devices with their start and end apart: 152 -> 146, of which waited for: 43 -> 48; matrix products, arithmetic and copies ran while one was open for 31% -> 36% of each run, Pallas kernels for 0% -> 0%
where the time goes in v4:
time: 1250 us; the launch traced here: 1240 us
  starting transfers between devices  337 us (27%)
  waiting for transfers between devices  307 us (25%)
  matrix products  283 us (23%)
  other arithmetic  143 us (11%)
  local copies, waits for them, and re-layouts  95.2 us (8%)
  blocking collectives  42 us (3%)
  between operations  34.9 us (3%)
    ppermute x33, waiting for transfers between devices, spread(): lax.ppermute(other, 'narrow', [(k, k - 1) for k in range(1, n - step + 1)])  189 us
    ppermute x33, starting transfers between devices, sink(): lax.ppermute(one.astype(BF), 'narrow', [(k, k + 1) for k in range(step)])  155 us
    ppermute x33, starting transfers between devices, spread(): lax.ppermute(one, 'narrow', [(k, k + 1) for k in range(step - 1, n - 1)])  95.9 us
    ppermute x33, waiting for transfers between devices, sink(): lax.ppermute(one.astype(BF), 'narrow', [(k, k + 1) for k in range(step)])  87.1 us
    dot_general x12, matrix products, product(): lax.dot_general(left_side, right_side, (((left_side.ndim - 1,), (0,)), ((...  72 us
    dot_general x12, matrix products, right_inner(): lax.dot_general(left_side, right_side, (((left_side.ndim - 1,), (1,)), ((...  70.3 us
    dot_general x7, matrix products, left_inner(): lax.dot_general(left_side, right_side, ((rows, rows), ((), ())), preferre...  53.6 us
    ppermute x33, starting transfers between devices, spread(): lax.ppermute(other, 'narrow', [(k, k - 1) for k in range(1, n - step + 1)])  43.4 us
  transfers between devices with their start and end apart: 146, of which 48 were waited for; matrix products, arithmetic and copies ran while one was open for 36% of the time, Pallas kernels for 0%

profile of v4, /device:TPU:0, one launch (start us, length us, event | category | flops | bytes accessed | tf_op | source)
XLA Modules:
  0.0 1242.1 jit_solution(12241359171279397782)
XLA Ops:
  28.3 21.2 %collective-permute-done.1 = bf16[256,2048]{1,0:T(8,128)(2,1)S(1)} collective-permute-done((bf16[256,2048]{1,0:T(8,128)(2,1)S(1)}, bf16[256,2048]{1,0:T(8,128)(2,1)S(1)}, u32[]{:S(2)}, u32[]{:S(2)}) %collective-permute-start.1) | collective-permute-done | bytes 1048608 | tf_op jit(solution)/shard_map/spread_n1/ppermute | solution.py:62
  53.1 22.8 %collective-permute-done.2 = bf16[256,2048]{1,0:T(8,128)(2,1)} collective-permute-done((bf16[256,2048]{1,0:T(8,128)(2,1)S(1)}, bf16[256,2048]{1,0:T(8,128)(2,1)}, u32[]{:S(2)}, u32[]{:S(2)}) %collective-permute-start.2) | collective-permute-done | bytes 1048608 | tf_op jit(solution)/shard_map/spread_n1/ppermute | solution.py:62
  80.2 21.5 %collective-permute-done.3 = bf16[256,2048]{1,0:T(8,128)(2,1)} collective-permute-done((bf16[256,2048]{1,0:T(8,128)(2,1)}, bf16[256,2048]{1,0:T(8,128)(2,1)}, u32[]{:S(2)}, u32[]{:S(2)}) %collective-permute-start.3) | collective-permute-done | bytes 1048608 | tf_op jit(solution)/shard_map/spread_n1/ppermute | solution.py:62
  108.5 9.4 fusion.91
  198.0 10.6 collective-permute-start.12
  210.0 10.5 collective-permute-done.11
  256.2 9.2 collective-permute-done.37
  278.7 9.3 collective-permute-done.38
  326.8 9.1 convolution_convert_fusion.7
  352.6 14.2 %collective-permute-start.24 = (bf16[128,2048]{1,0:T(8,128)(2,1)}, bf16[128,2048]{1,0:T(8,128)(2,1)}, u32[]{:S(2)}, u32[]{:S(2)}) collective-permute-start(bf16[128,2048]{1,0:T(8,128)(2,1)} %get-tuple-element.112), channel_id=1, source_target_pairs={{0,1},{4,5},{8,9},{12,13},{16,17},{20,21},{24,25},{28,29}} | collective-permute-start | bytes 1572872 | tf_op jit(solution)/shard_map/sink_r2_0/ppermute | solution.py:80
  398.4 13.5 %collective-permute-start.25 = (bf16[128,2048]{1,0:T(8,128)(2,1)S(1)}, bf16[128,2048]{1,0:T(8,128)(2,1)S(1)}, u32[]{:S(2)}, u32[]{:S(2)}) collective-permute-start(bf16[128,2048]{1,0:T(8,128)(2,1)S(1)} %get-tuple-element.110), channel_id=1, source_target_pairs={{0,1},{1,2},{4,5},{5,6},{8,9},{9,10},{12,13},{13,14},{16,17},{17,1... | collective-permute-start | bytes 1572872 | tf_op jit(solution)/shard_map/sink_r2_0/ppermute | solution.py:80
  442.7 9.2 collective-permute-done.47
  536.9 11.9 multiply_convert_fusion.3
  548.9 10.5 fusion.36
  559.5 11.4 multiply_convert_fusion.4
  570.9 8.6 fusion.29
  580.8 11.8 convolution_bitcast_fusion.1
  592.7 8.7 fusion.114
  603.9 9.7 fusion.117
  635.6 11.4 convolution_bitcast_fusion.2
  752.2 9.7 fusion.270
  776.8 8.8 fusion.267
  841.8 8.9 fusion.233
  906.7 12.4 %collective-permute-start.108 = (bf16[128,2048]{1,0:T(8,128)(2,1)}, bf16[128,2048]{1,0:T(8,128)(2,1)}, u32[]{:S(2)}, u32[]{:S(2)}) collective-permute-start(bf16[128,2048]{1,0:T(8,128)(2,1)} %get-tuple-element.45), channel_id=1, source_target_pairs={{0,1},{1,2},{2,3},{4,5},{5,6},{6,7},{8,9},{9,10},{10,11},{12,13},{... | collective-permute-start | bytes 1572872 | tf_op jit(solution)/shard_map/spread_e1_0/ppermute | solution.py:61
  953.7 9.6 collective-permute-done.116
  1028.6 8.9 fusion.224
  1051.6 11.8 fusion.227
  1074.5 8.8 convolution_bitcast_fusion
  1085.5 9.0 fusion.94
  1103.6 19.5 %collective-permute-done.124 = bf16[256,2048]{1,0:T(8,128)(2,1)S(1)} collective-permute-done((bf16[256,2048]{1,0:T(8,128)(2,1)S(1)}, bf16[256,2048]{1,0:T(8,128)(2,1)S(1)}, u32[]{:S(2)}, u32[]{:S(2)}) %collective-permute-start.124) | collective-permute-done | bytes 1048608 | tf_op jit(solution)/shard_map/sink_d1/ppermute | solution.py:80
  1162.3 9.0 collective-permute-done.130
  1187.1 42.0 %psum.7 = f32[3,2,2048]{2,0,1:T(4,128)S(1)} all-reduce(f32[3,2,2048]{2,0,1:T(4,128)S(1)} %pad_maximum_fusion.16), channel_id=1, replica_groups=mesh['wide'=8,'narrow'=4] {'wide','narrow'}, use_global_device_ids=true, to_apply=%region_44.45 | all-reduce | flops 12288 | bytes 98304 | tf_op jit(solution)/shard_map/psum | solution.py:301
  (921 shorter events, 804.4 us)
Async XLA Ops:
  7.2 101.3 %all-gather.8.cloned.1.call-start = ((), (), s32[]{:S(2)}) async-start(), calls=%async_computation.7 | async-start | bytes 7077888 | tf_op jit(solution)/shard_map/all_gather | solution.py:158
  11.6 115.7 %all-gather.10.cloned.1.call-start = ((), (), s32[]{:S(2)}) async-start(), calls=%async_computation.8 | async-start | bytes 2359296 | tf_op jit(solution)/shard_map/all_gather | solution.py:163
  12.4 298.4 %all-gather.14.cloned.1.call-start = ((), (), s32[]{:S(2)}) async-start(), calls=%async_computation.10 | async-start | bytes 2359296 | tf_op jit(solution)/shard_map/all_gather | solution.py:158
  14.4 312.4 %all-gather.12.cloned.1.call-start = ((), (), s32[]{:S(2)}) async-start(), calls=%async_computation.9 | async-start | bytes 9437184 | tf_op jit(solution)/shard_map/all_gather | solution.py:158
  17.0 330.4 %all-gather.16.cloned.1.call-start = ((), (), s32[]{:S(2)}) async-start(), calls=%async_computation.11 | async-start | bytes 2359296 | tf_op jit(solution)/shard_map/all_gather | solution.py:163
  18.8 518.1 %all-gather.18.cloned.1.call-start = ((), (), s32[]{:S(2)}) async-start(), calls=%async_computation.12 | async-start | bytes 9437184 | tf_op jit(solution)/shard_map/all_gather | solution.py:158
  20.0 528.9 %all-gather.20.cloned.1.call-start = ((), (), s32[]{:S(2)}) async-start(), calls=%async_computation.13 | async-start | bytes 9437184 | tf_op jit(solution)/shard_map/all_gather | solution.py:163
  106.6 61.4 %collective-permute-start.13 = (bf16[128,4096]{1,0:T(8,128)(2,1)}, bf16[128,4096]{1,0:T(8,128)(2,1)}, u32[]{:S(2)}, u32[]{:S(2)}) collective-permute-start(bf16[128,4096]{1,0:T(8,128)(2,1)} %broadcast_add_fusion.3), channel_id=1, source_target_pairs={{1,0},{2,1},{3,2},{5,4},{6,5},{7,6},{9,8},{10,9},{11,10},{13,12},{... | collective-permute-start | bytes 3145736 | tf_op jit(solution)/shard_map/spread_text/ppermute | solution.py:62
  147.5 871.0 %reduce-scatter.10.cloned.1.call-start = ((), (), s32[]{:S(2)}) async-start(), calls=%async_computation.15 | async-start | bytes 9437184 | tf_op jit(solution)/shard_map/reduce_scatter | solution.py:166
  172.1 36.6 %collective-permute-start.32 = (bf16[128,2048]{1,0:T(8,128)(2,1)S(1)}, bf16[128,2048]{1,0:T(8,128)(2,1)S(1)}, u32[]{:S(2)}, u32[]{:S(2)}) collective-permute-start(bf16[128,2048]{1,0:T(8,128)(2,1)S(1)} %get-tuple-element.128), channel_id=1, source_target_pairs={{0,1},{1,2},{2,3},{4,5},{5,6},{6,7},{8,9},{9,10},{10,11},{12,13},{... | collective-permute-start | bytes 1572872 | tf_op jit(solution)/shard_map/sink_r1_1/ppermute | solution.py:80
  183.3 37.2 %collective-permute-start.11 = (bf16[128,2048]{1,0:T(8,128)(2,1)S(1)}, bf16[128,2048]{1,0:T(8,128)(2,1)S(1)}, u32[]{:S(2)}, u32[]{:S(2)}) collective-permute-start(bf16[128,2048]{1,0:T(8,128)(2,1)S(1)} %get-tuple-element.123), channel_id=1, source_target_pairs={{1,0},{2,1},{3,2},{5,4},{6,5},{7,6},{9,8},{10,9},{11,10},{13,12},{... | collective-permute-start | bytes 1572872 | tf_op jit(solution)/shard_map/sink_r1_0/ppermute | solution.py:81
  184.6 35.9 %collective-permute-start.8 = (bf16[128,2048]{1,0:T(8,128)(2,1)S(1)}, bf16[128,2048]{1,0:T(8,128)(2,1)S(1)}, u32[]{:S(2)}, u32[]{:S(2)}) collective-permute-start(bf16[128,2048]{1,0:T(8,128)(2,1)S(1)} %get-tuple-element.122), channel_id=1, source_target_pairs={{0,1},{1,2},{2,3},{4,5},{5,6},{6,7},{8,9},{9,10},{10,11},{12,13},{... | collective-permute-start | bytes 1572872 | tf_op jit(solution)/shard_map/sink_r1_0/ppermute | solution.py:80
  230.0 35.4 %collective-permute-start.37 = (bf16[128,2048]{1,0:T(8,128)(2,1)S(1)}, bf16[128,2048]{1,0:T(8,128)(2,1)S(1)}, u32[]{:S(2)}, u32[]{:S(2)}) collective-permute-start(bf16[128,2048]{1,0:T(8,128)(2,1)S(1)} %get-tuple-element.158), channel_id=1, source_target_pairs={{1,0},{2,1},{3,2},{5,4},{6,5},{7,6},{9,8},{10,9},{11,10},{13,12},{... | collective-permute-start | bytes 1572872 | tf_op jit(solution)/shard_map/spread_n2_1/ppermute | solution.py:62
  231.3 35.4 %collective-permute-start.36 = (bf16[128,2048]{1,0:T(8,128)(2,1)S(1)}, bf16[128,2048]{1,0:T(8,128)(2,1)S(1)}, u32[]{:S(2)}, u32[]{:S(2)}) collective-permute-start(bf16[128,2048]{1,0:T(8,128)(2,1)S(1)} %get-tuple-element.158), channel_id=1, source_target_pairs={{0,1},{1,2},{2,3},{4,5},{5,6},{6,7},{8,9},{9,10},{10,11},{12,13},{... | collective-permute-start | bytes 1572872 | tf_op jit(solution)/shard_map/spread_n2_1/ppermute | solution.py:61
  244.1 49.7 %collective-permute-start.16 = (bf16[128,4096]{1,0:T(8,128)(2,1)S(1)}, bf16[128,4096]{1,0:T(8,128)(2,1)}, u32[]{:S(2)}, u32[]{:S(2)}) collective-permute-start(bf16[128,4096]{1,0:T(8,128)(2,1)S(1)} %get-tuple-element.143), channel_id=1, source_target_pairs={{1,2},{2,3},{5,6},{6,7},{9,10},{10,11},{13,14},{14,15},{17,18},{18... | collective-permute-start | bytes 3145736 | tf_op jit(solution)/shard_map/spread_text/ppermute | solution.py:61
  301.9 69.0 %collective-permute-start.43 = (bf16[256,2048]{1,0:T(8,128)(2,1)}, bf16[256,2048]{1,0:T(8,128)(2,1)}, u32[]{:S(2)}, u32[]{:S(2)}) collective-permute-start(bf16[256,2048]{1,0:T(8,128)(2,1)} %broadcast_add_fusion), channel_id=1, source_target_pairs={{1,0},{2,1},{3,2},{5,4},{6,5},{7,6},{9,8},{10,9},{11,10},{13,12},{... | collective-permute-start | bytes 3145736 | tf_op jit(solution)/shard_map/spread_og/ppermute | solution.py:62
  303.1 65.2 %collective-permute-start.42 = (bf16[256,2048]{1,0:T(8,128)(2,1)}, bf16[256,2048]{1,0:T(8,128)(2,1)}, u32[]{:S(2)}, u32[]{:S(2)}) collective-permute-start(bf16[256,2048]{1,0:T(8,128)(2,1)} %broadcast_add_fusion), channel_id=1, source_target_pairs={{0,1},{1,2},{2,3},{4,5},{5,6},{6,7},{8,9},{9,10},{10,11},{12,13},{... | collective-permute-start | bytes 3145736 | tf_op jit(solution)/shard_map/spread_og/ppermute | solution.py:61
  352.6 44.3 %collective-permute-start.24 = (bf16[128,2048]{1,0:T(8,128)(2,1)}, bf16[128,2048]{1,0:T(8,128)(2,1)}, u32[]{:S(2)}, u32[]{:S(2)}) collective-permute-start(bf16[128,2048]{1,0:T(8,128)(2,1)} %get-tuple-element.112), channel_id=1, source_target_pairs={{0,1},{4,5},{8,9},{12,13},{16,17},{20,21},{24,25},{28,29}} | collective-permute-start | bytes 1572872 | tf_op jit(solution)/shard_map/sink_r2_0/ppermute | solution.py:80
  432.5 45.6 %collective-permute-start.64 = (bf16[256,2048]{1,0:T(8,128)(2,1)}, bf16[256,2048]{1,0:T(8,128)(2,1)S(1)}, u32[]{:S(2)}, u32[]{:S(2)}) collective-permute-start(bf16[256,2048]{1,0:T(8,128)(2,1)} %collective-permute-done.45), channel_id=1, source_target_pairs={{1,0},{5,4},{9,8},{13,12},{17,16},{21,20},{25,24},{29,28}} | collective-permute-start | bytes 3145736 | tf_op jit(solution)/shard_map/spread_og/ppermute | solution.py:62
  441.2 49.7 %collective-permute-start.65 = (bf16[256,2048]{1,0:T(8,128)(2,1)}, bf16[256,2048]{1,0:T(8,128)(2,1)S(1)}, u32[]{:S(2)}, u32[]{:S(2)}) collective-permute-start(bf16[256,2048]{1,0:T(8,128)(2,1)} %collective-permute-done.44), channel_id=1, source_target_pairs={{2,3},{6,7},{10,11},{14,15},{18,19},{22,23},{26,27},{30,31}} | collective-permute-start | bytes 3145736 | tf_op jit(solution)/shard_map/spread_og/ppermute | solution.py:61
  592.7 428.7 %reduce-scatter.8.cloned.1.call-start = ((), (), s32[]{:S(2)}) async-start(), calls=%async_computation.14 | async-start | bytes 9437184 | tf_op jit(solution)/shard_map/reduce_scatter | solution.py:169
  647.0 496.1 %reduce-scatter.14.cloned.1.call-start = ((), (), s32[]{:S(2)}) async-start(), calls=%async_computation.17 | async-start | bytes 2359296 | tf_op jit(solution)/shard_map/reduce_scatter | solution.py:166
  722.3 80.5 %collective-permute-start.79 = (bf16[256,2048]{1,0:T(8,128)(2,1)}, bf16[256,2048]{1,0:T(8,128)(2,1)}, u32[]{:S(2)}, u32[]{:S(2)}) collective-permute-start(bf16[256,2048]{1,0:T(8,128)(2,1)} %fusion.316), channel_id=1, source_target_pairs={{3,2},{7,6},{11,10},{15,14},{19,18},{23,22},{27,26},{31,30}} | collective-permute-start | bytes 3145736 | tf_op jit(solution)/shard_map/sink_out/ppermute | solution.py:81
  725.1 77.7 %collective-permute-start.76 = (bf16[256,2048]{1,0:T(8,128)(2,1)}, bf16[256,2048]{1,0:T(8,128)(2,1)}, u32[]{:S(2)}, u32[]{:S(2)}) collective-permute-start(bf16[256,2048]{1,0:T(8,128)(2,1)} %fusion.317), channel_id=1, source_target_pairs={{0,1},{4,5},{8,9},{12,13},{16,17},{20,21},{24,25},{28,29}} | collective-permute-start | bytes 3145736 | tf_op jit(solution)/shard_map/sink_out/ppermute | solution.py:80
  730.9 35.1 %collective-permute-start.91 = (bf16[128,2048]{1,0:T(8,128)(2,1)}, bf16[128,2048]{1,0:T(8,128)(2,1)}, u32[]{:S(2)}, u32[]{:S(2)}) collective-permute-start(bf16[128,2048]{1,0:T(8,128)(2,1)} %collective-permute-done.90), channel_id=1, source_target_pairs={{1,0},{5,4},{9,8},{13,12},{17,16},{21,20},{25,24},{29,28}} | collective-permute-start | bytes 1572872 | tf_op jit(solution)/shard_map/spread_e2_0/ppermute | solution.py:62
  850.7 294.3 %reduce-scatter.12.cloned.1.call-start = ((), (), s32[]{:S(2)}) async-start(), calls=%async_computation.16 | async-start | bytes 2359296 | tf_op jit(solution)/shard_map/reduce_scatter | solution.py:169
  947.7 199.2 %reduce-scatter.20.cloned.1.call-start = ((), (), s32[]{:S(2)}) async-start(), calls=%async_computation.20 | async-start | bytes 2359296 | tf_op jit(solution)/shard_map/reduce_scatter | solution.py:169
  983.1 191.5 %reduce-scatter.16.cloned.1.call-start = ((), (), s32[]{:S(2)}) async-start(), calls=%async_computation.18 | async-start | bytes 9437184 | tf_op jit(solution)/shard_map/reduce_scatter | solution.py:166
  983.8 249.2 %reduce-scatter.18.cloned.1.call-start = ((), (), s32[]{:S(2)}) async-start(), calls=%async_computation.19 | async-start | bytes 7077888 | tf_op jit(solution)/shard_map/reduce_scatter | solution.py:166
  1042.7 51.9 %collective-permute-start.122 = (bf16[128,4096]{1,0:T(8,128)(2,1)}, bf16[128,4096]{1,0:T(8,128)(2,1)}, u32[]{:S(2)}, u32[]{:S(2)}) collective-permute-start(bf16[128,4096]{1,0:T(8,128)(2,1)} %get-tuple-element.70), channel_id=1, source_target_pairs={{0,1},{1,2},{4,5},{5,6},{8,9},{9,10},{12,13},{13,14},{16,17},{17,1... | collective-permute-start | bytes 3145736 | tf_op jit(solution)/shard_map/sink_text/ppermute | solution.py:80
  1048.3 48.1 %collective-permute-start.123 = (bf16[128,4096]{1,0:T(8,128)(2,1)}, bf16[128,4096]{1,0:T(8,128)(2,1)}, u32[]{:S(2)}, u32[]{:S(2)}) collective-permute-start(bf16[128,4096]{1,0:T(8,128)(2,1)} %get-tuple-element.69), channel_id=1, source_target_pairs={{2,1},{3,2},{6,5},{7,6},{10,9},{11,10},{14,13},{15,14},{18,17},{19... | collective-permute-start | bytes 3145736 | tf_op jit(solution)/shard_map/sink_text/ppermute | solution.py:81
  1134.9 36.4 %collective-permute-start.130 = (bf16[128,4096]{1,0:T(8,128)(2,1)}, bf16[128,4096]{1,0:T(8,128)(2,1)}, u32[]{:S(2)}, u32[]{:S(2)}) collective-permute-start(bf16[128,4096]{1,0:T(8,128)(2,1)} %get-tuple-element.61), channel_id=1, source_target_pairs={{0,1},{1,2},{2,3},{4,5},{5,6},{6,7},{8,9},{9,10},{10,11},{12,13},{... | collective-permute-start | bytes 3145736 | tf_op jit(solution)/shard_map/sink_text/ppermute | solution.py:80
  (302 other events, 6672.0 us)
Sparse Core Ops, SparseCore 0:
  11.7 48.1 all-gather.7
  62.3 28.0 all-gather.9
  92.9 27.7 all-gather.13
  122.4 54.2 all-gather.11
  178.4 28.0 all-gather.15
  208.3 54.2 all-gather.17
  264.5 55.8 all-gather.19
  592.8 71.6 reduce-scatter.9
  667.9 71.2 reduce-scatter.7
  850.8 44.3 reduce-scatter.13
  947.8 50.7 reduce-scatter.11
  1001.7 41.1 reduce-scatter.19
  1046.3 71.5 reduce-scatter.15
  1121.1 61.7 reduce-scatter.17

commit v5 on v4

--- a/solution.py
+++ b/solution.py
@@ -64,22 +64,21 @@
         return jnp.stack(parts), [(up[s], down[s]) for s in range(1, n)]
 
 
-def sink(name, parts, gates={}):
+def sink(name, parts, gates={}, hops=(), until=None):
     n = lax.axis_size("narrow")
-    hops = []
+    hops = list(hops)
     with jax.named_scope("sink_" + name):
-        for step in range(1, n):
+        for step in range(len(hops) + 1, until or n):
             one, other = parts[step], parts[n - step]
-            gate = gates.get(step, ())
-            if callable(gate):
-                gate = gate(hops[0])
             if hops:
                 one = hops[-1][0].astype(F32) + one.astype(F32)
                 other = hops[-1][1].astype(F32) + other.astype(F32)
-            one, other = follow(one, *gate), follow(other, *gate)
+            one, other = follow(one, *gates.get(step, ())), follow(other, *gates.get(step, ()))
             up = lax.ppermute(one.astype(BF), "narrow", [(k, k + 1) for k in range(step)])
             down = lax.ppermute(other.astype(BF), "narrow", [(k, k - 1) for k in range(n - step, n)])
             hops.append((up, down))
+        if until:
+            return None, hops
         return up.astype(F32) + down.astype(F32) + parts[0].astype(F32), hops
 
 
@@ -169,16 +168,16 @@
         return lax.psum_scatter(g.astype(BF), "wide", scatter_dimension=1, tiled=True).astype(F32)
 
     full_qkv = rows_of(w_query, w_key, w_value)
+
+    residual0 = tokens.astype(F32)
+    xhat1, rstd1 = norm_stats(residual0)
+    own1 = (xhat1 * norm_gains[0] + norm_shifts[0]).astype(BF)
     full_out = columns_of(w_out)
     full_ckv = rows_of(w_cross_key, w_cross_value)
     full_cq = rows_of(w_cross_query)
     full_cout = columns_of(w_cross_out)
     full_up = rows_of(w_up)
     full_down = columns_of(w_down)
-
-    residual0 = tokens.astype(F32)
-    xhat1, rstd1 = norm_stats(residual0)
-    own1 = (xhat1 * norm_gains[0] + norm_shifts[0]).astype(BF)
     normed1 = spread("n1", own1)[0]
     qkv = product(normed1, full_qkv).astype(BF)
     heads_of = lambda x: x.reshape(x.shape[:-1] + (x.shape[-1] // HEAD_DIM, HEAD_DIM))
@@ -246,10 +245,8 @@
     grad_up = left_inner(n3, grad_hidden)
 
     e2, e2_hops = map(list, zip(*[spread(f"e2_{c}", g.astype(BF)) for c, g in enumerate(grad2)]))
-    out_sum, out_hops = sink(
-        "out", [jnp.concatenate([p[k] for p in out_parts]) for k in range(n)], {1: e2_hops[-1][1]}
-    )
-    block_out = (jnp.concatenate([s[0] for s in state3]) + out_sum).astype(BF)
+    out_parts = [jnp.concatenate([p[k] for p in out_parts]) for k in range(n)]
+    out_hops = sink("out", out_parts, {1: e2_hops[-1][1]}, until=n - 1)[1]
     own_down = to_columns(grad_down)
     own_up = to_rows(grad_up)
     e2[-1] = after(e2[-1], grad_down, grad_up)
@@ -276,7 +273,6 @@
     grad_text_part = whole(right_inner(grad_ckv, full_ckv).astype(BF).reshape(n, -1, text.shape[2]))
     grad_wckv = left_inner(text_rows, grad_ckv)
 
-    grad1[0] = follow(grad1[0], *out_hops[2])
     e1, e1_hops = map(list, zip(*[spread(f"e1_{c}", g.astype(BF)) for c, g in enumerate(grad1)]))
     own_cout = to_columns(grad_cout)
     own_cq = to_rows(grad_cq)
@@ -285,16 +281,18 @@
     grad_mix = heads_of(cat([right_inner(e, full_out).astype(BF) for e in e1]))
     grad_mix = after(grad_mix, own_down, own_up)
     gq, gk, gv = attend_back(self_q, self_k, self_v, self_allowed, self_total, grad_mix, scale)
+    out_sum, out_hops = sink("out", out_parts, {n - 1: e1_hops[-1][1]}, out_hops)
+    block_out = (jnp.concatenate([s[0] for s in state3]) + out_sum).astype(BF)
     grad_text, text_hops = sink("text", grad_text_part, {1: e1_hops[-1][1], 2: (gq,)})
     grad_text = grad_text.astype(BF)
     grad_qkv = jnp.concatenate(
         [g.astype(BF).reshape(n, PIX, width) for g in (gq, gk, gv)], axis=-1
     )
-    grad_qkv = follow(grad_qkv, *text_hops[0])
+    grad_qkv = follow(grad_qkv, *text_hops[1])
     grad_out = left_inner(self_mix, cat(e1))
-    grad_wqkv = left_inner(normed1, grad_qkv)
-    grad_n1_part = whole(right_inner(after(grad_qkv, grad_wqkv), full_qkv).astype(BF))
-    grad_n1 = sink("d1", grad_n1_part, {1: text_hops[1]})[0]
+    grad_n1_part = whole(right_inner(grad_qkv, full_qkv).astype(BF))
+    grad_n1 = sink("d1", grad_n1_part, {1: out_hops[-1]})[0]
+    grad_wqkv = left_inner(normed1, after(grad_qkv, grad_n1_part))
     grad1 = jnp.concatenate(grad1)
     grad_n1 = after(grad_n1, own_cout, own_cq, own_ckv)
     grad_tokens = (grad1 + norm_back(grad_n1, xhat1, rstd1, norm_gains[0])).astype(BF)

time: 1250 us -> 1240 us (level)
  other arithmetic: 143 us -> 159 us
  waiting for transfers between devices: 307 us -> 294 us
    ppermute x33, waiting for transfers between devices: 87.1 us -> 70.8 us  [sink(): lax.ppermute(one.astype(BF), 'narrow', [(k, k + 1) for k in range(step)])]
  transfers between devices with their start and end apart: 146 -> 146, of which waited for: 48 -> 44; matrix products, arithmetic and copies ran while one was open for 36% -> 38% of each run, Pallas kernels for 0% -> 0%
where the time goes in v5:
time: 1240 us; the launch traced here: 1230 us
  starting transfers between devices  329 us (27%)
  waiting for transfers between devices  294 us (24%)
  matrix products  290 us (23%)
  other arithmetic  159 us (13%)
  local copies, waits for them, and re-layouts  86 us (7%)
  blocking collectives  40.7 us (3%)
  between operations  33 us (3%)
    ppermute x33, waiting for transfers between devices, spread(): lax.ppermute(other, 'narrow', [(k, k - 1) for k in range(1, n - step + 1)])  189 us
    ppermute x33, starting transfers between devices, sink(): lax.ppermute(one.astype(BF), 'narrow', [(k, k + 1) for k in range(step)])  152 us
    ppermute x33, starting transfers between devices, spread(): lax.ppermute(one, 'narrow', [(k, k + 1) for k in range(step - 1, n - 1)])  89.2 us
    dot_general x12, matrix products, right_inner(): lax.dot_general(left_side, right_side, (((left_side.ndim - 1,), (1,)), ((...  73.6 us
    dot_general x12, matrix products, product(): lax.dot_general(left_side, right_side, (((left_side.ndim - 1,), (0,)), ((...  72 us
    ppermute x33, waiting for transfers between devices, sink(): lax.ppermute(one.astype(BF), 'narrow', [(k, k + 1) for k in range(step)])  70.8 us
    dot_general x7, matrix products, left_inner(): lax.dot_general(left_side, right_side, ((rows, rows), ((), ())), preferre...  53.8 us
    ppermute x33, starting transfers between devices, spread(): lax.ppermute(other, 'narrow', [(k, k - 1) for k in range(1, n - step + 1)])  43.4 us
  transfers between devices with their start and end apart: 146, of which 44 were waited for; matrix products, arithmetic and copies ran while one was open for 38% of the time, Pallas kernels for 0%

profile of v5, /device:TPU:0, one launch (start us, length us, event | category | flops | bytes accessed | tf_op | source)
XLA Modules:
  0.0 1231.6 jit_solution(17541343661595300280)
XLA Ops:
  28.3 21.2 %collective-permute-done.1 = bf16[256,2048]{1,0:T(8,128)(2,1)S(1)} collective-permute-done((bf16[256,2048]{1,0:T(8,128)(2,1)S(1)}, bf16[256,2048]{1,0:T(8,128)(2,1)S(1)}, u32[]{:S(2)}, u32[]{:S(2)}) %collective-permute-start.1) | collective-permute-done | bytes 1048608 | tf_op jit(solution)/shard_map/spread_n1/ppermute | solution.py:62
  53.1 22.8 %collective-permute-done.2 = bf16[256,2048]{1,0:T(8,128)(2,1)} collective-permute-done((bf16[256,2048]{1,0:T(8,128)(2,1)S(1)}, bf16[256,2048]{1,0:T(8,128)(2,1)}, u32[]{:S(2)}, u32[]{:S(2)}) %collective-permute-start.2) | collective-permute-done | bytes 1048608 | tf_op jit(solution)/shard_map/spread_n1/ppermute | solution.py:62
  80.2 21.5 %collective-permute-done.3 = bf16[256,2048]{1,0:T(8,128)(2,1)} collective-permute-done((bf16[256,2048]{1,0:T(8,128)(2,1)}, bf16[256,2048]{1,0:T(8,128)(2,1)}, u32[]{:S(2)}, u32[]{:S(2)}) %collective-permute-start.3) | collective-permute-done | bytes 1048608 | tf_op jit(solution)/shard_map/spread_n1/ppermute | solution.py:62
  108.5 9.4 fusion.91
  198.0 10.8 collective-permute-start.12
  210.2 10.3 collective-permute-done.11
  256.2 9.2 collective-permute-done.37
  278.7 9.3 collective-permute-done.38
  326.5 9.1 convolution_convert_fusion.7
  352.3 14.5 %collective-permute-start.24 = (bf16[128,2048]{1,0:T(8,128)(2,1)}, bf16[128,2048]{1,0:T(8,128)(2,1)}, u32[]{:S(2)}, u32[]{:S(2)}) collective-permute-start(bf16[128,2048]{1,0:T(8,128)(2,1)} %get-tuple-element.112), channel_id=1, source_target_pairs={{0,1},{4,5},{8,9},{12,13},{16,17},{20,21},{24,25},{28,29}} | collective-permute-start | bytes 1572872 | tf_op jit(solution)/shard_map/sink_r2_0/ppermute | solution.py:77
  398.3 13.5 %collective-permute-start.25 = (bf16[128,2048]{1,0:T(8,128)(2,1)S(1)}, bf16[128,2048]{1,0:T(8,128)(2,1)S(1)}, u32[]{:S(2)}, u32[]{:S(2)}) collective-permute-start(bf16[128,2048]{1,0:T(8,128)(2,1)S(1)} %get-tuple-element.110), channel_id=1, source_target_pairs={{0,1},{1,2},{4,5},{5,6},{8,9},{9,10},{12,13},{13,14},{16,17},{17,1... | collective-permute-start | bytes 1572872 | tf_op jit(solution)/shard_map/sink_r2_0/ppermute | solution.py:77
  442.9 9.2 collective-permute-done.47
  537.1 11.9 multiply_convert_fusion.3
  549.0 10.5 fusion.36
  559.6 11.4 multiply_convert_fusion.4
  581.0 11.8 convolution_bitcast_fusion
  592.9 8.7 fusion.114
  604.0 9.6 fusion.117
  635.8 11.4 convolution_bitcast_fusion.1
  757.4 9.6 fusion.270
  777.6 8.8 fusion.267
  835.8 9.9 fusion.131
  859.4 10.0 fusion.233
  936.2 9.5 collective-permute-done.91
  968.0 9.7 convolution_convert_fusion
  1011.5 9.0 fusion.224
  1039.3 11.6 fusion.227
  1063.3 11.3 fusion.94
  1074.5 8.9 bitcast_convert_fusion
  1099.0 11.7 collective-permute-done.124
  1132.8 8.7 collective-permute-done.125
  1177.8 40.7 %psum.7 = f32[3,2,2048]{2,0,1:T(4,128)S(1)} all-reduce(f32[3,2,2048]{2,0,1:T(4,128)S(1)} %pad_maximum_fusion.16), channel_id=1, replica_groups=mesh['wide'=8,'narrow'=4] {'wide','narrow'}, use_global_device_ids=true, to_apply=%region_44.45 | all-reduce | flops 12288 | bytes 98304 | tf_op jit(solution)/shard_map/psum | solution.py:299
  (903 shorter events, 803.3 us)
Async XLA Ops:
  7.2 101.3 %all-gather.8.cloned.1.call-start = ((), (), s32[]{:S(2)}) async-start(), calls=%async_computation.7 | async-start | bytes 7077888 | tf_op jit(solution)/shard_map/all_gather | solution.py:157
  11.6 115.8 %all-gather.10.cloned.1.call-start = ((), (), s32[]{:S(2)}) async-start(), calls=%async_computation.8 | async-start | bytes 2359296 | tf_op jit(solution)/shard_map/all_gather | solution.py:162
  12.4 298.2 %all-gather.14.cloned.1.call-start = ((), (), s32[]{:S(2)}) async-start(), calls=%async_computation.10 | async-start | bytes 2359296 | tf_op jit(solution)/shard_map/all_gather | solution.py:157
  14.4 312.2 %all-gather.12.cloned.1.call-start = ((), (), s32[]{:S(2)}) async-start(), calls=%async_computation.9 | async-start | bytes 9437184 | tf_op jit(solution)/shard_map/all_gather | solution.py:157
  17.0 330.0 %all-gather.16.cloned.1.call-start = ((), (), s32[]{:S(2)}) async-start(), calls=%async_computation.11 | async-start | bytes 2359296 | tf_op jit(solution)/shard_map/all_gather | solution.py:162
  18.8 518.2 %all-gather.18.cloned.1.call-start = ((), (), s32[]{:S(2)}) async-start(), calls=%async_computation.12 | async-start | bytes 9437184 | tf_op jit(solution)/shard_map/all_gather | solution.py:157
  20.0 529.0 %all-gather.20.cloned.1.call-start = ((), (), s32[]{:S(2)}) async-start(), calls=%async_computation.13 | async-start | bytes 9437184 | tf_op jit(solution)/shard_map/all_gather | solution.py:162
  106.6 61.4 %collective-permute-start.13 = (bf16[128,4096]{1,0:T(8,128)(2,1)}, bf16[128,4096]{1,0:T(8,128)(2,1)}, u32[]{:S(2)}, u32[]{:S(2)}) collective-permute-start(bf16[128,4096]{1,0:T(8,128)(2,1)} %broadcast_add_fusion.3), channel_id=1, source_target_pairs={{1,0},{2,1},{3,2},{5,4},{6,5},{7,6},{9,8},{10,9},{11,10},{13,12},{... | collective-permute-start | bytes 3145736 | tf_op jit(solution)/shard_map/spread_text/ppermute | solution.py:62
  147.5 853.0 %reduce-scatter.10.cloned.1.call-start = ((), (), s32[]{:S(2)}) async-start(), calls=%async_computation.15 | async-start | bytes 9437184 | tf_op jit(solution)/shard_map/reduce_scatter | solution.py:165
  172.1 36.8 %collective-permute-start.32 = (bf16[128,2048]{1,0:T(8,128)(2,1)S(1)}, bf16[128,2048]{1,0:T(8,128)(2,1)S(1)}, u32[]{:S(2)}, u32[]{:S(2)}) collective-permute-start(bf16[128,2048]{1,0:T(8,128)(2,1)S(1)} %get-tuple-element.128), channel_id=1, source_target_pairs={{0,1},{1,2},{2,3},{4,5},{5,6},{6,7},{8,9},{9,10},{10,11},{12,13},{... | collective-permute-start | bytes 1572872 | tf_op jit(solution)/shard_map/sink_r1_1/ppermute | solution.py:77
  183.3 37.2 %collective-permute-start.11 = (bf16[128,2048]{1,0:T(8,128)(2,1)S(1)}, bf16[128,2048]{1,0:T(8,128)(2,1)S(1)}, u32[]{:S(2)}, u32[]{:S(2)}) collective-permute-start(bf16[128,2048]{1,0:T(8,128)(2,1)S(1)} %get-tuple-element.123), channel_id=1, source_target_pairs={{1,0},{2,1},{3,2},{5,4},{6,5},{7,6},{9,8},{10,9},{11,10},{13,12},{... | collective-permute-start | bytes 1572872 | tf_op jit(solution)/shard_map/sink_r1_0/ppermute | solution.py:78
  184.6 35.9 %collective-permute-start.8 = (bf16[128,2048]{1,0:T(8,128)(2,1)S(1)}, bf16[128,2048]{1,0:T(8,128)(2,1)S(1)}, u32[]{:S(2)}, u32[]{:S(2)}) collective-permute-start(bf16[128,2048]{1,0:T(8,128)(2,1)S(1)} %get-tuple-element.122), channel_id=1, source_target_pairs={{0,1},{1,2},{2,3},{4,5},{5,6},{6,7},{8,9},{9,10},{10,11},{12,13},{... | collective-permute-start | bytes 1572872 | tf_op jit(solution)/shard_map/sink_r1_0/ppermute | solution.py:77
  244.1 49.7 %collective-permute-start.16 = (bf16[128,4096]{1,0:T(8,128)(2,1)S(1)}, bf16[128,4096]{1,0:T(8,128)(2,1)}, u32[]{:S(2)}, u32[]{:S(2)}) collective-permute-start(bf16[128,4096]{1,0:T(8,128)(2,1)S(1)} %get-tuple-element.143), channel_id=1, source_target_pairs={{1,2},{2,3},{5,6},{6,7},{9,10},{10,11},{13,14},{14,15},{17,18},{18... | collective-permute-start | bytes 3145736 | tf_op jit(solution)/shard_map/spread_text/ppermute | solution.py:61
  301.9 68.8 %collective-permute-start.43 = (bf16[256,2048]{1,0:T(8,128)(2,1)}, bf16[256,2048]{1,0:T(8,128)(2,1)}, u32[]{:S(2)}, u32[]{:S(2)}) collective-permute-start(bf16[256,2048]{1,0:T(8,128)(2,1)} %broadcast_add_fusion), channel_id=1, source_target_pairs={{1,0},{2,1},{3,2},{5,4},{6,5},{7,6},{9,8},{10,9},{11,10},{13,12},{... | collective-permute-start | bytes 3145736 | tf_op jit(solution)/shard_map/spread_og/ppermute | solution.py:62
  303.1 65.1 %collective-permute-start.42 = (bf16[256,2048]{1,0:T(8,128)(2,1)}, bf16[256,2048]{1,0:T(8,128)(2,1)}, u32[]{:S(2)}, u32[]{:S(2)}) collective-permute-start(bf16[256,2048]{1,0:T(8,128)(2,1)} %broadcast_add_fusion), channel_id=1, source_target_pairs={{0,1},{1,2},{2,3},{4,5},{5,6},{6,7},{8,9},{9,10},{10,11},{12,13},{... | collective-permute-start | bytes 3145736 | tf_op jit(solution)/shard_map/spread_og/ppermute | solution.py:61
  352.3 44.5 %collective-permute-start.24 = (bf16[128,2048]{1,0:T(8,128)(2,1)}, bf16[128,2048]{1,0:T(8,128)(2,1)}, u32[]{:S(2)}, u32[]{:S(2)}) collective-permute-start(bf16[128,2048]{1,0:T(8,128)(2,1)} %get-tuple-element.112), channel_id=1, source_target_pairs={{0,1},{4,5},{8,9},{12,13},{16,17},{20,21},{24,25},{28,29}} | collective-permute-start | bytes 1572872 | tf_op jit(solution)/shard_map/sink_r2_0/ppermute | solution.py:77
  432.6 45.3 %collective-permute-start.64 = (bf16[256,2048]{1,0:T(8,128)(2,1)}, bf16[256,2048]{1,0:T(8,128)(2,1)S(1)}, u32[]{:S(2)}, u32[]{:S(2)}) collective-permute-start(bf16[256,2048]{1,0:T(8,128)(2,1)} %collective-permute-done.45), channel_id=1, source_target_pairs={{1,0},{5,4},{9,8},{13,12},{17,16},{21,20},{25,24},{29,28}} | collective-permute-start | bytes 3145736 | tf_op jit(solution)/shard_map/spread_og/ppermute | solution.py:62
  441.4 49.4 %collective-permute-start.65 = (bf16[256,2048]{1,0:T(8,128)(2,1)}, bf16[256,2048]{1,0:T(8,128)(2,1)S(1)}, u32[]{:S(2)}, u32[]{:S(2)}) collective-permute-start(bf16[256,2048]{1,0:T(8,128)(2,1)} %collective-permute-done.44), channel_id=1, source_target_pairs={{2,3},{6,7},{10,11},{14,15},{18,19},{22,23},{26,27},{30,31}} | collective-permute-start | bytes 3145736 | tf_op jit(solution)/shard_map/spread_og/ppermute | solution.py:61
  592.8 410.4 %reduce-scatter.8.cloned.1.call-start = ((), (), s32[]{:S(2)}) async-start(), calls=%async_computation.14 | async-start | bytes 9437184 | tf_op jit(solution)/shard_map/reduce_scatter | solution.py:168
  647.3 447.9 %reduce-scatter.14.cloned.1.call-start = ((), (), s32[]{:S(2)}) async-start(), calls=%async_computation.17 | async-start | bytes 2359296 | tf_op jit(solution)/shard_map/reduce_scatter | solution.py:165
  722.1 75.5 %collective-permute-start.80 = (bf16[256,2048]{1,0:T(8,128)(2,1)}, bf16[256,2048]{1,0:T(8,128)(2,1)}, u32[]{:S(2)}, u32[]{:S(2)}) collective-permute-start(bf16[256,2048]{1,0:T(8,128)(2,1)} %fusion.316), channel_id=1, source_target_pairs={{3,2},{7,6},{11,10},{15,14},{19,18},{23,22},{27,26},{31,30}} | collective-permute-start | bytes 3145736 | tf_op jit(solution)/shard_map/sink_out/ppermute | solution.py:78
  725.0 72.7 %collective-permute-start.76 = (bf16[256,2048]{1,0:T(8,128)(2,1)}, bf16[256,2048]{1,0:T(8,128)(2,1)}, u32[]{:S(2)}, u32[]{:S(2)}) collective-permute-start(bf16[256,2048]{1,0:T(8,128)(2,1)} %fusion.317), channel_id=1, source_target_pairs={{0,1},{4,5},{8,9},{12,13},{16,17},{20,21},{24,25},{28,29}} | collective-permute-start | bytes 3145736 | tf_op jit(solution)/shard_map/sink_out/ppermute | solution.py:77
  787.7 41.8 %collective-permute-start.106 = (bf16[128,2048]{1,0:T(8,128)(2,1)}, bf16[128,2048]{1,0:T(8,128)(2,1)}, u32[]{:S(2)}, u32[]{:S(2)}) collective-permute-start(bf16[128,2048]{1,0:T(8,128)(2,1)} %get-tuple-element.80), channel_id=1, source_target_pairs={{0,1},{4,5},{8,9},{12,13},{16,17},{20,21},{24,25},{28,29}} | collective-permute-start | bytes 1572872 | tf_op jit(solution)/shard_map/sink_d2_0/ppermute | solution.py:77
  790.4 39.2 %collective-permute-start.109 = (bf16[128,2048]{1,0:T(8,128)(2,1)}, bf16[128,2048]{1,0:T(8,128)(2,1)}, u32[]{:S(2)}, u32[]{:S(2)}) collective-permute-start(bf16[128,2048]{1,0:T(8,128)(2,1)} %get-tuple-element.81), channel_id=1, source_target_pairs={{3,2},{7,6},{11,10},{15,14},{19,18},{23,22},{27,26},{31,30}} | collective-permute-start | bytes 1572872 | tf_op jit(solution)/shard_map/sink_d2_0/ppermute | solution.py:78
  869.4 227.6 %reduce-scatter.12.cloned.1.call-start = ((), (), s32[]{:S(2)}) async-start(), calls=%async_computation.16 | async-start | bytes 2359296 | tf_op jit(solution)/shard_map/reduce_scatter | solution.py:168
  928.9 202.1 %reduce-scatter.20.cloned.1.call-start = ((), (), s32[]{:S(2)}) async-start(), calls=%async_computation.20 | async-start | bytes 2359296 | tf_op jit(solution)/shard_map/reduce_scatter | solution.py:168
  966.8 198.6 %reduce-scatter.16.cloned.1.call-start = ((), (), s32[]{:S(2)}) async-start(), calls=%async_computation.18 | async-start | bytes 9437184 | tf_op jit(solution)/shard_map/reduce_scatter | solution.py:165
  967.5 254.9 %reduce-scatter.18.cloned.1.call-start = ((), (), s32[]{:S(2)}) async-start(), calls=%async_computation.19 | async-start | bytes 7077888 | tf_op jit(solution)/shard_map/reduce_scatter | solution.py:165
  984.8 37.0 %collective-permute-start.120 = (bf16[128,4096]{1,0:T(8,128)(2,1)}, bf16[128,4096]{1,0:T(8,128)(2,1)}, u32[]{:S(2)}, u32[]{:S(2)}) collective-permute-start(bf16[128,4096]{1,0:T(8,128)(2,1)} %get-tuple-element.72), channel_id=1, source_target_pairs={{0,1},{4,5},{8,9},{12,13},{16,17},{20,21},{24,25},{28,29}} | collective-permute-start | bytes 3145736 | tf_op jit(solution)/shard_map/sink_text/ppermute | solution.py:77
  994.0 89.5 %collective-permute-start.92 = (bf16[256,2048]{1,0:T(8,128)(2,1)}, bf16[256,2048]{1,0:T(8,128)(2,1)}, u32[]{:S(2)}, u32[]{:S(2)}) collective-permute-start(bf16[256,2048]{1,0:T(8,128)(2,1)} %add_convert_fusion.1), channel_id=1, source_target_pairs={{0,1},{1,2},{2,3},{4,5},{5,6},{6,7},{8,9},{9,10},{10,11},{12,13},{... | collective-permute-start | bytes 3145736 | tf_op jit(solution)/shard_map/sink_out/ppermute | solution.py:77
  1036.3 48.3 %collective-permute-start.93 = (bf16[256,2048]{1,0:T(8,128)(2,1)}, bf16[256,2048]{1,0:T(8,128)(2,1)}, u32[]{:S(2)}, u32[]{:S(2)}) collective-permute-start(bf16[256,2048]{1,0:T(8,128)(2,1)} %add_convert_fusion), channel_id=1, source_target_pairs={{1,0},{2,1},{3,2},{5,4},{6,5},{7,6},{9,8},{10,9},{11,10},{13,12},{... | collective-permute-start | bytes 3145736 | tf_op jit(solution)/shard_map/sink_out/ppermute | solution.py:78
  1124.0 38.0 %collective-permute-start.130 = (bf16[128,4096]{1,0:T(8,128)(2,1)}, bf16[128,4096]{1,0:T(8,128)(2,1)}, u32[]{:S(2)}, u32[]{:S(2)}) collective-permute-start(bf16[128,4096]{1,0:T(8,128)(2,1)} %get-tuple-element.61), channel_id=1, source_target_pairs={{0,1},{1,2},{2,3},{4,5},{5,6},{6,7},{8,9},{9,10},{10,11},{12,13},{... | collective-permute-start | bytes 3145736 | tf_op jit(solution)/shard_map/sink_text/ppermute | solution.py:77
  (294 other events, 6441.6 us)
Sparse Core Ops, SparseCore 0:
  11.7 48.1 all-gather.7
  62.3 28.0 all-gather.9
  92.9 27.7 all-gather.13
  122.4 54.2 all-gather.11
  178.4 28.0 all-gather.15
  208.3 54.2 all-gather.17
  264.5 55.8 all-gather.19
  592.9 71.3 reduce-scatter.9
  667.8 71.2 reduce-scatter.7
  869.5 48.8 reduce-scatter.13
  929.0 51.7 reduce-scatter.11
  983.9 41.1 reduce-scatter.19
  1028.5 71.5 reduce-scatter.15
  1103.3 61.7 reduce-scatter.17

commit v6 on v5

--- a/solution.py
+++ b/solution.py
@@ -119,7 +119,7 @@
     grad_soft = jnp.einsum("iphe,iqhe->ihpq", grad_mix, values_in, preferred_element_type=F32)
     grad_values = jnp.einsum("ihpq,iphe->iqhe", soft.astype(BF), grad_mix, preferred_element_type=F32)
     row_dot = jnp.sum(soft * grad_soft, axis=-1, keepdims=True)
-    grad_scores = (soft * (grad_soft - row_dot) * score_scale).astype(BF)
+    grad_scores = whole((soft * (grad_soft - row_dot) * score_scale).astype(BF))
     grad_queries = jnp.einsum("ihpq,iqhe->iphe", grad_scores, keys_in, preferred_element_type=F32)
     grad_keys = jnp.einsum("ihpq,iphe->iqhe", grad_scores, queries, preferred_element_type=F32)
     return grad_queries.astype(BF), grad_keys, grad_values

time: 1240 us -> 1230 us (level)
  matrix products: 290 us -> 263 us
  starting transfers between devices: 329 us -> 346 us
    dot_general x3, matrix products: 31.4 us -> 4.21 us  [attend_back(): jnp.einsum('ihpq,iphe->iqhe', grad_scores, queries, preferred_element_typ...]
    dot_general x3, matrix products: 27.3 us -> 4.61 us  [attend_back(): jnp.einsum('ihpq,iqhe->iphe', grad_scores, keys_in, preferred_element_typ...]
    sub x0 -> x3, matrix products: none -> 22.7 us  [attend_back(): grad_scores = whole((soft * (grad_soft - row_dot) * score_scale).astype(BF))]
    ppermute x33, waiting for transfers between devices: 189 us -> 171 us  [spread(): lax.ppermute(other, 'narrow', [(k, k - 1) for k in range(1, n - step + 1)])]
    ppermute x33, starting transfers between devices: 152 us -> 169 us  [sink(): lax.ppermute(one.astype(BF), 'narrow', [(k, k + 1) for k in range(step)])]
  transfers between devices with their start and end apart: 146 -> 146, of which waited for: 44 -> 40; matrix products, arithmetic and copies ran while one was open for 38% -> 36% of each run, Pallas kernels for 0% -> 0%
where the time goes in v6:
time: 1230 us; the launch traced here: 1220 us
  starting transfers between devices  346 us (28%)
  waiting for transfers between devices  289 us (23%)
  matrix products  263 us (21%)
  other arithmetic  156 us (13%)
  local copies, waits for them, and re-layouts  86.9 us (7%)
  blocking collectives  46.5 us (4%)
  between operations  33.2 us (3%)
    ppermute x33, waiting for transfers between devices, spread(): lax.ppermute(other, 'narrow', [(k, k - 1) for k in range(1, n - step + 1)])  171 us
    ppermute x33, starting transfers between devices, sink(): lax.ppermute(one.astype(BF), 'narrow', [(k, k + 1) for k in range(step)])  169 us
    ppermute x33, starting transfers between devices, spread(): lax.ppermute(one, 'narrow', [(k, k + 1) for k in range(step - 1, n - 1)])  90.7 us
    dot_general x12, matrix products, right_inner(): lax.dot_general(left_side, right_side, (((left_side.ndim - 1,), (1,)), ((...  74.4 us
    ppermute x33, waiting for transfers between devices, sink(): lax.ppermute(one.astype(BF), 'narrow', [(k, k + 1) for k in range(step)])  73.1 us
    dot_general x12, matrix products, product(): lax.dot_general(left_side, right_side, (((left_side.ndim - 1,), (0,)), ((...  71.5 us
    dot_general x7, matrix products, left_inner(): lax.dot_general(left_side, right_side, ((rows, rows), ((), ())), preferre...  53.7 us
    psum x1, blocking collectives, body(): lax.psum(jnp.stack([norm_sums(grad_n1, xhat1), sum(sums2), sum(sums3)]),...  46.5 us
  transfers between devices with their start and end apart: 146, of which 40 were waited for; matrix products, arithmetic and copies ran while one was open for 36% of the time, Pallas kernels for 0%

profile of v6, /device:TPU:0, one launch (start us, length us, event | category | flops | bytes accessed | tf_op | source)
XLA Modules:
  0.0 1219.4 jit_solution(14398081103135194425)
XLA Ops:
  28.3 21.2 %collective-permute-done.1 = bf16[256,2048]{1,0:T(8,128)(2,1)S(1)} collective-permute-done((bf16[256,2048]{1,0:T(8,128)(2,1)S(1)}, bf16[256,2048]{1,0:T(8,128)(2,1)S(1)}, u32[]{:S(2)}, u32[]{:S(2)}) %collective-permute-start.1) | collective-permute-done | bytes 1048608 | tf_op jit(solution)/shard_map/spread_n1/ppermute | solution.py:62
  53.1 22.8 %collective-permute-done.2 = bf16[256,2048]{1,0:T(8,128)(2,1)} collective-permute-done((bf16[256,2048]{1,0:T(8,128)(2,1)S(1)}, bf16[256,2048]{1,0:T(8,128)(2,1)}, u32[]{:S(2)}, u32[]{:S(2)}) %collective-permute-start.2) | collective-permute-done | bytes 1048608 | tf_op jit(solution)/shard_map/spread_n1/ppermute | solution.py:62
  80.2 21.5 %collective-permute-done.3 = bf16[256,2048]{1,0:T(8,128)(2,1)} collective-permute-done((bf16[256,2048]{1,0:T(8,128)(2,1)}, bf16[256,2048]{1,0:T(8,128)(2,1)}, u32[]{:S(2)}, u32[]{:S(2)}) %collective-permute-start.3) | collective-permute-done | bytes 1048608 | tf_op jit(solution)/shard_map/spread_n1/ppermute | solution.py:62
  108.5 9.4 fusion.91
  198.0 10.7 collective-permute-start.12
  210.0 10.4 collective-permute-done.11
  245.7 8.5 collective-permute-done.19
  256.2 9.2 collective-permute-done.37
  278.6 9.3 collective-permute-done.38
  324.5 9.1 convolution_convert_fusion.7
  348.7 14.2 %collective-permute-start.24 = (bf16[128,2048]{1,0:T(8,128)(2,1)}, bf16[128,2048]{1,0:T(8,128)(2,1)}, u32[]{:S(2)}, u32[]{:S(2)}) collective-permute-start(bf16[128,2048]{1,0:T(8,128)(2,1)} %get-tuple-element.112), channel_id=1, source_target_pairs={{0,1},{4,5},{8,9},{12,13},{16,17},{20,21},{24,25},{28,29}} | collective-permute-start | bytes 1572872 | tf_op jit(solution)/shard_map/sink_r2_0/ppermute | solution.py:77
  389.9 17.2 %collective-permute-start.25 = (bf16[128,2048]{1,0:T(8,128)(2,1)S(1)}, bf16[128,2048]{1,0:T(8,128)(2,1)S(1)}, u32[]{:S(2)}, u32[]{:S(2)}) collective-permute-start(bf16[128,2048]{1,0:T(8,128)(2,1)S(1)} %get-tuple-element.110), channel_id=1, source_target_pairs={{0,1},{1,2},{4,5},{5,6},{8,9},{9,10},{12,13},{13,14},{16,17},{17,1... | collective-permute-start | bytes 1572872 | tf_op jit(solution)/shard_map/sink_r2_0/ppermute | solution.py:77
  447.8 8.8 collective-permute-start.48
  458.2 8.8 collective-permute-done.48
  533.0 11.9 multiply_convert_fusion.3
  545.0 10.5 fusion.36
  555.6 11.4 multiply_convert_fusion.4
  567.0 8.6 fusion.29
  577.0 11.8 convolution_bitcast_fusion
  588.9 8.7 fusion.114
  600.0 9.7 fusion.117
  630.3 11.4 convolution_bitcast_fusion.1
  752.6 8.3 fusion.223
  823.2 10.9 collective-permute-done.77
  871.3 9.0 collective-permute-start.84
  886.9 10.0 collective-permute-done.87
  945.8 12.0 collective-permute-done.118
  967.7 9.7 convolution_convert_fusion
  1051.6 11.8 fusion.94
  1063.5 8.9 bitcast_convert_fusion
  1088.0 17.9 %collective-permute-done.124 = bf16[256,2048]{1,0:T(8,128)(2,1)S(1)} collective-permute-done((bf16[256,2048]{1,0:T(8,128)(2,1)S(1)}, bf16[256,2048]{1,0:T(8,128)(2,1)S(1)}, u32[]{:S(2)}, u32[]{:S(2)}) %collective-permute-start.124) | collective-permute-done | bytes 1048608 | tf_op jit(solution)/shard_map/sink_d1/ppermute | solution.py:77
  1159.8 46.5 %psum.7 = f32[3,2,2048]{2,0,1:T(4,128)S(1)} all-reduce(f32[3,2,2048]{2,0,1:T(4,128)S(1)} %pad_maximum_fusion.16), channel_id=1, replica_groups=mesh['wide'=8,'narrow'=4] {'wide','narrow'}, use_global_device_ids=true, to_apply=%region_44.45 | all-reduce | flops 12288 | bytes 98304 | tf_op jit(solution)/shard_map/psum | solution.py:299
  (930 shorter events, 776.2 us)
Async XLA Ops:
  7.2 101.2 %all-gather.8.cloned.1.call-start = ((), (), s32[]{:S(2)}) async-start(), calls=%async_computation.7 | async-start | bytes 7077888 | tf_op jit(solution)/shard_map/all_gather | solution.py:157
  11.6 115.7 %all-gather.10.cloned.1.call-start = ((), (), s32[]{:S(2)}) async-start(), calls=%async_computation.8 | async-start | bytes 2359296 | tf_op jit(solution)/shard_map/all_gather | solution.py:162
  12.4 296.9 %all-gather.14.cloned.1.call-start = ((), (), s32[]{:S(2)}) async-start(), calls=%async_computation.10 | async-start | bytes 2359296 | tf_op jit(solution)/shard_map/all_gather | solution.py:157
  14.4 310.1 %all-gather.12.cloned.1.call-start = ((), (), s32[]{:S(2)}) async-start(), calls=%async_computation.9 | async-start | bytes 9437184 | tf_op jit(solution)/shard_map/all_gather | solution.py:157
  17.0 326.5 %all-gather.16.cloned.1.call-start = ((), (), s32[]{:S(2)}) async-start(), calls=%async_computation.11 | async-start | bytes 2359296 | tf_op jit(solution)/shard_map/all_gather | solution.py:162
  18.8 514.2 %all-gather.18.cloned.1.call-start = ((), (), s32[]{:S(2)}) async-start(), calls=%async_computation.12 | async-start | bytes 9437184 | tf_op jit(solution)/shard_map/all_gather | solution.py:157
  20.0 524.9 %all-gather.20.cloned.1.call-start = ((), (), s32[]{:S(2)}) async-start(), calls=%async_computation.13 | async-start | bytes 9437184 | tf_op jit(solution)/shard_map/all_gather | solution.py:162
  106.6 61.4 %collective-permute-start.13 = (bf16[128,4096]{1,0:T(8,128)(2,1)}, bf16[128,4096]{1,0:T(8,128)(2,1)}, u32[]{:S(2)}, u32[]{:S(2)}) collective-permute-start(bf16[128,4096]{1,0:T(8,128)(2,1)} %broadcast_add_fusion.3), channel_id=1, source_target_pairs={{1,0},{2,1},{3,2},{5,4},{6,5},{7,6},{9,8},{10,9},{11,10},{13,12},{... | collective-permute-start | bytes 3145736 | tf_op jit(solution)/shard_map/spread_text/ppermute | solution.py:62
  147.4 853.1 %reduce-scatter.10.cloned.1.call-start = ((), (), s32[]{:S(2)}) async-start(), calls=%async_computation.15 | async-start | bytes 9437184 | tf_op jit(solution)/shard_map/reduce_scatter | solution.py:165
  172.0 36.7 %collective-permute-start.32 = (bf16[128,2048]{1,0:T(8,128)(2,1)S(1)}, bf16[128,2048]{1,0:T(8,128)(2,1)S(1)}, u32[]{:S(2)}, u32[]{:S(2)}) collective-permute-start(bf16[128,2048]{1,0:T(8,128)(2,1)S(1)} %get-tuple-element.128), channel_id=1, source_target_pairs={{0,1},{1,2},{2,3},{4,5},{5,6},{6,7},{8,9},{9,10},{10,11},{12,13},{... | collective-permute-start | bytes 1572872 | tf_op jit(solution)/shard_map/sink_r1_1/ppermute | solution.py:77
  183.3 37.2 %collective-permute-start.11 = (bf16[128,2048]{1,0:T(8,128)(2,1)S(1)}, bf16[128,2048]{1,0:T(8,128)(2,1)S(1)}, u32[]{:S(2)}, u32[]{:S(2)}) collective-permute-start(bf16[128,2048]{1,0:T(8,128)(2,1)S(1)} %get-tuple-element.123), channel_id=1, source_target_pairs={{1,0},{2,1},{3,2},{5,4},{6,5},{7,6},{9,8},{10,9},{11,10},{13,12},{... | collective-permute-start | bytes 1572872 | tf_op jit(solution)/shard_map/sink_r1_0/ppermute | solution.py:78
  184.6 35.9 %collective-permute-start.8 = (bf16[128,2048]{1,0:T(8,128)(2,1)S(1)}, bf16[128,2048]{1,0:T(8,128)(2,1)S(1)}, u32[]{:S(2)}, u32[]{:S(2)}) collective-permute-start(bf16[128,2048]{1,0:T(8,128)(2,1)S(1)} %get-tuple-element.122), channel_id=1, source_target_pairs={{0,1},{1,2},{2,3},{4,5},{5,6},{6,7},{8,9},{9,10},{10,11},{12,13},{... | collective-permute-start | bytes 1572872 | tf_op jit(solution)/shard_map/sink_r1_0/ppermute | solution.py:77
  229.9 35.5 %collective-permute-start.37 = (bf16[128,2048]{1,0:T(8,128)(2,1)S(1)}, bf16[128,2048]{1,0:T(8,128)(2,1)S(1)}, u32[]{:S(2)}, u32[]{:S(2)}) collective-permute-start(bf16[128,2048]{1,0:T(8,128)(2,1)S(1)} %get-tuple-element.158), channel_id=1, source_target_pairs={{1,0},{2,1},{3,2},{5,4},{6,5},{7,6},{9,8},{10,9},{11,10},{13,12},{... | collective-permute-start | bytes 1572872 | tf_op jit(solution)/shard_map/spread_n2_1/ppermute | solution.py:62
  244.0 48.9 %collective-permute-start.16 = (bf16[128,4096]{1,0:T(8,128)(2,1)S(1)}, bf16[128,4096]{1,0:T(8,128)(2,1)}, u32[]{:S(2)}, u32[]{:S(2)}) collective-permute-start(bf16[128,4096]{1,0:T(8,128)(2,1)S(1)} %get-tuple-element.143), channel_id=1, source_target_pairs={{1,2},{2,3},{5,6},{6,7},{9,10},{10,11},{13,14},{14,15},{17,18},{18... | collective-permute-start | bytes 3145736 | tf_op jit(solution)/shard_map/spread_text/ppermute | solution.py:61
  300.2 66.6 %collective-permute-start.43 = (bf16[256,2048]{1,0:T(8,128)(2,1)}, bf16[256,2048]{1,0:T(8,128)(2,1)}, u32[]{:S(2)}, u32[]{:S(2)}) collective-permute-start(bf16[256,2048]{1,0:T(8,128)(2,1)} %broadcast_add_fusion), channel_id=1, source_target_pairs={{1,0},{2,1},{3,2},{5,4},{6,5},{7,6},{9,8},{10,9},{11,10},{13,12},{... | collective-permute-start | bytes 3145736 | tf_op jit(solution)/shard_map/spread_og/ppermute | solution.py:62
  301.5 62.8 %collective-permute-start.42 = (bf16[256,2048]{1,0:T(8,128)(2,1)}, bf16[256,2048]{1,0:T(8,128)(2,1)}, u32[]{:S(2)}, u32[]{:S(2)}) collective-permute-start(bf16[256,2048]{1,0:T(8,128)(2,1)} %broadcast_add_fusion), channel_id=1, source_target_pairs={{0,1},{1,2},{2,3},{4,5},{5,6},{6,7},{8,9},{9,10},{10,11},{12,13},{... | collective-permute-start | bytes 3145736 | tf_op jit(solution)/shard_map/spread_og/ppermute | solution.py:61
  348.7 39.7 %collective-permute-start.24 = (bf16[128,2048]{1,0:T(8,128)(2,1)}, bf16[128,2048]{1,0:T(8,128)(2,1)}, u32[]{:S(2)}, u32[]{:S(2)}) collective-permute-start(bf16[128,2048]{1,0:T(8,128)(2,1)} %get-tuple-element.112), channel_id=1, source_target_pairs={{0,1},{4,5},{8,9},{12,13},{16,17},{20,21},{24,25},{28,29}} | collective-permute-start | bytes 1572872 | tf_op jit(solution)/shard_map/sink_r2_0/ppermute | solution.py:77
  426.4 53.9 %collective-permute-start.64 = (bf16[256,2048]{1,0:T(8,128)(2,1)}, bf16[256,2048]{1,0:T(8,128)(2,1)S(1)}, u32[]{:S(2)}, u32[]{:S(2)}) collective-permute-start(bf16[256,2048]{1,0:T(8,128)(2,1)} %collective-permute-done.45), channel_id=1, source_target_pairs={{1,0},{5,4},{9,8},{13,12},{17,16},{21,20},{25,24},{29,28}} | collective-permute-start | bytes 3145736 | tf_op jit(solution)/shard_map/spread_og/ppermute | solution.py:62
  437.0 56.1 %collective-permute-start.65 = (bf16[256,2048]{1,0:T(8,128)(2,1)}, bf16[256,2048]{1,0:T(8,128)(2,1)S(1)}, u32[]{:S(2)}, u32[]{:S(2)}) collective-permute-start(bf16[256,2048]{1,0:T(8,128)(2,1)} %collective-permute-done.44), channel_id=1, source_target_pairs={{2,3},{6,7},{10,11},{14,15},{18,19},{22,23},{26,27},{30,31}} | collective-permute-start | bytes 3145736 | tf_op jit(solution)/shard_map/spread_og/ppermute | solution.py:61
  588.8 414.5 %reduce-scatter.8.cloned.1.call-start = ((), (), s32[]{:S(2)}) async-start(), calls=%async_computation.14 | async-start | bytes 9437184 | tf_op jit(solution)/shard_map/reduce_scatter | solution.py:168
  702.4 381.8 %reduce-scatter.14.cloned.1.call-start = ((), (), s32[]{:S(2)}) async-start(), calls=%async_computation.17 | async-start | bytes 2359296 | tf_op jit(solution)/shard_map/reduce_scatter | solution.py:165
  721.3 83.9 %collective-permute-start.80 = (bf16[256,2048]{1,0:T(8,128)(2,1)}, bf16[256,2048]{1,0:T(8,128)(2,1)}, u32[]{:S(2)}, u32[]{:S(2)}) collective-permute-start(bf16[256,2048]{1,0:T(8,128)(2,1)} %fusion.308), channel_id=1, source_target_pairs={{3,2},{7,6},{11,10},{15,14},{19,18},{23,22},{27,26},{31,30}} | collective-permute-start | bytes 3145736 | tf_op jit(solution)/shard_map/sink_out/ppermute | solution.py:78
  724.2 81.1 %collective-permute-start.76 = (bf16[256,2048]{1,0:T(8,128)(2,1)}, bf16[256,2048]{1,0:T(8,128)(2,1)}, u32[]{:S(2)}, u32[]{:S(2)}) collective-permute-start(bf16[256,2048]{1,0:T(8,128)(2,1)} %fusion.309), channel_id=1, source_target_pairs={{0,1},{4,5},{8,9},{12,13},{16,17},{20,21},{24,25},{28,29}} | collective-permute-start | bytes 3145736 | tf_op jit(solution)/shard_map/sink_out/ppermute | solution.py:77
  794.0 48.9 %collective-permute-start.106 = (bf16[128,2048]{1,0:T(8,128)(2,1)}, bf16[128,2048]{1,0:T(8,128)(2,1)}, u32[]{:S(2)}, u32[]{:S(2)}) collective-permute-start(bf16[128,2048]{1,0:T(8,128)(2,1)} %get-tuple-element.80), channel_id=1, source_target_pairs={{0,1},{4,5},{8,9},{12,13},{16,17},{20,21},{24,25},{28,29}} | collective-permute-start | bytes 1572872 | tf_op jit(solution)/shard_map/sink_d2_0/ppermute | solution.py:77
  798.0 45.0 %collective-permute-start.109 = (bf16[128,2048]{1,0:T(8,128)(2,1)}, bf16[128,2048]{1,0:T(8,128)(2,1)}, u32[]{:S(2)}, u32[]{:S(2)}) collective-permute-start(bf16[128,2048]{1,0:T(8,128)(2,1)} %get-tuple-element.81), channel_id=1, source_target_pairs={{3,2},{7,6},{11,10},{15,14},{19,18},{23,22},{27,26},{31,30}} | collective-permute-start | bytes 1572872 | tf_op jit(solution)/shard_map/sink_d2_0/ppermute | solution.py:78
  869.1 217.0 %reduce-scatter.12.cloned.1.call-start = ((), (), s32[]{:S(2)}) async-start(), calls=%async_computation.16 | async-start | bytes 2359296 | tf_op jit(solution)/shard_map/reduce_scatter | solution.py:168
  934.8 193.3 %reduce-scatter.20.cloned.1.call-start = ((), (), s32[]{:S(2)}) async-start(), calls=%async_computation.20 | async-start | bytes 2359296 | tf_op jit(solution)/shard_map/reduce_scatter | solution.py:168
  966.5 177.6 %reduce-scatter.16.cloned.1.call-start = ((), (), s32[]{:S(2)}) async-start(), calls=%async_computation.18 | async-start | bytes 9437184 | tf_op jit(solution)/shard_map/reduce_scatter | solution.py:165
  967.2 243.1 %reduce-scatter.18.cloned.1.call-start = ((), (), s32[]{:S(2)}) async-start(), calls=%async_computation.19 | async-start | bytes 7077888 | tf_op jit(solution)/shard_map/reduce_scatter | solution.py:165
  984.4 38.0 %collective-permute-start.120 = (bf16[128,4096]{1,0:T(8,128)(2,1)}, bf16[128,4096]{1,0:T(8,128)(2,1)}, u32[]{:S(2)}, u32[]{:S(2)}) collective-permute-start(bf16[128,4096]{1,0:T(8,128)(2,1)} %get-tuple-element.72), channel_id=1, source_target_pairs={{0,1},{4,5},{8,9},{12,13},{16,17},{20,21},{24,25},{28,29}} | collective-permute-start | bytes 3145736 | tf_op jit(solution)/shard_map/sink_text/ppermute | solution.py:77
  993.6 78.8 %collective-permute-start.92 = (bf16[256,2048]{1,0:T(8,128)(2,1)}, bf16[256,2048]{1,0:T(8,128)(2,1)}, u32[]{:S(2)}, u32[]{:S(2)}) collective-permute-start(bf16[256,2048]{1,0:T(8,128)(2,1)} %add_convert_fusion.1), channel_id=1, source_target_pairs={{0,1},{1,2},{2,3},{4,5},{5,6},{6,7},{8,9},{9,10},{10,11},{12,13},{... | collective-permute-start | bytes 3145736 | tf_op jit(solution)/shard_map/sink_out/ppermute | solution.py:77
  1032.9 40.7 %collective-permute-start.93 = (bf16[256,2048]{1,0:T(8,128)(2,1)}, bf16[256,2048]{1,0:T(8,128)(2,1)}, u32[]{:S(2)}, u32[]{:S(2)}) collective-permute-start(bf16[256,2048]{1,0:T(8,128)(2,1)} %add_convert_fusion), channel_id=1, source_target_pairs={{1,0},{2,1},{3,2},{5,4},{6,5},{7,6},{9,8},{10,9},{11,10},{13,12},{... | collective-permute-start | bytes 3145736 | tf_op jit(solution)/shard_map/sink_out/ppermute | solution.py:78
  (306 other events, 6682.6 us)
Sparse Core Ops, SparseCore 0:
  11.7 48.1 all-gather.7
  62.3 28.0 all-gather.9
  92.9 27.7 all-gather.13
  122.4 54.2 all-gather.11
  178.4 28.0 all-gather.15
  208.3 54.2 all-gather.17
  264.5 55.8 all-gather.19
  588.9 71.7 reduce-scatter.9
  702.6 72.5 reduce-scatter.7
  869.2 41.1 reduce-scatter.13
  935.0 45.4 reduce-scatter.11
  983.6 41.1 reduce-scatter.19
  1028.2 71.5 reduce-scatter.15
  1103.0 61.7 reduce-scatter.17

commit v7 on v6

--- a/solution.py
+++ b/solution.py
@@ -117,7 +117,7 @@
 def attend_back(queries, keys_in, values_in, allowed, log_total, grad_mix, score_scale):
     soft = jnp.exp(score_block(queries, keys_in, allowed, score_scale) - log_total)
     grad_soft = jnp.einsum("iphe,iqhe->ihpq", grad_mix, values_in, preferred_element_type=F32)
-    grad_values = jnp.einsum("ihpq,iphe->iqhe", soft.astype(BF), grad_mix, preferred_element_type=F32)
+    grad_values = jnp.einsum("ihpq,iphe->iqhe", whole(soft.astype(BF)), grad_mix, preferred_element_type=F32)
     row_dot = jnp.sum(soft * grad_soft, axis=-1, keepdims=True)
     grad_scores = whole((soft * (grad_soft - row_dot) * score_scale).astype(BF))
     grad_queries = jnp.einsum("ihpq,iqhe->iphe", grad_scores, keys_in, preferred_element_type=F32)

time: 1230 us -> 1230 us (level)
  waiting for transfers between devices: 289 us -> 309 us
  matrix products: 263 us -> 250 us
    ppermute x33, waiting for transfers between devices: 5.37 us -> 21.1 us  [spread(): lax.ppermute(one, 'narrow', [(k, k + 1) for k in range(step - 1, n - 1)])]
  transfers between devices with their start and end apart: 146 -> 146, of which waited for: 40 -> 46; matrix products, arithmetic and copies ran while one was open for 36% -> 39% of each run, Pallas kernels for 0% -> 0%
where the time goes in v7:
time: 1230 us; the launch traced here: 1220 us
  starting transfers between devices  335 us (27%)
  waiting for transfers between devices  309 us (25%)
  matrix products  250 us (20%)
  other arithmetic  162 us (13%)
  local copies, waits for them, and re-layouts  86.3 us (7%)
  blocking collectives  40 us (3%)
  between operations  33.3 us (3%)
    ppermute x33, waiting for transfers between devices, spread(): lax.ppermute(other, 'narrow', [(k, k - 1) for k in range(1, n - step + 1)])  169 us
    ppermute x33, starting transfers between devices, sink(): lax.ppermute(one.astype(BF), 'narrow', [(k, k + 1) for k in range(step)])  158 us
    ppermute x33, starting transfers between devices, spread(): lax.ppermute(one, 'narrow', [(k, k + 1) for k in range(step - 1, n - 1)])  89.9 us
    ppermute x33, waiting for transfers between devices, sink(): lax.ppermute(one.astype(BF), 'narrow', [(k, k + 1) for k in range(step)])  81.6 us
    dot_general x12, matrix products, right_inner(): lax.dot_general(left_side, right_side, (((left_side.ndim - 1,), (1,)), ((...  72.9 us
    dot_general x12, matrix products, product(): lax.dot_general(left_side, right_side, (((left_side.ndim - 1,), (0,)), ((...  68.6 us
    dot_general x7, matrix products, left_inner(): lax.dot_general(left_side, right_side, ((rows, rows), ((), ())), preferre...  52.4 us
    ppermute x33, starting transfers between devices, spread(): lax.ppermute(other, 'narrow', [(k, k - 1) for k in range(1, n - step + 1)])  43.1 us
  transfers between devices with their start and end apart: 146, of which 46 were waited for; matrix products, arithmetic and copies ran while one was open for 39% of the time, Pallas kernels for 0%

profile of v7, /device:TPU:0, one launch (start us, length us, event | category | flops | bytes accessed | tf_op | source)
XLA Modules:
  0.0 1216.4 jit_solution(7606526087314520934)
XLA Ops:
  27.7 21.0 %collective-permute-done = bf16[256,2048]{1,0:T(8,128)(2,1)S(1)} collective-permute-done((bf16[256,2048]{1,0:T(8,128)(2,1)S(1)}, bf16[256,2048]{1,0:T(8,128)(2,1)S(1)}, u32[]{:S(2)}, u32[]{:S(2)}) %collective-permute-start) | collective-permute-done | bytes 1048608 | tf_op jit(solution)/shard_map/spread_n1/ppermute | solution.py:61
  57.3 22.7 %collective-permute-done.2 = bf16[256,2048]{1,0:T(8,128)(2,1)} collective-permute-done((bf16[256,2048]{1,0:T(8,128)(2,1)}, bf16[256,2048]{1,0:T(8,128)(2,1)}, u32[]{:S(2)}, u32[]{:S(2)}) %collective-permute-start.2) | collective-permute-done | bytes 1048608 | tf_op jit(solution)/shard_map/spread_n1/ppermute | solution.py:62
  85.6 19.8 %collective-permute-done.3 = bf16[256,2048]{1,0:T(8,128)(2,1)S(1)} collective-permute-done((bf16[256,2048]{1,0:T(8,128)(2,1)}, bf16[256,2048]{1,0:T(8,128)(2,1)S(1)}, u32[]{:S(2)}, u32[]{:S(2)}) %collective-permute-start.3) | collective-permute-done | bytes 1048608 | tf_op jit(solution)/shard_map/spread_n1/ppermute | solution.py:62
  110.0 10.7 fusion.91
  199.6 11.8 collective-permute-start.12
  212.8 9.2 collective-permute-done.35
  247.2 8.5 collective-permute-done.19
  257.6 9.2 collective-permute-done.37
  280.1 9.3 collective-permute-done.38
  303.1 9.1 collective-permute-start.42
  328.0 9.1 convolution_convert_fusion.7
  352.4 14.3 %collective-permute-start.24 = (bf16[128,2048]{1,0:T(8,128)(2,1)}, bf16[128,2048]{1,0:T(8,128)(2,1)}, u32[]{:S(2)}, u32[]{:S(2)}) collective-permute-start(bf16[128,2048]{1,0:T(8,128)(2,1)} %get-tuple-element.112), channel_id=1, source_target_pairs={{0,1},{4,5},{8,9},{12,13},{16,17},{20,21},{24,25},{28,29}} | collective-permute-start | bytes 1572872 | tf_op jit(solution)/shard_map/sink_r2_0/ppermute | solution.py:77
  396.5 15.2 %collective-permute-start.25 = (bf16[128,2048]{1,0:T(8,128)(2,1)S(1)}, bf16[128,2048]{1,0:T(8,128)(2,1)S(1)}, u32[]{:S(2)}, u32[]{:S(2)}) collective-permute-start(bf16[128,2048]{1,0:T(8,128)(2,1)S(1)} %get-tuple-element.110), channel_id=1, source_target_pairs={{0,1},{1,2},{4,5},{5,6},{8,9},{9,10},{12,13},{13,14},{16,17},{17,1... | collective-permute-start | bytes 1572872 | tf_op jit(solution)/shard_map/sink_r2_0/ppermute | solution.py:77
  462.8 8.4 collective-permute-done.48
  497.8 9.2 collective-permute-done.59
  537.7 11.3 multiply_convert_fusion.3
  557.3 11.2 convolution_bitcast_fusion.1
  574.3 10.4 fusion.36
  584.7 9.3 fusion.114
  596.7 11.4 fusion.29
  608.2 8.6 fusion.117
  637.4 11.2 convolution_bitcast_fusion
  668.1 8.9 fusion.123
  704.6 9.3 collective-permute-done.74
  721.1 9.6 collective-permute-done.75
  794.8 8.2 fusion.227
  832.8 10.7 collective-permute-done.77
  971.4 9.7 convolution_convert_fusion
  1051.3 11.4 fusion.94
  1062.7 8.9 bitcast_convert_fusion
  1087.3 17.9 %collective-permute-done.124 = bf16[256,2048]{1,0:T(8,128)(2,1)S(1)} collective-permute-done((bf16[256,2048]{1,0:T(8,128)(2,1)S(1)}, bf16[256,2048]{1,0:T(8,128)(2,1)S(1)}, u32[]{:S(2)}, u32[]{:S(2)}) %collective-permute-start.124) | collective-permute-done | bytes 1048608 | tf_op jit(solution)/shard_map/sink_d1/ppermute | solution.py:77
  1163.2 40.0 %psum.7 = f32[3,2,2048]{2,0,1:T(4,128)S(1)} all-reduce(f32[3,2,2048]{2,0,1:T(4,128)S(1)} %pad_maximum_fusion.16), channel_id=1, replica_groups=mesh['wide'=8,'narrow'=4] {'wide','narrow'}, use_global_device_ids=true, to_apply=%region_44.45 | all-reduce | flops 12288 | bytes 98304 | tf_op jit(solution)/shard_map/psum | solution.py:299
  (943 shorter events, 787.3 us)
Async XLA Ops:
  7.2 102.8 %all-gather.8.cloned.1.call-start = ((), (), s32[]{:S(2)}) async-start(), calls=%async_computation.7 | async-start | bytes 7077888 | tf_op jit(solution)/shard_map/all_gather | solution.py:157
  11.6 119.0 %all-gather.10.cloned.1.call-start = ((), (), s32[]{:S(2)}) async-start(), calls=%async_computation.8 | async-start | bytes 2359296 | tf_op jit(solution)/shard_map/all_gather | solution.py:162
  12.4 299.8 %all-gather.14.cloned.1.call-start = ((), (), s32[]{:S(2)}) async-start(), calls=%async_computation.10 | async-start | bytes 2359296 | tf_op jit(solution)/shard_map/all_gather | solution.py:157
  14.4 313.6 %all-gather.12.cloned.1.call-start = ((), (), s32[]{:S(2)}) async-start(), calls=%async_computation.9 | async-start | bytes 9437184 | tf_op jit(solution)/shard_map/all_gather | solution.py:157
  17.0 330.0 %all-gather.16.cloned.1.call-start = ((), (), s32[]{:S(2)}) async-start(), calls=%async_computation.11 | async-start | bytes 2359296 | tf_op jit(solution)/shard_map/all_gather | solution.py:162
  18.8 518.8 %all-gather.18.cloned.1.call-start = ((), (), s32[]{:S(2)}) async-start(), calls=%async_computation.12 | async-start | bytes 9437184 | tf_op jit(solution)/shard_map/all_gather | solution.py:157
  20.0 554.2 %all-gather.20.cloned.1.call-start = ((), (), s32[]{:S(2)}) async-start(), calls=%async_computation.13 | async-start | bytes 9437184 | tf_op jit(solution)/shard_map/all_gather | solution.py:162
  108.5 61.7 %collective-permute-start.13 = (bf16[128,4096]{1,0:T(8,128)(2,1)}, bf16[128,4096]{1,0:T(8,128)(2,1)}, u32[]{:S(2)}, u32[]{:S(2)}) collective-permute-start(bf16[128,4096]{1,0:T(8,128)(2,1)} %broadcast_add_fusion.3), channel_id=1, source_target_pairs={{1,0},{2,1},{3,2},{5,4},{6,5},{7,6},{9,8},{10,9},{11,10},{13,12},{... | collective-permute-start | bytes 3145736 | tf_op jit(solution)/shard_map/spread_text/ppermute | solution.py:62
  150.2 853.7 %reduce-scatter.8.cloned.1.call-start = ((), (), s32[]{:S(2)}) async-start(), calls=%async_computation.14 | async-start | bytes 9437184 | tf_op jit(solution)/shard_map/reduce_scatter | solution.py:168
  174.8 36.7 %collective-permute-start.8 = (bf16[128,2048]{1,0:T(8,128)(2,1)S(1)}, bf16[128,2048]{1,0:T(8,128)(2,1)S(1)}, u32[]{:S(2)}, u32[]{:S(2)}) collective-permute-start(bf16[128,2048]{1,0:T(8,128)(2,1)S(1)} %get-tuple-element.122), channel_id=1, source_target_pairs={{0,1},{1,2},{2,3},{4,5},{5,6},{6,7},{8,9},{9,10},{10,11},{12,13},{... | collective-permute-start | bytes 1572872 | tf_op jit(solution)/shard_map/sink_r1_0/ppermute | solution.py:77
  179.2 33.6 %collective-permute-start.11 = (bf16[128,2048]{1,0:T(8,128)(2,1)S(1)}, bf16[128,2048]{1,0:T(8,128)(2,1)S(1)}, u32[]{:S(2)}, u32[]{:S(2)}) collective-permute-start(bf16[128,2048]{1,0:T(8,128)(2,1)S(1)} %get-tuple-element.123), channel_id=1, source_target_pairs={{1,0},{2,1},{3,2},{5,4},{6,5},{7,6},{9,8},{10,9},{11,10},{13,12},{... | collective-permute-start | bytes 1572872 | tf_op jit(solution)/shard_map/sink_r1_0/ppermute | solution.py:78
  199.6 34.5 %collective-permute-start.12 = (bf16[128,4096]{1,0:T(8,128)(2,1)}, bf16[128,4096]{1,0:T(8,128)(2,1)S(1)}, u32[]{:S(2)}, u32[]{:S(2)}) collective-permute-start(bf16[128,4096]{1,0:T(8,128)(2,1)} %broadcast_add_fusion.3), channel_id=1, source_target_pairs={{0,1},{1,2},{2,3},{4,5},{5,6},{6,7},{8,9},{9,10},{10,11},{12,13},{... | collective-permute-start | bytes 3145736 | tf_op jit(solution)/shard_map/spread_text/ppermute | solution.py:61
  232.8 34.1 %collective-permute-start.37 = (bf16[128,2048]{1,0:T(8,128)(2,1)S(1)}, bf16[128,2048]{1,0:T(8,128)(2,1)S(1)}, u32[]{:S(2)}, u32[]{:S(2)}) collective-permute-start(bf16[128,2048]{1,0:T(8,128)(2,1)S(1)} %get-tuple-element.160), channel_id=1, source_target_pairs={{1,0},{2,1},{3,2},{5,4},{6,5},{7,6},{9,8},{10,9},{11,10},{13,12},{... | collective-permute-start | bytes 1572872 | tf_op jit(solution)/shard_map/spread_n2_1/ppermute | solution.py:62
  234.1 34.0 %collective-permute-start.36 = (bf16[128,2048]{1,0:T(8,128)(2,1)S(1)}, bf16[128,2048]{1,0:T(8,128)(2,1)S(1)}, u32[]{:S(2)}, u32[]{:S(2)}) collective-permute-start(bf16[128,2048]{1,0:T(8,128)(2,1)S(1)} %get-tuple-element.160), channel_id=1, source_target_pairs={{0,1},{1,2},{2,3},{4,5},{5,6},{6,7},{8,9},{9,10},{10,11},{12,13},{... | collective-permute-start | bytes 1572872 | tf_op jit(solution)/shard_map/spread_n2_1/ppermute | solution.py:61
  245.5 48.9 %collective-permute-start.16 = (bf16[128,4096]{1,0:T(8,128)(2,1)S(1)}, bf16[128,4096]{1,0:T(8,128)(2,1)}, u32[]{:S(2)}, u32[]{:S(2)}) collective-permute-start(bf16[128,4096]{1,0:T(8,128)(2,1)S(1)} %get-tuple-element.143), channel_id=1, source_target_pairs={{1,2},{2,3},{5,6},{6,7},{9,10},{10,11},{13,14},{14,15},{17,18},{18... | collective-permute-start | bytes 3145736 | tf_op jit(solution)/shard_map/spread_text/ppermute | solution.py:61
  301.8 69.0 %collective-permute-start.43 = (bf16[256,2048]{1,0:T(8,128)(2,1)}, bf16[256,2048]{1,0:T(8,128)(2,1)}, u32[]{:S(2)}, u32[]{:S(2)}) collective-permute-start(bf16[256,2048]{1,0:T(8,128)(2,1)} %broadcast_add_fusion), channel_id=1, source_target_pairs={{1,0},{2,1},{3,2},{5,4},{6,5},{7,6},{9,8},{10,9},{11,10},{13,12},{... | collective-permute-start | bytes 3145736 | tf_op jit(solution)/shard_map/spread_og/ppermute | solution.py:62
  303.1 65.2 %collective-permute-start.42 = (bf16[256,2048]{1,0:T(8,128)(2,1)}, bf16[256,2048]{1,0:T(8,128)(2,1)}, u32[]{:S(2)}, u32[]{:S(2)}) collective-permute-start(bf16[256,2048]{1,0:T(8,128)(2,1)} %broadcast_add_fusion), channel_id=1, source_target_pairs={{0,1},{1,2},{2,3},{4,5},{5,6},{6,7},{8,9},{9,10},{10,11},{12,13},{... | collective-permute-start | bytes 3145736 | tf_op jit(solution)/shard_map/spread_og/ppermute | solution.py:61
  352.4 42.6 %collective-permute-start.24 = (bf16[128,2048]{1,0:T(8,128)(2,1)}, bf16[128,2048]{1,0:T(8,128)(2,1)}, u32[]{:S(2)}, u32[]{:S(2)}) collective-permute-start(bf16[128,2048]{1,0:T(8,128)(2,1)} %get-tuple-element.112), channel_id=1, source_target_pairs={{0,1},{4,5},{8,9},{12,13},{16,17},{20,21},{24,25},{28,29}} | collective-permute-start | bytes 1572872 | tf_op jit(solution)/shard_map/sink_r2_0/ppermute | solution.py:77
  432.6 54.0 %collective-permute-start.64 = (bf16[256,2048]{1,0:T(8,128)(2,1)}, bf16[256,2048]{1,0:T(8,128)(2,1)S(1)}, u32[]{:S(2)}, u32[]{:S(2)}) collective-permute-start(bf16[256,2048]{1,0:T(8,128)(2,1)} %collective-permute-done.45), channel_id=1, source_target_pairs={{1,0},{5,4},{9,8},{13,12},{17,16},{21,20},{25,24},{29,28}} | collective-permute-start | bytes 3145736 | tf_op jit(solution)/shard_map/spread_og/ppermute | solution.py:62
  444.0 65.0 %collective-permute-start.65 = (bf16[256,2048]{1,0:T(8,128)(2,1)}, bf16[256,2048]{1,0:T(8,128)(2,1)S(1)}, u32[]{:S(2)}, u32[]{:S(2)}) collective-permute-start(bf16[256,2048]{1,0:T(8,128)(2,1)} %collective-permute-done.44), channel_id=1, source_target_pairs={{2,3},{6,7},{10,11},{14,15},{18,19},{22,23},{26,27},{30,31}} | collective-permute-start | bytes 3145736 | tf_op jit(solution)/shard_map/spread_og/ppermute | solution.py:61
  568.5 438.2 %reduce-scatter.10.cloned.1.call-start = ((), (), s32[]{:S(2)}) async-start(), calls=%async_computation.15 | async-start | bytes 9437184 | tf_op jit(solution)/shard_map/reduce_scatter | solution.py:165
  648.7 434.8 %reduce-scatter.12.cloned.1.call-start = ((), (), s32[]{:S(2)}) async-start(), calls=%async_computation.16 | async-start | bytes 2359296 | tf_op jit(solution)/shard_map/reduce_scatter | solution.py:168
  735.7 78.8 %collective-permute-start.76 = (bf16[256,2048]{1,0:T(8,128)(2,1)}, bf16[256,2048]{1,0:T(8,128)(2,1)}, u32[]{:S(2)}, u32[]{:S(2)}) collective-permute-start(bf16[256,2048]{1,0:T(8,128)(2,1)} %fusion.318), channel_id=1, source_target_pairs={{0,1},{4,5},{8,9},{12,13},{16,17},{20,21},{24,25},{28,29}} | collective-permute-start | bytes 3145736 | tf_op jit(solution)/shard_map/sink_out/ppermute | solution.py:77
  740.5 74.0 %collective-permute-start.80 = (bf16[256,2048]{1,0:T(8,128)(2,1)}, bf16[256,2048]{1,0:T(8,128)(2,1)}, u32[]{:S(2)}, u32[]{:S(2)}) collective-permute-start(bf16[256,2048]{1,0:T(8,128)(2,1)} %fusion.317), channel_id=1, source_target_pairs={{3,2},{7,6},{11,10},{15,14},{19,18},{23,22},{27,26},{31,30}} | collective-permute-start | bytes 3145736 | tf_op jit(solution)/shard_map/sink_out/ppermute | solution.py:78
  788.2 64.2 %collective-permute-start.106 = (bf16[128,2048]{1,0:T(8,128)(2,1)}, bf16[128,2048]{1,0:T(8,128)(2,1)}, u32[]{:S(2)}, u32[]{:S(2)}) collective-permute-start(bf16[128,2048]{1,0:T(8,128)(2,1)} %get-tuple-element.80), channel_id=1, source_target_pairs={{0,1},{4,5},{8,9},{12,13},{16,17},{20,21},{24,25},{28,29}} | collective-permute-start | bytes 1572872 | tf_op jit(solution)/shard_map/sink_d2_0/ppermute | solution.py:77
  790.5 61.9 %collective-permute-start.109 = (bf16[128,2048]{1,0:T(8,128)(2,1)}, bf16[128,2048]{1,0:T(8,128)(2,1)}, u32[]{:S(2)}, u32[]{:S(2)}) collective-permute-start(bf16[128,2048]{1,0:T(8,128)(2,1)} %get-tuple-element.81), channel_id=1, source_target_pairs={{3,2},{7,6},{11,10},{15,14},{19,18},{23,22},{27,26},{31,30}} | collective-permute-start | bytes 1572872 | tf_op jit(solution)/shard_map/sink_d2_0/ppermute | solution.py:78
  814.4 270.9 %reduce-scatter.14.cloned.1.call-start = ((), (), s32[]{:S(2)}) async-start(), calls=%async_computation.17 | async-start | bytes 2359296 | tf_op jit(solution)/shard_map/reduce_scatter | solution.py:165
  880.4 245.2 %reduce-scatter.20.cloned.1.call-start = ((), (), s32[]{:S(2)}) async-start(), calls=%async_computation.20 | async-start | bytes 2359296 | tf_op jit(solution)/shard_map/reduce_scatter | solution.py:168
  970.2 178.2 %reduce-scatter.16.cloned.1.call-start = ((), (), s32[]{:S(2)}) async-start(), calls=%async_computation.18 | async-start | bytes 9437184 | tf_op jit(solution)/shard_map/reduce_scatter | solution.py:165
  970.9 236.3 %reduce-scatter.18.cloned.1.call-start = ((), (), s32[]{:S(2)}) async-start(), calls=%async_computation.19 | async-start | bytes 7077888 | tf_op jit(solution)/shard_map/reduce_scatter | solution.py:165
  987.6 84.0 %collective-permute-start.92 = (bf16[256,2048]{1,0:T(8,128)(2,1)}, bf16[256,2048]{1,0:T(8,128)(2,1)}, u32[]{:S(2)}, u32[]{:S(2)}) collective-permute-start(bf16[256,2048]{1,0:T(8,128)(2,1)} %add_convert_fusion.1), channel_id=1, source_target_pairs={{0,1},{1,2},{2,3},{4,5},{5,6},{6,7},{8,9},{9,10},{10,11},{12,13},{... | collective-permute-start | bytes 3145736 | tf_op jit(solution)/shard_map/sink_out/ppermute | solution.py:77
  1037.6 35.2 %collective-permute-start.93 = (bf16[256,2048]{1,0:T(8,128)(2,1)}, bf16[256,2048]{1,0:T(8,128)(2,1)}, u32[]{:S(2)}, u32[]{:S(2)}) collective-permute-start(bf16[256,2048]{1,0:T(8,128)(2,1)} %add_convert_fusion), channel_id=1, source_target_pairs={{1,0},{2,1},{3,2},{5,4},{6,5},{7,6},{9,8},{10,9},{11,10},{13,12},{... | collective-permute-start | bytes 3145736 | tf_op jit(solution)/shard_map/sink_out/ppermute | solution.py:78
  (311 other events, 6571.3 us)
Sparse Core Ops, SparseCore 0:
  11.7 48.1 all-gather.7
  62.3 28.0 all-gather.9
  92.9 27.7 all-gather.13
  122.4 54.2 all-gather.11
  178.4 28.0 all-gather.15
  208.3 54.2 all-gather.17
  264.5 55.8 all-gather.19
  568.6 74.8 reduce-scatter.7
  648.8 76.2 reduce-scatter.9
  814.5 40.9 reduce-scatter.11
  880.5 42.3 reduce-scatter.13
  970.3 40.5 reduce-scatter.19
  1014.3 71.4 reduce-scatter.15
  1089.0 61.7 reduce-scatter.17
